TPU v7x, 128 devices: a whole 4x4x4 slice. The times are simulated.
128 devices in a mesh: blk: 64 (over x, z, y_lo, core), ep: 2 (over y_hi).
Axes of the slice: x: 4, y: 4 (y_hi: 2, y_lo: 2; y = y_hi * 2 + y_lo), z: 4, core: 2. Of those that a mesh axis runs over, the one named last changes fastest.
Arguments:
- hidden_in: bfloat16 [1024, 4096], P('blk'), may hold values from -6 to 6
- out_grad: bfloat16 [1024, 4096], P('blk'), may hold values from -6 to 6
- expert_ids: int32 [1024, 2], P('blk'), may hold values from 0 to 3, all different within a row; in each aligned block of 16 rows (0 to 15, 16 to 31, ...) at most 12 rows name the same one
- gate_values: bfloat16 [1024, 2], P('blk'), may hold values from 0.099609375 to 1
- w_gate: bfloat16 [4, 14336, 4096], P('ep', 'blk'), may hold values from -0.09375 to 0.09375
- w_up: bfloat16 [4, 14336, 4096], P('ep', 'blk'), may hold values from -0.09375 to 0.09375
- w_down: bfloat16 [4, 14336, 4096], P('ep', 'blk'), may hold values from -0.046875 to 0.046875
Outputs:
- input_grad: bfloat16 [1024, 4096], P('blk')
- gate_grad: float32 [1024, 2], P('blk')
- grad_gate: bfloat16 [4, 14336, 4096], P('ep', 'blk')
- grad_up: bfloat16 [4, 14336, 4096], P('ep', 'blk')
- grad_down: bfloat16 [4, 14336, 4096], P('ep', 'blk')
Inputs may be any that keep to these rules, and one draw needn't show every extreme that they name: `expert_ids`: each row names 2 different experts; in each aligned block of 16 rows (the rows of one device) no expert is named by more than 12 rows, a bound that some block reaches.
All inputs are finite; a program needn't handle non-finite values.
Results may differ from a plain program's by a relative error of at most 0.008.
Values may be sent and summed in bfloat16 or wider, within the bound.
No kernel may reach another device: no remote copies, remote signals or barrier semaphores. Data moves between devices by JAX's collectives and lax.ppermute only.
A program may use at most 256 MiB of HBM per device.

v0:
```python
import jax
import jax.numpy as jnp
from jax import lax
from jax.sharding import PartitionSpec as P

TOK_DEV = 16
CAP = 12


def sent_together(arrays, axis, dim, along):
    ends, at = ([], 0)
    for a in arrays[:-1]:
        at += a.shape[along]
        ends.append(at)
    both = jnp.concatenate(arrays, axis=along)
    return tuple(jnp.split(lax.all_gather(both, axis, axis=dim, tiled=True), ends, axis=along))


def side_by_side(arrays, axis, dim, along):
    both = jnp.concatenate(arrays, axis=along)
    filled, at, gathered = (lax.psum_scatter(both, axis, scatter_dimension=dim, tiled=True), 0, [])
    for a in arrays:
        gathered.append(lax.slice_in_dim(filled, at, at + a.shape[along], axis=along))
        at += a.shape[along]
    return tuple(gathered)


def sent_to_all(value, axis):
    copies = jnp.broadcast_to(value, (lax.axis_size(axis), *value.shape))
    return lax.all_to_all(copies, axis, split_axis=0, concat_axis=0, tiled=True)


def taken_together(value, axis):
    return sent_to_all(value, axis).astype(jnp.float32).sum(axis=0)


def routed(expert_ids, gate_values, expert, blocks):
    chosen = expert_ids == expert
    hits = jnp.any(chosen, axis=1).astype(jnp.int32).reshape(blocks, TOK_DEV)
    weight = jnp.sum(
        jnp.where(chosen, gate_values.astype(jnp.float32), jnp.float32(0.0)), axis=1
    ).reshape(blocks, TOK_DEV)
    position = jnp.cumsum(hits, axis=1) - hits
    slot_index = lax.broadcasted_iota(jnp.int32, (blocks, CAP, TOK_DEV), 1)
    picked = (position[:, None, :] == slot_index) & (hits[:, None, :] > 0)
    selector = jnp.where(picked, jnp.float32(1.0), jnp.float32(0.0))
    return (selector, weight, chosen)


def expert_pass(selector, weight, hidden_in, out_grad, gate_mat, up_mat, down_mat, blocks):
    width = hidden_in.shape[1]
    select_low = selector.astype(jnp.bfloat16)
    x_slots = (
        jnp.einsum(
            "bct,btd->bcd",
            select_low,
            hidden_in.reshape(blocks, TOK_DEV, width),
            preferred_element_type=jnp.float32,
        )
        .astype(jnp.bfloat16)
        .reshape(-1, width)
    )
    dy_slots = (
        jnp.einsum(
            "bct,btd->bcd",
            select_low,
            out_grad.reshape(blocks, TOK_DEV, width),
            preferred_element_type=jnp.float32,
        )
        .astype(jnp.bfloat16)
        .reshape(-1, width)
    )
    slot_weight = jnp.einsum("bct,bt->bc", selector, weight).reshape(-1, 1)
    contract_cols = (((1,), (1,)), ((), ()))
    gate_pre = lax.dot_general(x_slots, gate_mat, contract_cols, preferred_element_type=jnp.float32)
    up_pre = lax.dot_general(x_slots, up_mat, contract_cols, preferred_element_type=jnp.float32)
    back = lax.dot_general(dy_slots, down_mat, contract_cols, preferred_element_type=jnp.float32)
    sigmoid_gate = jax.nn.sigmoid(gate_pre)
    activation = gate_pre * sigmoid_gate * up_pre
    slot_gate = jnp.sum(activation * back, axis=1)
    dact = slot_weight * back
    d_up = (dact * gate_pre * sigmoid_gate).astype(jnp.bfloat16)
    d_gate = (dact * up_pre * sigmoid_gate * (1.0 + gate_pre * (1.0 - sigmoid_gate))).astype(
        jnp.bfloat16
    )
    act_low = activation.astype(jnp.bfloat16)
    dy_weighted = (slot_weight * dy_slots.astype(jnp.float32)).astype(jnp.bfloat16)
    contract_rows = (((0,), (0,)), ((), ()))
    grad_g = lax.dot_general(
        d_gate, x_slots, contract_rows, preferred_element_type=jnp.float32
    ).astype(jnp.bfloat16)
    grad_u = lax.dot_general(
        d_up, x_slots, contract_rows, preferred_element_type=jnp.float32
    ).astype(jnp.bfloat16)
    grad_d = lax.dot_general(
        act_low, dy_weighted, contract_rows, preferred_element_type=jnp.float32
    ).astype(jnp.bfloat16)
    dx_slots = jnp.dot(d_gate, gate_mat, preferred_element_type=jnp.float32) + jnp.dot(
        d_up, up_mat, preferred_element_type=jnp.float32
    )
    dx_tokens = jnp.einsum("bct,bcd->btd", selector, dx_slots.reshape(blocks, CAP, width)).reshape(
        -1, width
    )
    gate_tokens = jnp.einsum("bct,bc->bt", selector, slot_gate.reshape(blocks, CAP)).reshape(-1)
    return (grad_g, grad_u, grad_d, dx_tokens, gate_tokens)


def shards(hidden_in, out_grad, expert_ids, gate_values, w_gate, w_up, w_down):
    whole_x, whole_dy, whole_ids, whole_gates = (
        *sent_together((hidden_in, out_grad), "blk", 0, 1),
        lax.all_gather(expert_ids, "blk", axis=0, tiled=True),
        lax.all_gather(gate_values, "blk", axis=0, tiled=True),
    )
    blocks = whole_x.shape[0] // TOK_DEV
    first_expert = lax.axis_index("ep") * w_gate.shape[0]
    token_grad = jnp.zeros(whole_x.shape, jnp.float32)
    gate_grad = jnp.zeros(whole_ids.shape, jnp.float32)
    grads_g, grads_u, grads_d = ([], [], [])
    for local_expert in range(w_gate.shape[0]):
        selector, weight, chosen = routed(
            whole_ids, whole_gates, first_expert + local_expert, blocks
        )
        grad_g, grad_u, grad_d, dx_tokens, gate_tokens = expert_pass(
            selector,
            weight,
            whole_x,
            whole_dy,
            w_gate[local_expert],
            w_up[local_expert],
            w_down[local_expert],
            blocks,
        )
        grads_g.append(grad_g)
        grads_u.append(grad_u)
        grads_d.append(grad_d)
        token_grad = token_grad + dx_tokens
        gate_grad = gate_grad + jnp.where(chosen, gate_tokens[:, None], jnp.float32(0.0))
    part_x, part_g = side_by_side((token_grad, gate_grad), "blk", 0, 1)
    summed_x, gate_out = (
        taken_together(part_x.astype(jnp.bfloat16), "ep").astype(jnp.float32),
        taken_together(part_g.astype(jnp.bfloat16), "ep").astype(jnp.float32),
    )
    input_grad = summed_x.astype(jnp.bfloat16)
    return (input_grad, gate_out, jnp.stack(grads_g), jnp.stack(grads_u), jnp.stack(grads_d))


def solution(mesh):
    in_specs = (
        P("blk", None),
        P("blk", None),
        P("blk", None),
        P("blk", None),
        P("ep", "blk", None),
        P("ep", "blk", None),
        P("ep", "blk", None),
    )
    out_specs = (
        P("blk", None),
        P("blk", None),
        P("ep", "blk", None),
        P("ep", "blk", None),
        P("ep", "blk", None),
    )
    return jax.shard_map(shards, mesh=mesh, in_specs=in_specs, out_specs=out_specs, check_vma=False)
```

profile of v0, /device:TPU:0, one launch (start us, length us, event | category | flops | bytes accessed | tf_op | source)
XLA Modules:
  0.0 689.8 jit_solution(14464461744498951361)
XLA Ops:
  9.0 83.9 %all-gather = s32[64,16,2]{1,2,0:T(2,128)S(1)} all-gather(s32[1,16,2]{1,2,0:T(2,128)} %bitcast.126), channel_id=1, replica_groups=mesh['blk'=64,'ep'=2] {'blk'}, dimensions={0}, use_global_device_ids=true | all-gather | bytes 8320 | tf_op jit(solution)/shard_map/all_gather | solution.py:111
  95.2 76.7 %all-gather.1 = bf16[64,16,2]{1,2,0:T(2,128)(2,1)S(1)} all-gather(bf16[1,16,2]{1,2,0:T(2,128)(2,1)} %bitcast.127), channel_id=1, replica_groups=mesh['blk'=64,'ep'=2] {'blk'}, dimensions={0}, use_global_device_ids=true | all-gather | bytes 4160 | tf_op jit(solution)/shard_map/all_gather | solution.py:112
  173.8 7.0 %fusion.50 = (bf16[1024,4096]{1,0:T(8,128)(2,1)S(1)}, bf16[1024,4096]{1,0:T(8,128)(2,1)S(1)}) fusion(bf16[1024,8192]{1,0:T(8,128)(2,1)} %all-gather.4.cloned.1.call-done), kind=kLoop, calls=%fused_computation.90 | loop fusion | bytes 33554432 | tf_op jit(solution)/shard_map/split | solution.py:16
  180.8 5.6 convolution_convert_fusion.2
  186.3 5.6 convolution_convert_fusion.3
  191.9 5.6 convolution_convert_fusion
  197.5 5.6 convolution_convert_fusion.1
  203.0 10.0 %reshape.115 = bf16[768,4096]{1,0:T(8,128)(2,1)} reshape(bf16[64,12,4096]{2,1,0:T(8,128)(2,1)} %convolution_convert_fusion.2) | data formatting | bytes 12582912 | tf_op jit(solution)/shard_map/reshape | solution.py:61
  213.0 9.9 %reshape.113 = bf16[768,4096]{1,0:T(8,128)(2,1)} reshape(bf16[64,12,4096]{2,1,0:T(8,128)(2,1)} %convolution_convert_fusion.3) | data formatting | bytes 12582912 | tf_op jit(solution)/shard_map/reshape | solution.py:71
  222.9 10.1 %reshape.119 = bf16[768,4096]{1,0:T(8,128)(2,1)} reshape(bf16[64,12,4096]{2,1,0:T(8,128)(2,1)} %convolution_convert_fusion) | data formatting | bytes 12582912 | tf_op jit(solution)/shard_map/reshape | solution.py:61
  233.0 5.5 fusion.26
  239.1 2.9 fusion.17
  242.1 9.9 %reshape.118 = bf16[768,4096]{1,0:T(8,128)(2,1)} reshape(bf16[64,12,4096]{2,1,0:T(8,128)(2,1)} %convolution_convert_fusion.1) | data formatting | bytes 12582912 | tf_op jit(solution)/shard_map/reshape | solution.py:71
  252.0 5.5 fusion.28
  257.5 4.5 fusion.19
  262.1 3.2 multiply_convert_fusion.15
  267.4 4.6 convolution_add_fusion.2
  271.9 10.0 %reshape.116 = bf16[64,12,4096]{2,1,0:T(8,128)(2,1)} reshape(bf16[768,4096]{1,0:T(8,128)(2,1)} %convolution_add_fusion.2) | data formatting | bytes 12582912 | tf_op jit(solution)/shard_map/reshape | solution.py:101
  281.9 6.9 %multiply_convert_fusion.13 = (bf16[768,224]{0,1:T(8,128)(2,1)S(1)}, f32[768]{0:T(1024)S(1)}, bf16[768,224]{0,1:T(8,128)(2,1)S(1)}, f32[768,224]{0,1:T(8,128)}) fusion(f32[768,224]{0,1:T(8,128)} %fusion.17, f32[768,224]{0,1:T(8,128)} %fusion.19, f32[768]{0:T(1024)S(1)} %mul.103, bf16[768,4096]{1,0:T(8,128)(2,1)} %reshape.119, bf16[2,224,4096]{2,1,0:T(8,128)(2,1)} %param.11), kind=kOutput, calls=%fused_computation.62 | convolution fusion | flops 1412381952 | bytes 10885120 | tf_op jit(solution)/shard_map/dot_general | solution.py:75
  290.9 4.5 convolution_add_fusion.1
  295.4 9.8 %reshape.120 = bf16[64,12,4096]{2,1,0:T(8,128)(2,1)} reshape(bf16[768,4096]{1,0:T(8,128)(2,1)} %convolution_add_fusion.1) | data formatting | bytes 12582912 | tf_op jit(solution)/shard_map/reshape | solution.py:101
  306.2 11.5 %fusion.52 = f32[64,16,4096]{2,1,0:T(8,128)} fusion(bf16[64,12,16]{1,2,0:T(8,128)(2,1)S(1)} %copy.49, bf16[64,12,4096]{2,1,0:T(8,128)(2,1)} %reshape.116), kind=kOutput, calls=%fused_computation.92 | convolution fusion | flops 100663296 | bytes 23093248 | tf_op jit(solution)/shard_map/bct,bcd->btd/dot_general | solution.py:101
  317.8 16.2 %convolution_add_fusion = f32[64,16,4096]{2,1,0:T(8,128)} fusion(f32[64,16,4096]{2,1,0:T(8,128)} %fusion.52, bf16[64,12,16]{1,2,0:T(8,128)(2,1)S(1)} %copy.55, bf16[64,12,4096]{2,1,0:T(8,128)(2,1)} %reshape.120), kind=kOutput, calls=%fused_computation.3 | convolution fusion | flops 104857600 | bytes 39870464 | tf_op jit(solution)/shard_map/bct,bcd->btd/dot_general | solution.py:101
  334.0 11.7 %pad_maximum_fusion = f32[1024,4098]{1,0:T(8,128)} fusion(f32[1024,2]{1,0:T(8,128)S(1)} %copy.56, f32[1024,4096]{1,0:T(8,128)} %bitcast.107), kind=kLoop, calls=%fused_computation | loop fusion | flops 4196352 | bytes 33570816 | tf_op jit(solution)/shard_map/concatenate | solution.py:20
  345.8 4.5 fusion.8
  350.3 4.6 fusion.9
  357.8 2.9 fusion.7
  369.0 290.9 %reduce-scatter.2.cloned.1.call-done = f32[16,4098]{1,0:T(8,128)} async-done(((f32[1024,4098]{1,0:T(8,128)}), f32[16,4098]{1,0:T(8,128)}) %reduce-scatter.2.cloned.1.call-update) | async-done | bytes 262288 | tf_op jit(solution)/shard_map/reduce_scatter | solution.py:21
  661.5 4.3 all-to-all-start.1
  665.8 5.2 all-to-all-done.1
  671.7 3.4 all-to-all-start
  675.1 3.7 pad_maximum_fusion.1
  (115 shorter events, 28.6 us)
Async XLA Ops:
  7.2 166.6 %all-gather.4.cloned.1.call-start = ((), (), s32[]{:S(2)}) async-start(), calls=%async_computation.3 | async-start | bytes 17039360 | tf_op jit(solution)/shard_map/all_gather | solution.py:16
  8.9 650.9 %reduce-scatter.2.cloned.1.call-start = ((), (), s32[]{:S(2)}) async-start(), calls=%async_computation.4 | async-start | bytes 17571840 | tf_op jit(solution)/shard_map/reduce_scatter | solution.py:21
  232.9 5.5 copy-start.1
  233.0 6.2 copy-start.2
  239.1 22.9 %copy-start.9 = (f32[768,224]{0,1:T(8,128)}, f32[768,224]{0,1:T(8,128)S(1)}, u32[]{:S(2)}) copy-start(f32[768,224]{0,1:T(8,128)S(1)} %fusion.26) | copy-start | bytes 2064388
  252.0 5.5 copy-start
  252.0 10.1 %slice-start.4 = ((s8[6291456]{0:T(1024)(128)(4,1)}), s8[4194304]{0:T(1024)(128)(4,1)S(1)}, s32[]{:S(2)}) async-start(s8[6291456]{0:T(1024)(128)(4,1)} %bitcast.112), calls=%async_computation.9 | async-start | bytes 8388608
  257.5 4.6 slice-start.5
  257.5 4.6 copy-start.5
  265.3 2.0 copy-start.3
  281.9 6.9 %copy-start.6 = (bf16[2,224,4096]{2,1,0:T(8,128)(2,1)S(1)}, bf16[2,224,4096]{2,1,0:T(8,128)(2,1)}, u32[]{:S(2)}) copy-start(bf16[2,224,4096]{2,1,0:T(8,128)(2,1)} %param.11) | copy-start | bytes 11010052
  288.9 2.0 copy-start.4
  345.7 9.2 %slice-start.6 = ((s8[6291456]{0:T(1024)(128)(4,1)}), s8[2097152]{0:T(1024)(128)(4,1)S(1)}, s32[]{:S(2)}) async-start(s8[6291456]{0:T(1024)(128)(4,1)} %bitcast.114), calls=%async_computation.11 | async-start | bytes 4194304
  345.7 9.2 %slice-start.7 = ((s8[6291456]{0:T(1024)(128)(4,1)}), s8[4194304]{0:T(1024)(128)(4,1)S(1)}, s32[]{:S(2)}) async-start(s8[6291456]{0:T(1024)(128)(4,1)} %bitcast.114), calls=%async_computation.12 | async-start | bytes 8388608
  350.3 7.5 %slice-start.8 = ((s8[6291456]{0:T(1024)(128)(4,1)}), s8[4194304]{0:T(1024)(128)(4,1)S(1)}, s32[]{:S(2)}) async-start(s8[6291456]{0:T(1024)(128)(4,1)} %bitcast.116), calls=%async_computation.13 | async-start | bytes 8388608
  350.3 10.4 %slice-start.2 = ((s8[6291456]{0:T(1024)(128)(4,1)}), s8[4194304]{0:T(1024)(128)(4,1)S(1)}, s32[]{:S(2)}) async-start(s8[6291456]{0:T(1024)(128)(4,1)} %bitcast.110), calls=%async_computation.7 | async-start | bytes 8388608
  354.9 2.9 slice-start.9
  355.0 5.8 slice-start.3
  357.8 3.0 copy-start.10
  357.8 3.0 copy-start.11
  357.8 4.9 slice-start
  360.8 1.9 slice-start.1
  360.8 1.9 copy-start.8
  360.8 2.0 copy-start.12
  366.8 308.3 %copy-start.7 = (bf16[1,224,4096]{2,1,0:T(8,128)(2,1)S(1)}, bf16[1,224,4096]{2,1,0:T(8,128)(2,1)}, u32[]{:S(2)}) copy-start(bf16[1,224,4096]{2,1,0:T(8,128)(2,1)} %fusion.6) | copy-start | bytes 5505028
  661.5 9.5 %all-to-all-start.1 = ((bf16[2,16,2]{1,2,0:T(2,128)(2,1)}), bf16[2,16,2]{1,2,0:T(2,128)(2,1)S(1)}, u32[]{:S(2)}, u32[]{:S(2)}) async-start(bf16[2,16,2]{1,2,0:T(2,128)(2,1)} %broadcast_in_dim.51), calls=%async_computation.2 | async-start | bytes 2048 | tf_op jit(solution)/shard_map/all_to_all | solution.py:30
  671.7 10.1 %all-to-all-start = ((bf16[2,16,4096]{2,1,0:T(8,128)(2,1)}), bf16[2,16,4096]{2,1,0:T(8,128)(2,1)S(1)}, u32[]{:S(2)}, u32[]{:S(2)}) async-start(bf16[2,16,4096]{2,1,0:T(8,128)(2,1)} %broadcast_in_dim.50), calls=%async_computation.1 | async-start | bytes 524288 | tf_op jit(solution)/shard_map/all_to_all | solution.py:30
Sparse Core Ops, SparseCore 0:
  10.3 124.1 all-gather.3
  345.9 313.9 reduce-scatter.1
where the time goes:
time: 695 us; the launch traced here: 690 us
  waiting for transfers between devices  299 us (43%)
  blocking collectives  161 us (23%)
  matrix products  111 us (16%)
  local copies, waits for them, and re-layouts  72.5 us (10%)
  other arithmetic  24.4 us (4%)
  between operations  15 us (2%)
  starting transfers between devices  7.78 us (1%)
    reduce_scatter x1, waiting for transfers between devices, side_by_side(): lax.psum_scatter(both, axis, scatter_dimension=dim, tiled=True)  291 us
    all_gather x1, blocking collectives, shards(): lax.all_gather(expert_ids, 'blk', axis=0, tiled=True)  83.9 us
    all_gather x1, blocking collectives, shards(): lax.all_gather(gate_values, 'blk', axis=0, tiled=True)  76.7 us
    dot_general x2, matrix products, expert_pass(): jnp.einsum('bct,bcd->btd', selector, dx_slots.reshape(blocks, CAP, width))  27.8 us
    reshape x2, local copies, waits for them, and re-layouts, expert_pass(): x_slots = jnp.einsum('bct,btd->bcd', select_low, hidden_in.reshape(blocks...  20 us
    reshape x2, local copies, waits for them, and re-layouts, expert_pass(): dy_slots = jnp.einsum('bct,btd->bcd', select_low, out_grad.reshape(blocks...  19.8 us
    reshape x2, local copies, waits for them, and re-layouts, expert_pass(): dx_slots.reshape(blocks, CAP, width)  19.7 us
  transfers between devices with their start and end apart: 4, of which 3 were waited for; matrix products, arithmetic and copies ran while one was open for 5% of the time, Pallas kernels for 0%

commit v1 on v0

v1 whole, which is shorter than its diff:
```python
import functools

import jax
import jax.numpy as jnp
from jax import lax
from jax.experimental import pallas as pl
from jax.experimental.pallas import tpu as pltpu
from jax.sharding import PartitionSpec as P


AXES = ("blk", "ep")
X, Z, Y, CORE, EP = 4, 4, 2, 2, 2
D = 4096
EXTRA = 128
EXPERTS = 4
TILE = 512
BF16, F32 = jnp.bfloat16, jnp.float32


def place(i):
    i, e = divmod(i, EP)
    i, c = divmod(i, CORE)
    i, y = divmod(i, Y)
    x, z = divmod(i, Z)
    return x, z, y, c, e


def index(x, z, y, c, e):
    return ((((x % X) * Z + z % Z) * Y + y % Y) * CORE + c % CORE) * EP + e % EP


def pairs(to):
    return [(i, index(*to(*place(i)))) for i in range(X * Z * Y * CORE * EP)]


def first(by):
    return pairs(lambda x, z, y, c, e: (x + by * (c == 0), z + by * (c == 1), y, c, e))


def second(by):
    return pairs(lambda x, z, y, c, e: (x + by * (c == 1), z + by * (c == 0), y, c, e))


OTHER_Y = pairs(lambda x, z, y, c, e: (x, z, y + 1, c, e))
OTHER_CORE = pairs(lambda x, z, y, c, e: (x, z, y, c + 1, e))
OTHER_EP = pairs(lambda x, z, y, c, e: (x, z, y, c, e + 1))


def sent(value, to):
    return lax.ppermute(value, AXES, to)


def ring(v, step):
    half = v.shape[0] // 2
    ahead, behind = sent(v, step(-1)), sent(v, step(1))
    far_a = sent(ahead[:half], step(-1))
    return ahead, behind, far_a, sent(behind[half:], step(1))


def plus(a, *others):
    total = a.astype(F32)
    for b in others:
        total = total + b.astype(F32)
    return total.astype(BF16)


def ring_back(own, ahead, behind, far, step):
    half = own.shape[0] // 2
    to_ahead = sent(far[:half], step(1))
    to_behind = sent(far[half:], step(-1))
    ahead = jnp.concatenate([plus(ahead[:half], to_ahead), ahead[half:]], axis=0)
    behind = jnp.concatenate([behind[:half], plus(behind[half:], to_behind)], axis=0)
    up = sent(ahead, step(1))
    return plus(own, up, sent(behind, step(-1)))


NT = (((1,), (1,)), ((), ()))


def expert_kernel(count, held, at, ep_ref, *refs):
    chunks = refs[:count]
    wg_ref, wu_ref, wd_ref = refs[count : count + 3]
    mine_ref, theirs_ref, x_ref, y_ref, coef_ref, cg, cu = refs[count + 3 + held :]
    extra = []
    tokens = cg.shape[0]
    begin = at
    for c in chunks:
        rows = c.shape[0]
        x_ref[at : at + rows, :] = c[:, :D]
        y_ref[at : at + rows, :] = c[:, D : 2 * D]
        extra.append(c[:, 2 * D :].astype(F32))
        at += rows
    xs, ys = x_ref.at[begin:at, :], y_ref.at[begin:at, :]
    coef_ref = coef_ref.at[:, begin:at]
    extra = jnp.concatenate(extra, axis=0).T
    low = ep_ref[0] == 0
    hidden = wg_ref.shape[0] // 2
    gate = lax.dot_general(wg_ref[...], xs[...], NT, preferred_element_type=F32)
    up = lax.dot_general(wu_ref[...], xs[...], NT, preferred_element_type=F32)
    back = lax.dot_general(wd_ref[...], ys[...], NT, preferred_element_type=F32)
    s = 1.0 / (1.0 + jnp.exp(-gate))
    gs = gate * s
    act = gs * up
    product = act * back
    slot_rows = []
    for e in (0, 1):
        mine = slice(e * hidden, (e + 1) * hidden)
        slot_rows.append(jnp.sum(product[mine], axis=0, keepdims=True))
        weight = jnp.where(low, extra[e : e + 1, :], extra[e + 2 : e + 3, :])
        dact = weight * back[mine]
        dgate = dact * up[mine] * s[mine] * (1.0 + gate[mine] * (1.0 - s[mine]))
        coef_ref[e * hidden : (e + 1) * hidden, :] = dgate.astype(BF16)
        coef_ref[(2 + e) * hidden : (3 + e) * hidden, :] = (dact * gs[mine]).astype(BF16)
        coef_ref[(4 + e) * hidden : (5 + e) * hidden, :] = (weight * act[mine]).astype(BF16)
    cg[...] = coef_ref[: 2 * hidden, :].astype(F32).T.astype(BF16)
    cu[...] = coef_ref[2 * hidden : 4 * hidden, :].astype(F32).T.astype(BF16)
    half = tokens // 2

    def column(j, carry):
        cols = pl.ds(pl.multiple_of(j * TILE, TILE), TILE)
        dx = jnp.dot(cg[...], wg_ref[:, cols], preferred_element_type=F32) + jnp.dot(
            cu[...], wu_ref[:, cols], preferred_element_type=F32
        )
        mine_ref[:, cols] = dx[:half].astype(BF16)
        theirs_ref[:, cols] = dx[half:].astype(BF16)
        return carry

    lax.fori_loop(0, D // TILE, column, 0)
    row = lax.broadcasted_iota(jnp.int32, (EXTRA, tokens), 0)
    base = 2 * ep_ref[0]
    slot = jnp.where(row == base, slot_rows[0], 0.0) + jnp.where(row == base + 1, slot_rows[1], 0.0)
    slot = slot.T.astype(BF16)
    mine_ref[:, D:] = slot[:half]
    theirs_ref[:, D:] = slot[half:]


def expert_group(ep, chunks, weights, held, at, total):
    tokens = sum(c.shape[0] for c in chunks)
    hidden2 = weights[0].shape[0]
    vm = pl.BlockSpec(memory_space=pltpu.VMEM)
    part = jax.ShapeDtypeStruct((tokens // 2, D + EXTRA), BF16)
    whole = jax.ShapeDtypeStruct((total, D), BF16)
    before = 1 + len(chunks) + 3
    mine, theirs, *held = pl.pallas_call(
        functools.partial(expert_kernel, len(chunks), len(held), at),
        out_shape=(part, part, whole, whole, jax.ShapeDtypeStruct((3 * hidden2, total), BF16)),
        in_specs=[pl.BlockSpec(memory_space=pltpu.SMEM)] + [vm] * (len(chunks) + 3 + len(held)),
        out_specs=(vm,) * 5,
        scratch_shapes=[pltpu.VMEM((tokens, hidden2), BF16), pltpu.VMEM((tokens, hidden2), BF16)],
        input_output_aliases={before + i: 2 + i for i in range(len(held))},
        cost_estimate=pl.CostEstimate(
            flops=2 * tokens * D * hidden2 * 5,
            bytes_accessed=3 * hidden2 * D * 2 + tokens * 3 * D * 2,
            transcendentals=0,
        ),
        compiler_params=pltpu.CompilerParams(vmem_limit_bytes=8 * 1024 * 1024),
        name="experts",
    )(ep, *chunks, *weights, *held)
    return mine, theirs, held


def weight_kernel(which, side_ref, coef_ref, out_ref):
    h = out_ref.shape[0]
    cols = pl.ds(pl.multiple_of(pl.program_id(0) * TILE, TILE), TILE)
    out_ref[...] = jnp.dot(
        coef_ref[which * h : (which + 1) * h, :], side_ref[:, cols], preferred_element_type=F32
    ).astype(BF16)


def weight_grad(which, side, coef):
    tokens, hidden2 = side.shape[0], coef.shape[0] // 3
    vm = pl.BlockSpec(memory_space=pltpu.VMEM)
    return pl.pallas_call(
        functools.partial(weight_kernel, which),
        grid=(D // TILE,),
        out_shape=jax.ShapeDtypeStruct((hidden2, D), BF16),
        in_specs=[vm, vm],
        out_specs=pl.BlockSpec((hidden2, TILE), lambda j: (0, j)),
        cost_estimate=pl.CostEstimate(
            flops=2 * tokens * D * hidden2,
            bytes_accessed=hidden2 * D * 2 + tokens * D * 2,
            transcendentals=0,
        ),
        compiler_params=pltpu.CompilerParams(vmem_limit_bytes=8 * 1024 * 1024),
        name="weights",
    )(side, coef)


def shards(hidden_in, out_grad, expert_ids, gate_values, w_gate, w_up, w_down):
    local, hidden = w_gate.shape[:2]
    wg, wu, wd = (w.reshape(local * hidden, D) for w in (w_gate, w_up, w_down))
    ep = lax.axis_index("ep").astype(jnp.int32).reshape(1)
    experts = lax.broadcasted_iota(jnp.int32, (1, EXTRA), 1)
    weights = sum(
        jnp.where(expert_ids[:, k : k + 1] == experts, gate_values[:, k : k + 1], 0)
        for k in range(expert_ids.shape[1])
    ).astype(BF16)
    own = jnp.concatenate([hidden_in, out_grad, weights], axis=1)

    two = jnp.concatenate([own, sent(own, OTHER_Y)], axis=0)
    near = jnp.concatenate([two, *ring(two, first)], axis=0)
    near_c = sent(near, OTHER_CORE)
    ahead, behind, far_a, far_b = ring(near, second)
    ahead_c, behind_c = sent(ahead, OTHER_CORE), sent(behind, OTHER_CORE)
    far_ac, far_bc = sent(far_a, OTHER_CORE), sent(far_b, OTHER_CORE)

    groups = ((near, near_c), (ahead, ahead_c), (behind, behind_c), (far_a, far_b, far_ac, far_bc))
    sums, held, at = [], (), 0
    tokens = hidden_in.shape[0] * X * Z * Y * CORE
    for group in groups:
        mine, theirs, held = expert_group(ep, group, (wg, wu, wd), held, at, tokens)
        at += sum(c.shape[0] for c in group)
        sums.append(plus(mine, sent(theirs, OTHER_CORE)))
    x_all, y_all, coef_all = held

    total = ring_back(*sums, second)
    q = total.shape[0] // 4
    total = ring_back(*(total[i * q : (i + 1) * q] for i in range(4)), first)
    q = total.shape[0] // 2
    total = plus(total[:q], sent(total[q:], OTHER_Y))
    other = sent(total, OTHER_EP)
    total = total.astype(F32) + other.astype(F32)
    input_grad = total[:, :D].astype(BF16)
    slot = total[:, D : D + EXPERTS]
    ids = lax.broadcasted_iota(jnp.int32, (1, 1, EXPERTS), 2)
    gate_grad = jnp.sum(jnp.where(expert_ids[:, :, None] == ids, slot[:, None, :], 0.0), axis=2)

    grads = []
    for which, side in enumerate((x_all, x_all, y_all)):
        grads.append(weight_grad(which, side, coef_all).reshape(local, hidden, D))
    return (input_grad, gate_grad, *grads)


def solution(mesh):
    rows, split = P("blk", None), P("ep", "blk", None)
    return jax.shard_map(
        shards,
        mesh=mesh,
        in_specs=(rows, rows, rows, rows, split, split, split),
        out_specs=(rows, rows, split, split, split),
        check_vma=False,
    )
```

time: 695 us -> 199 us (0.29)
  waiting for transfers between devices: 299 us -> 89.4 us
  blocking collectives: 161 us -> 0 us
  matrix products: 111 us -> 0 us
  Pallas kernels: 0 us -> 56.3 us
  local copies, waits for them, and re-layouts: 72.5 us -> 16.7 us
  starting transfers between devices: 7.78 us -> 30.1 us
  other arithmetic: 24.4 us -> 5.34 us
  between operations: 15 us -> 0.86 us
    reduce_scatter x1 -> x0, waiting for transfers between devices: 291 us -> none  [side_by_side(): lax.psum_scatter(both, axis, scatter_dimension=dim, tiled=True)]
    all_gather x2 -> x0, blocking collectives: 161 us -> none  [the longest x1 83.9 us: shards(): lax.all_gather(expert_ids, 'blk', axis=0, tiled=True)]
    dot_general x26 -> x0, matrix products: 111 us -> none  [the longest x2 27.8 us: expert_pass(): jnp.einsum('bct,bcd->btd', selector, dx_slots.reshape(blocks, CAP, width))]
    ppermute x0 -> x28, waiting for transfers between devices: none -> 89.4 us  [sent(): return lax.ppermute(value, AXES, to)]
    reshape x10 -> x0, local copies, waits for them, and re-layouts: 59.9 us -> none  [the longest x2 20 us: expert_pass(): x_slots = jnp.einsum('bct,btd->bcd', select_low, hidden_in.reshape(blocks...]
    pallas_call x0 -> x7, Pallas kernels: none -> 56.3 us  [the longest x4 37.3 us: expert_group(): pl.pallas_call(functools.partial(expert_kernel, len(chunks), len(held), a...]
    ppermute x0 -> x28, starting transfers between devices: none -> 30.1 us  [sent(): return lax.ppermute(value, AXES, to)]
    concatenate x2 -> x6, other arithmetic: 13.4 us -> 2.9 us  [the longest x1 1.71 us: shards(): own = jnp.concatenate([hidden_in, out_grad, weights], axis=1)]
  transfers between devices with their start and end apart: 4 -> 28, of which waited for: 3 -> 16; matrix products, arithmetic and copies ran while one was open for 5% -> 4% of each run, Pallas kernels for 0% -> 24%
where the time goes in v1:
time: 199 us
  waiting for transfers between devices  89.4 us (45%)
  Pallas kernels  56.3 us (28%)
  starting transfers between devices  30.1 us (15%)
  local copies, waits for them, and re-layouts  16.7 us (8%)
  other arithmetic  5.34 us (3%)
    ppermute x28, waiting for transfers between devices, sent(): return lax.ppermute(value, AXES, to)  89.4 us
    pallas_call x4, Pallas kernels, expert_group(): pl.pallas_call(functools.partial(expert_kernel, len(chunks), len(held), a...  37.3 us
    ppermute x28, starting transfers between devices, sent(): return lax.ppermute(value, AXES, to)  30.1 us
    pallas_call x3, Pallas kernels, weight_grad(): pl.pallas_call(functools.partial(weight_kernel, which), grid=(D // TILE,)...  19 us
    unnamed x20, local copies, waits for them, and re-layouts  10.2 us
  transfers between devices with their start and end apart: 28, of which 16 were waited for; matrix products, arithmetic and copies ran while one was open for 4% of the time, Pallas kernels for 24%

profile of v1, /device:TPU:0, one launch (start us, length us, event | category | flops | bytes accessed | tf_op | source)
XLA Modules:
  0.0 198.7 jit_solution(16600376809608711895)
XLA Ops:
  2.2 1.7 pad_maximum_fusion.5
  5.6 6.4 %collective-permute-done = bf16[16,8320]{1,0:T(8,128)(2,1)S(1)} collective-permute-done((bf16[16,8320]{1,0:T(8,128)(2,1)S(1)}, bf16[16,8320]{1,0:T(8,128)(2,1)S(1)}, u32[]{:S(2)}, u32[]{:S(2)}) %collective-permute-start) | collective-permute-done | bytes 266272 | tf_op jit(solution)/shard_map/ppermute | solution.py:50
  13.0 3.0 %collective-permute-start.1 = (bf16[32,8320]{1,0:T(8,128)(2,1)S(1)}, bf16[32,8320]{1,0:T(8,128)(2,1)S(1)}, u32[]{:S(2)}, u32[]{:S(2)}) collective-permute-start(bf16[32,8320]{1,0:T(8,128)(2,1)S(1)} %pad_maximum_fusion.2), channel_id=1, source_target_pairs={{0,96},{1,97},{2,26},{3,27},{4,100},{5,101},{6,30},{7,31},{8,104},... | collective-permute-start | bytes 1597448 | tf_op jit(solution)/shard_map/ppermute | solution.py:50
  16.7 6.1 %collective-permute-done.1 = bf16[32,8320]{1,0:T(8,128)(2,1)S(1)} collective-permute-done((bf16[32,8320]{1,0:T(8,128)(2,1)S(1)}, bf16[32,8320]{1,0:T(8,128)(2,1)S(1)}, u32[]{:S(2)}, u32[]{:S(2)}) %collective-permute-start.1) | collective-permute-done | bytes 532512 | tf_op jit(solution)/shard_map/ppermute | solution.py:50
  22.8 3.8 %collective-permute-start.3 = (bf16[16,8320]{1,0:T(8,128)(2,1)S(1)}, bf16[16,8320]{1,0:T(8,128)(2,1)S(1)}, u32[]{:S(2)}, u32[]{:S(2)}) collective-permute-start(bf16[16,8320]{1,0:T(8,128)(2,1)S(1)} %slice.110), channel_id=1, source_target_pairs={{0,96},{1,97},{2,26},{3,27},{4,100},{5,101},{6,30},{7,31},{8,104},... | collective-permute-start | bytes 798728 | tf_op jit(solution)/shard_map/ppermute | solution.py:50
  28.3 2.2 %collective-permute-done.3 = bf16[16,8320]{1,0:T(8,128)(2,1)S(1)} collective-permute-done((bf16[16,8320]{1,0:T(8,128)(2,1)S(1)}, bf16[16,8320]{1,0:T(8,128)(2,1)S(1)}, u32[]{:S(2)}, u32[]{:S(2)}) %collective-permute-start.3) | collective-permute-done | bytes 266272 | tf_op jit(solution)/shard_map/ppermute | solution.py:50
  31.2 3.1 %collective-permute-done.4 = bf16[16,8320]{1,0:T(8,128)(2,1)S(1)} collective-permute-done((bf16[16,8320]{1,0:T(8,128)(2,1)S(1)}, bf16[16,8320]{1,0:T(8,128)(2,1)S(1)}, u32[]{:S(2)}, u32[]{:S(2)}) %collective-permute-start.4) | collective-permute-done | bytes 266272 | tf_op jit(solution)/shard_map/ppermute | solution.py:50
  35.0 4.0 %collective-permute-start.7 = (bf16[128,8320]{1,0:T(8,128)(2,1)}, bf16[128,8320]{1,0:T(8,128)(2,1)}, u32[]{:S(2)}, u32[]{:S(2)}) collective-permute-start(bf16[128,8320]{1,0:T(8,128)(2,1)} %constant_dynamic-update-slice_fusion.refs_0_), channel_id=1, source_target_pairs={{0,24},{1,25},{2,98},{3,99},{4,28},{5,29},{6,102},{7,103},{8,0},{9... | collective-permute-start | bytes 6389768 | tf_op jit(solution)/shard_map/ppermute | solution.py:50
  39.1 24.2 %collective-permute-done.7.refs_0_ = bf16[128,8320]{1,0:T(8,128)(2,1)} collective-permute-done((bf16[128,8320]{1,0:T(8,128)(2,1)}, bf16[128,8320]{1,0:T(8,128)(2,1)}, u32[]{:S(2)}, u32[]{:S(2)}) %collective-permute-start.7) | collective-permute-done | bytes 2129952 | tf_op jit(solution)/shard_map/ppermute | solution.py:50
  63.3 3.6 %collective-permute-done.11.refs_0_ = bf16[128,8320]{1,0:T(8,128)(2,1)S(1)} collective-permute-done((bf16[128,8320]{1,0:T(8,128)(2,1)}, bf16[128,8320]{1,0:T(8,128)(2,1)S(1)}, u32[]{:S(2)}, u32[]{:S(2)}) %collective-permute-start.11) | collective-permute-done | bytes 2129952 | tf_op jit(solution)/shard_map/ppermute | solution.py:50
  66.9 2.3 %slice.113 = bf16[64,8320]{1,0:T(8,128)(2,1)} slice(bf16[128,8320]{1,0:T(8,128)(2,1)} %collective-permute-done.7.refs_0_), slice={[0:64], [0:8320]} | slice | bytes 2129920 | tf_op jit(solution)/shard_map/slice | solution.py:56
  72.2 12.1 %collective-permute-done.10.refs_0_ = bf16[64,8320]{1,0:T(8,128)(2,1)S(1)} collective-permute-done((bf16[64,8320]{1,0:T(8,128)(2,1)}, bf16[64,8320]{1,0:T(8,128)(2,1)S(1)}, u32[]{:S(2)}, u32[]{:S(2)}) %collective-permute-start.10) | collective-permute-done | bytes 1064992 | tf_op jit(solution)/shard_map/ppermute | solution.py:50
  84.3 3.0 %collective-permute-done.12.refs_1_ = bf16[64,8320]{1,0:T(8,128)(2,1)} collective-permute-done((bf16[64,8320]{1,0:T(8,128)(2,1)}, bf16[64,8320]{1,0:T(8,128)(2,1)}, u32[]{:S(2)}, u32[]{:S(2)}) %collective-permute-start.12) | collective-permute-done | bytes 1064992 | tf_op jit(solution)/shard_map/ppermute | solution.py:50
  87.3 2.0 %copy-done = bf16[2,224,4096]{2,1,0:T(8,128)(2,1)S(1)} copy-done((bf16[2,224,4096]{2,1,0:T(8,128)(2,1)S(1)}, bf16[2,224,4096]{2,1,0:T(8,128)(2,1)}, u32[]{:S(2)}) %copy-start) | copy-done | bytes 3670040
  89.3 2.0 %copy-done.2 = bf16[2,224,4096]{2,1,0:T(8,128)(2,1)S(1)} copy-done((bf16[2,224,4096]{2,1,0:T(8,128)(2,1)S(1)}, bf16[2,224,4096]{2,1,0:T(8,128)(2,1)}, u32[]{:S(2)}) %copy-start.2) | copy-done | bytes 3670040
  91.4 2.0 %copy-done.4 = bf16[2,224,4096]{2,1,0:T(8,128)(2,1)S(1)} copy-done((bf16[2,224,4096]{2,1,0:T(8,128)(2,1)S(1)}, bf16[2,224,4096]{2,1,0:T(8,128)(2,1)}, u32[]{:S(2)}) %copy-start.4) | copy-done | bytes 3670040
  93.4 9.3 %experts.4 = (bf16[128,4224]{1,0:T(8,128)(2,1)S(1)}, bf16[128,4224]{1,0:T(8,128)(2,1)S(1)}, bf16[1024,4096]{1,0:T(8,128)(2,1)S(1)}, bf16[1024,4096]{1,0:T(8,128)(2,1)S(1)}, bf16[1344,1024]{1,0:T(8,128)(2,1)S(1)}) custom-call(s32[1]{0:T(128)} %bitcast.ep_ref, bf16[128,8320]{1,0:T(8,128)(2,1)} %constant_dynamic-update-slice_fusion.refs_0_, ...), custom_call_target="tpu_custom_call" | custom-call | flops 4697620480 | bytes 17301504 | tf_op jit(solution)/shard_map/experts/pallas_call | solution.py:144
  103.8 10.2 %experts.5 = (bf16[128,4224]{1,0:T(8,128)(2,1)S(1)}, bf16[128,4224]{1,0:T(8,128)(2,1)}, bf16[1024,4096]{1,0:T(8,128)(2,1)S(1)}, bf16[1024,4096]{1,0:T(8,128)(2,1)S(1)}, bf16[1344,1024]{1,0:T(8,128)(2,1)S(1)}) custom-call(s32[1]{0:T(128)} %bitcast.ep_ref, ...), custom_call_target="tpu_custom_call", output_to_operand_aliasing={{2}: (6, {}), {3}: (7, {}), {4}: (8, {})} | custom-call | flops 4697620480 | bytes 17301504 | tf_op jit(solution)/shard_map/experts/pallas_call | solution.py:144
  113.9 9.5 %experts.6 = (bf16[128,4224]{1,0:T(8,128)(2,1)S(1)}, bf16[128,4224]{1,0:T(8,128)(2,1)}, bf16[1024,4096]{1,0:T(8,128)(2,1)S(1)}, bf16[1024,4096]{1,0:T(8,128)(2,1)S(1)}, bf16[1344,1024]{1,0:T(8,128)(2,1)S(1)}) custom-call(s32[1]{0:T(128)} %bitcast.ep_ref, ...), custom_call_target="tpu_custom_call", output_to_operand_aliasing={{2}: (6, {}), {3}: (7, {}), {4}: (8, {})} | custom-call | flops 4697620480 | bytes 17301504 | tf_op jit(solution)/shard_map/experts/pallas_call | solution.py:144
  123.5 8.3 %experts.7 = (bf16[128,4224]{1,0:T(8,128)(2,1)S(1)}, bf16[128,4224]{1,0:T(8,128)(2,1)S(1)}, bf16[1024,4096]{1,0:T(8,128)(2,1)S(1)}, bf16[1024,4096]{1,0:T(8,128)(2,1)S(1)}, bf16[1344,1024]{1,0:T(8,128)(2,1)S(1)}) custom-call(s32[1]{0:T(128)} %bitcast.ep_ref, ...), custom_call_target="tpu_custom_call", output_to_operand_aliasing={{2}: (8, {}), {3}: (9, {}), {4}: (10, {})} | custom-call | flops 4697620480 | bytes 17301504 | tf_op jit(solution)/shard_map/experts/pallas_call | solution.py:144
  133.2 1.7 collective-permute-done.16
  135.5 2.5 %collective-permute-done.9 = bf16[128,4224]{1,0:T(8,128)(2,1)S(1)} collective-permute-done((bf16[128,4224]{1,0:T(8,128)(2,1)}, bf16[128,4224]{1,0:T(8,128)(2,1)S(1)}, u32[]{:S(2)}, u32[]{:S(2)}) %collective-permute-start.9) | collective-permute-done | bytes 1081376 | tf_op jit(solution)/shard_map/ppermute | solution.py:50
  139.9 6.0 %collective-permute-done.17 = bf16[64,4224]{1,0:T(8,128)(2,1)S(1)} collective-permute-done((bf16[64,4224]{1,0:T(8,128)(2,1)S(1)}, bf16[64,4224]{1,0:T(8,128)(2,1)S(1)}, u32[]{:S(2)}, u32[]{:S(2)}) %collective-permute-start.17) | collective-permute-done | bytes 540704 | tf_op jit(solution)/shard_map/ppermute | solution.py:50
  148.0 1.8 collective-permute-start.21
  149.8 12.7 %collective-permute-done.18 = bf16[128,4224]{1,0:T(8,128)(2,1)S(1)} collective-permute-done((bf16[128,4224]{1,0:T(8,128)(2,1)S(1)}, bf16[128,4224]{1,0:T(8,128)(2,1)S(1)}, u32[]{:S(2)}, u32[]{:S(2)}) %collective-permute-start.18) | collective-permute-done | bytes 1081376 | tf_op jit(solution)/shard_map/ppermute | solution.py:50
  163.8 3.2 %collective-permute-start.24 = (bf16[16,4224]{1,0:T(8,128)(2,1)S(1)}, bf16[16,4224]{1,0:T(8,128)(2,1)S(1)}, u32[]{:S(2)}, u32[]{:S(2)}) collective-permute-start(bf16[16,4224]{1,0:T(8,128)(2,1)S(1)} %get-tuple-element.48), channel_id=1, source_target_pairs={{0,96},{1,97},{2,26},{3,27},{4,100},{5,101},{6,30},{7,31},{8,104},... | collective-permute-start | bytes 405512 | tf_op jit(solution)/shard_map/ppermute | solution.py:50
  167.1 3.0 %collective-permute-done.22 = bf16[16,4224]{1,0:T(8,128)(2,1)S(1)} collective-permute-done((bf16[16,4224]{1,0:T(8,128)(2,1)S(1)}, bf16[16,4224]{1,0:T(8,128)(2,1)S(1)}, u32[]{:S(2)}, u32[]{:S(2)}) %collective-permute-start.22) | collective-permute-done | bytes 135200 | tf_op jit(solution)/shard_map/ppermute | solution.py:50
  170.3 3.3 %collective-permute-start.25 = (bf16[32,4224]{1,0:T(8,128)(2,1)S(1)}, bf16[32,4224]{1,0:T(8,128)(2,1)S(1)}, u32[]{:S(2)}, u32[]{:S(2)}) collective-permute-start(bf16[32,4224]{1,0:T(8,128)(2,1)S(1)} %pad_maximum_fusion.4), channel_id=1, source_target_pairs={{0,96},{1,97},{2,26},{3,27},{4,100},{5,101},{6,30},{7,31},{8,104},... | collective-permute-start | bytes 811016 | tf_op jit(solution)/shard_map/ppermute | solution.py:50
  173.6 6.3 %weights.4 = bf16[448,4096]{1,0:T(8,128)(2,1)} custom-call(bf16[1024,4096]{1,0:T(8,128)(2,1)S(1)} %get-tuple-element.42.side_ref, bf16[1344,1024]{1,0:T(8,128)(2,1)S(1)} %get-tuple-element.43.coef_ref), custom_call_target="tpu_custom_call" | custom-call | flops 3758096384 | bytes 12058624 | tf_op jit(solution)/shard_map/weights/pallas_call | solution.py:173
  181.7 6.3 %weights.3 = bf16[448,4096]{1,0:T(8,128)(2,1)} custom-call(bf16[1024,4096]{1,0:T(8,128)(2,1)S(1)} %get-tuple-element.42.side_ref, bf16[1344,1024]{1,0:T(8,128)(2,1)S(1)} %get-tuple-element.43.coef_ref), custom_call_target="tpu_custom_call" | custom-call | flops 3758096384 | bytes 12058624 | tf_op jit(solution)/shard_map/weights/pallas_call | solution.py:173
  188.0 3.0 %collective-permute-start.27 = (bf16[16,4224]{1,0:T(8,128)(2,1)S(1)}, bf16[16,4224]{1,0:T(8,128)(2,1)S(1)}, u32[]{:S(2)}, u32[]{:S(2)}) collective-permute-start(bf16[16,4224]{1,0:T(8,128)(2,1)S(1)} %add_convert_fusion.8), channel_id=1, source_target_pairs={{0,1},{1,0},{2,3},{3,2},{4,5},{5,4},{6,7},{7,6},{8,9},{9,8},{10,11... | collective-permute-start | bytes 405512 | tf_op jit(solution)/shard_map/ppermute | solution.py:50
  191.0 6.3 %weights.5 = bf16[448,4096]{1,0:T(8,128)(2,1)} custom-call(bf16[1024,4096]{1,0:T(8,128)(2,1)S(1)} %get-tuple-element.44.side_ref, bf16[1344,1024]{1,0:T(8,128)(2,1)S(1)} %get-tuple-element.43.coef_ref), custom_call_target="tpu_custom_call" | custom-call | flops 3758096384 | bytes 12058624 | tf_op jit(solution)/shard_map/weights/pallas_call | solution.py:173
  (84 shorter events, 22.8 us)
Async XLA Ops:
  3.9 8.1 %collective-permute-start = (bf16[16,8320]{1,0:T(8,128)(2,1)S(1)}, bf16[16,8320]{1,0:T(8,128)(2,1)S(1)}, u32[]{:S(2)}, u32[]{:S(2)}) collective-permute-start(bf16[16,8320]{1,0:T(8,128)(2,1)S(1)} %get-tuple-element.53), channel_id=1, source_target_pairs={{0,4},{1,5},{2,6},{3,7},{4,0},{5,1},{6,2},{7,3},{8,12},{9,13},{10,... | collective-permute-start | bytes 798728 | tf_op jit(solution)/shard_map/ppermute | solution.py:50
  13.0 9.8 %collective-permute-start.1 = (bf16[32,8320]{1,0:T(8,128)(2,1)S(1)}, bf16[32,8320]{1,0:T(8,128)(2,1)S(1)}, u32[]{:S(2)}, u32[]{:S(2)}) collective-permute-start(bf16[32,8320]{1,0:T(8,128)(2,1)S(1)} %pad_maximum_fusion.2), channel_id=1, source_target_pairs={{0,96},{1,97},{2,26},{3,27},{4,100},{5,101},{6,30},{7,31},{8,104},... | collective-permute-start | bytes 1597448 | tf_op jit(solution)/shard_map/ppermute | solution.py:50
  16.0 10.6 %collective-permute-start.2 = (bf16[32,8320]{1,0:T(8,128)(2,1)S(1)}, bf16[32,8320]{1,0:T(8,128)(2,1)S(1)}, u32[]{:S(2)}, u32[]{:S(2)}) collective-permute-start(bf16[32,8320]{1,0:T(8,128)(2,1)S(1)} %pad_maximum_fusion.2), channel_id=1, source_target_pairs={{0,32},{1,33},{2,10},{3,11},{4,36},{5,37},{6,14},{7,15},{8,40},{9,... | collective-permute-start | bytes 1597448 | tf_op jit(solution)/shard_map/ppermute | solution.py:50
  22.8 7.7 %collective-permute-start.3 = (bf16[16,8320]{1,0:T(8,128)(2,1)S(1)}, bf16[16,8320]{1,0:T(8,128)(2,1)S(1)}, u32[]{:S(2)}, u32[]{:S(2)}) collective-permute-start(bf16[16,8320]{1,0:T(8,128)(2,1)S(1)} %slice.110), channel_id=1, source_target_pairs={{0,96},{1,97},{2,26},{3,27},{4,100},{5,101},{6,30},{7,31},{8,104},... | collective-permute-start | bytes 798728 | tf_op jit(solution)/shard_map/ppermute | solution.py:50
  26.6 7.7 %collective-permute-start.4 = (bf16[16,8320]{1,0:T(8,128)(2,1)S(1)}, bf16[16,8320]{1,0:T(8,128)(2,1)S(1)}, u32[]{:S(2)}, u32[]{:S(2)}) collective-permute-start(bf16[16,8320]{1,0:T(8,128)(2,1)S(1)} %slice.111), channel_id=1, source_target_pairs={{0,32},{1,33},{2,10},{3,11},{4,36},{5,37},{6,14},{7,15},{8,40},{9,... | collective-permute-start | bytes 798728 | tf_op jit(solution)/shard_map/ppermute | solution.py:50
  35.0 28.3 %collective-permute-start.7 = (bf16[128,8320]{1,0:T(8,128)(2,1)}, bf16[128,8320]{1,0:T(8,128)(2,1)}, u32[]{:S(2)}, u32[]{:S(2)}) collective-permute-start(bf16[128,8320]{1,0:T(8,128)(2,1)} %constant_dynamic-update-slice_fusion.refs_0_), channel_id=1, source_target_pairs={{0,24},{1,25},{2,98},{3,99},{4,28},{5,29},{6,102},{7,103},{8,0},{9... | collective-permute-start | bytes 6389768 | tf_op jit(solution)/shard_map/ppermute | solution.py:50
  39.0 27.8 %collective-permute-start.11 = (bf16[128,8320]{1,0:T(8,128)(2,1)}, bf16[128,8320]{1,0:T(8,128)(2,1)S(1)}, u32[]{:S(2)}, u32[]{:S(2)}) collective-permute-start(bf16[128,8320]{1,0:T(8,128)(2,1)} %constant_dynamic-update-slice_fusion.refs_0_), channel_id=1, source_target_pairs={{0,8},{1,9},{2,34},{3,35},{4,12},{5,13},{6,38},{7,39},{8,16},{9,17... | collective-permute-start | bytes 6389768 | tf_op jit(solution)/shard_map/ppermute | solution.py:50
  39.0 48.3 %collective-permute-start.5 = (bf16[128,8320]{1,0:T(8,128)(2,1)}, bf16[128,8320]{1,0:T(8,128)(2,1)}, u32[]{:S(2)}, u32[]{:S(2)}) collective-permute-start(bf16[128,8320]{1,0:T(8,128)(2,1)} %constant_dynamic-update-slice_fusion.refs_0_), channel_id=1, source_target_pairs={{0,2},{1,3},{2,0},{3,1},{4,6},{5,7},{6,4},{7,5},{8,10},{9,11},{10,... | collective-permute-start | bytes 6389768 | tf_op jit(solution)/shard_map/ppermute | solution.py:50
  63.3 40.5 %collective-permute-start.8 = (bf16[128,8320]{1,0:T(8,128)(2,1)}, bf16[128,8320]{1,0:T(8,128)(2,1)}, u32[]{:S(2)}, u32[]{:S(2)}) collective-permute-start(bf16[128,8320]{1,0:T(8,128)(2,1)} %collective-permute-done.7.refs_0_), channel_id=1, source_target_pairs={{0,2},{1,3},{2,0},{3,1},{4,6},{5,7},{6,4},{7,5},{8,10},{9,11},{10,... | collective-permute-start | bytes 6389768 | tf_op jit(solution)/shard_map/ppermute | solution.py:50
  66.9 47.1 %collective-permute-start.15 = (bf16[128,8320]{1,0:T(8,128)(2,1)S(1)}, bf16[128,8320]{1,0:T(8,128)(2,1)}, u32[]{:S(2)}, u32[]{:S(2)}) collective-permute-start(bf16[128,8320]{1,0:T(8,128)(2,1)S(1)} %collective-permute-done.11.refs_0_), channel_id=1, source_target_pairs={{0,2},{1,3},{2,0},{3,1},{4,6},{5,7},{6,4},{7,5},{8,10},{9,11},{10,... | collective-permute-start | bytes 6389768 | tf_op jit(solution)/shard_map/ppermute | solution.py:50
  69.1 15.2 %collective-permute-start.10 = (bf16[64,8320]{1,0:T(8,128)(2,1)}, bf16[64,8320]{1,0:T(8,128)(2,1)S(1)}, u32[]{:S(2)}, u32[]{:S(2)}) collective-permute-start(bf16[64,8320]{1,0:T(8,128)(2,1)} %slice.113), channel_id=1, source_target_pairs={{0,24},{1,25},{2,98},{3,99},{4,28},{5,29},{6,102},{7,103},{8,0},{9... | collective-permute-start | bytes 3194888 | tf_op jit(solution)/shard_map/ppermute | solution.py:50
  70.8 16.5 %collective-permute-start.12 = (bf16[64,8320]{1,0:T(8,128)(2,1)}, bf16[64,8320]{1,0:T(8,128)(2,1)}, u32[]{:S(2)}, u32[]{:S(2)}) collective-permute-start(bf16[64,8320]{1,0:T(8,128)(2,1)} %slice.114), channel_id=1, source_target_pairs={{0,8},{1,9},{2,34},{3,35},{4,12},{5,13},{6,38},{7,39},{8,16},{9,17... | collective-permute-start | bytes 3194888 | tf_op jit(solution)/shard_map/ppermute | solution.py:50
  84.3 39.2 %collective-permute-start.13 = (bf16[64,8320]{1,0:T(8,128)(2,1)S(1)}, bf16[64,8320]{1,0:T(8,128)(2,1)S(1)}, u32[]{:S(2)}, u32[]{:S(2)}) collective-permute-start(bf16[64,8320]{1,0:T(8,128)(2,1)S(1)} %collective-permute-done.10.refs_0_), channel_id=1, source_target_pairs={{0,2},{1,3},{2,0},{3,1},{4,6},{5,7},{6,4},{7,5},{8,10},{9,11},{10,... | collective-permute-start | bytes 3194888 | tf_op jit(solution)/shard_map/ppermute | solution.py:50
  87.3 36.2 %collective-permute-start.14 = (bf16[64,8320]{1,0:T(8,128)(2,1)}, bf16[64,8320]{1,0:T(8,128)(2,1)S(1)}, u32[]{:S(2)}, u32[]{:S(2)}) collective-permute-start(bf16[64,8320]{1,0:T(8,128)(2,1)} %collective-permute-done.12.refs_1_), channel_id=1, source_target_pairs={{0,2},{1,3},{2,0},{3,1},{4,6},{5,7},{6,4},{7,5},{8,10},{9,11},{10,... | collective-permute-start | bytes 3194888 | tf_op jit(solution)/shard_map/ppermute | solution.py:50
  93.4 10.3 %copy-start.1 = (bf16[2,224,4096]{2,1,0:T(8,128)(2,1)S(1)}, bf16[2,224,4096]{2,1,0:T(8,128)(2,1)}, u32[]{:S(2)}) copy-start(bf16[2,224,4096]{2,1,0:T(8,128)(2,1)} %param.11) | copy-start | bytes 11010052
  93.4 10.3 %copy-start.3 = (bf16[2,224,4096]{2,1,0:T(8,128)(2,1)S(1)}, bf16[2,224,4096]{2,1,0:T(8,128)(2,1)}, u32[]{:S(2)}) copy-start(bf16[2,224,4096]{2,1,0:T(8,128)(2,1)} %param.12) | copy-start | bytes 11010052
  123.5 9.1 %copy-start.6 = (bf16[128,4224]{1,0:T(8,128)(2,1)S(1)}, bf16[128,4224]{1,0:T(8,128)(2,1)}, u32[]{:S(2)}) copy-start(bf16[128,4224]{1,0:T(8,128)(2,1)} %copy-done.5) | copy-start | bytes 3244036
  131.8 3.1 %collective-permute-start.16 = (bf16[128,4224]{1,0:T(8,128)(2,1)S(1)}, bf16[128,4224]{1,0:T(8,128)(2,1)S(1)}, u32[]{:S(2)}, u32[]{:S(2)}) collective-permute-start(bf16[128,4224]{1,0:T(8,128)(2,1)S(1)} %get-tuple-element.39), channel_id=1, source_target_pairs={{0,2},{1,3},{2,0},{3,1},{4,6},{5,7},{6,4},{7,5},{8,10},{9,11},{10,... | collective-permute-start | bytes 3244040 | tf_op jit(solution)/shard_map/ppermute | solution.py:50
  132.6 17.2 %collective-permute-start.6 = (bf16[128,4224]{1,0:T(8,128)(2,1)S(1)}, bf16[128,4224]{1,0:T(8,128)(2,1)S(1)}, u32[]{:S(2)}, u32[]{:S(2)}) collective-permute-start(bf16[128,4224]{1,0:T(8,128)(2,1)S(1)} %copy-done.6), channel_id=1, source_target_pairs={{0,2},{1,3},{2,0},{3,1},{4,6},{5,7},{6,4},{7,5},{8,10},{9,11},{10,... | collective-permute-start | bytes 3244040 | tf_op jit(solution)/shard_map/ppermute | solution.py:50
  132.7 5.3 %collective-permute-start.9 = (bf16[128,4224]{1,0:T(8,128)(2,1)}, bf16[128,4224]{1,0:T(8,128)(2,1)S(1)}, u32[]{:S(2)}, u32[]{:S(2)}) collective-permute-start(bf16[128,4224]{1,0:T(8,128)(2,1)} %get-tuple-element.31), channel_id=1, source_target_pairs={{0,2},{1,3},{2,0},{3,1},{4,6},{5,7},{6,4},{7,5},{8,10},{9,11},{10,... | collective-permute-start | bytes 3244040 | tf_op jit(solution)/shard_map/ppermute | solution.py:50
  133.1 6.5 %collective-permute-start.19 = (bf16[128,4224]{1,0:T(8,128)(2,1)}, bf16[128,4224]{1,0:T(8,128)(2,1)S(1)}, u32[]{:S(2)}, u32[]{:S(2)}) collective-permute-start(bf16[128,4224]{1,0:T(8,128)(2,1)} %get-tuple-element.41), channel_id=1, source_target_pairs={{0,2},{1,3},{2,0},{3,1},{4,6},{5,7},{6,4},{7,5},{8,10},{9,11},{10,... | collective-permute-start | bytes 3244040 | tf_op jit(solution)/shard_map/ppermute | solution.py:50
  135.2 10.6 %collective-permute-start.17 = (bf16[64,4224]{1,0:T(8,128)(2,1)S(1)}, bf16[64,4224]{1,0:T(8,128)(2,1)S(1)}, u32[]{:S(2)}, u32[]{:S(2)}) collective-permute-start(bf16[64,4224]{1,0:T(8,128)(2,1)S(1)} %get-tuple-element.51), channel_id=1, source_target_pairs={{0,8},{1,9},{2,34},{3,35},{4,12},{5,13},{6,38},{7,39},{8,16},{9,17... | collective-permute-start | bytes 1622024 | tf_op jit(solution)/shard_map/ppermute | solution.py:50
  138.3 9.4 %collective-permute-start.20 = (bf16[64,4224]{1,0:T(8,128)(2,1)S(1)}, bf16[64,4224]{1,0:T(8,128)(2,1)S(1)}, u32[]{:S(2)}, u32[]{:S(2)}) collective-permute-start(bf16[64,4224]{1,0:T(8,128)(2,1)S(1)} %get-tuple-element.52), channel_id=1, source_target_pairs={{0,24},{1,25},{2,98},{3,99},{4,28},{5,29},{6,102},{7,103},{8,0},{9... | collective-permute-start | bytes 1622024 | tf_op jit(solution)/shard_map/ppermute | solution.py:50
  146.1 16.4 %collective-permute-start.18 = (bf16[128,4224]{1,0:T(8,128)(2,1)S(1)}, bf16[128,4224]{1,0:T(8,128)(2,1)S(1)}, u32[]{:S(2)}, u32[]{:S(2)}) collective-permute-start(bf16[128,4224]{1,0:T(8,128)(2,1)S(1)} %pad_maximum_fusion), channel_id=1, source_target_pairs={{0,8},{1,9},{2,34},{3,35},{4,12},{5,13},{6,38},{7,39},{8,16},{9,17... | collective-permute-start | bytes 3244040 | tf_op jit(solution)/shard_map/ppermute | solution.py:50
  148.0 15.2 %collective-permute-start.21 = (bf16[128,4224]{1,0:T(8,128)(2,1)S(1)}, bf16[128,4224]{1,0:T(8,128)(2,1)S(1)}, u32[]{:S(2)}, u32[]{:S(2)}) collective-permute-start(bf16[128,4224]{1,0:T(8,128)(2,1)S(1)} %pad_maximum_fusion.1), channel_id=1, source_target_pairs={{0,24},{1,25},{2,98},{3,99},{4,28},{5,29},{6,102},{7,103},{8,0},{9... | collective-permute-start | bytes 3244040 | tf_op jit(solution)/shard_map/ppermute | solution.py:50
  163.8 6.3 %collective-permute-start.22 = (bf16[16,4224]{1,0:T(8,128)(2,1)S(1)}, bf16[16,4224]{1,0:T(8,128)(2,1)S(1)}, u32[]{:S(2)}, u32[]{:S(2)}) collective-permute-start(bf16[16,4224]{1,0:T(8,128)(2,1)S(1)} %get-tuple-element.47), channel_id=1, source_target_pairs={{0,32},{1,33},{2,10},{3,11},{4,36},{5,37},{6,14},{7,15},{8,40},{9,... | collective-permute-start | bytes 405512 | tf_op jit(solution)/shard_map/ppermute | solution.py:50
  163.8 6.2 %collective-permute-start.24 = (bf16[16,4224]{1,0:T(8,128)(2,1)S(1)}, bf16[16,4224]{1,0:T(8,128)(2,1)S(1)}, u32[]{:S(2)}, u32[]{:S(2)}) collective-permute-start(bf16[16,4224]{1,0:T(8,128)(2,1)S(1)} %get-tuple-element.48), channel_id=1, source_target_pairs={{0,96},{1,97},{2,26},{3,27},{4,100},{5,101},{6,30},{7,31},{8,104},... | collective-permute-start | bytes 405512 | tf_op jit(solution)/shard_map/ppermute | solution.py:50
  170.2 9.7 %collective-permute-start.23 = (bf16[32,4224]{1,0:T(8,128)(2,1)S(1)}, bf16[32,4224]{1,0:T(8,128)(2,1)S(1)}, u32[]{:S(2)}, u32[]{:S(2)}) collective-permute-start(bf16[32,4224]{1,0:T(8,128)(2,1)S(1)} %pad_maximum_fusion.3), channel_id=1, source_target_pairs={{0,32},{1,33},{2,10},{3,11},{4,36},{5,37},{6,14},{7,15},{8,40},{9,... | collective-permute-start | bytes 811016 | tf_op jit(solution)/shard_map/ppermute | solution.py:50
  170.3 9.6 %collective-permute-start.25 = (bf16[32,4224]{1,0:T(8,128)(2,1)S(1)}, bf16[32,4224]{1,0:T(8,128)(2,1)S(1)}, u32[]{:S(2)}, u32[]{:S(2)}) collective-permute-start(bf16[32,4224]{1,0:T(8,128)(2,1)S(1)} %pad_maximum_fusion.4), channel_id=1, source_target_pairs={{0,96},{1,97},{2,26},{3,27},{4,100},{5,101},{6,30},{7,31},{8,104},... | collective-permute-start | bytes 811016 | tf_op jit(solution)/shard_map/ppermute | solution.py:50
  180.0 8.0 %collective-permute-start.26 = (bf16[16,4224]{1,0:T(8,128)(2,1)S(1)}, bf16[16,4224]{1,0:T(8,128)(2,1)S(1)}, u32[]{:S(2)}, u32[]{:S(2)}) collective-permute-start(bf16[16,4224]{1,0:T(8,128)(2,1)S(1)} %slice.128), channel_id=1, source_target_pairs={{0,4},{1,5},{2,6},{3,7},{4,0},{5,1},{6,2},{7,3},{8,12},{9,13},{10,... | collective-permute-start | bytes 405512 | tf_op jit(solution)/shard_map/ppermute | solution.py:50
  188.0 9.3 %collective-permute-start.27 = (bf16[16,4224]{1,0:T(8,128)(2,1)S(1)}, bf16[16,4224]{1,0:T(8,128)(2,1)S(1)}, u32[]{:S(2)}, u32[]{:S(2)}) collective-permute-start(bf16[16,4224]{1,0:T(8,128)(2,1)S(1)} %add_convert_fusion.8), channel_id=1, source_target_pairs={{0,1},{1,0},{2,3},{3,2},{4,5},{5,4},{6,7},{7,6},{8,9},{9,8},{10,11... | collective-permute-start | bytes 405512 | tf_op jit(solution)/shard_map/ppermute | solution.py:50
  191.0 7.1 %copy-start.7 = (s32[16,2]{0,1:T(2,128)S(1)}, s32[16,2]{0,1:T(2,128)}, u32[]{:S(2)}) copy-start(s32[16,2]{0,1:T(2,128)} %param.9) | copy-start | bytes 388
  (4 other events, 7.1 us)

commit v2 on v1

--- a/solution.py
+++ b/solution.py
@@ -13,7 +13,7 @@
 D = 4096
 EXTRA = 128
 EXPERTS = 4
-TILE = 512
+TILE = 1024
 BF16, F32 = jnp.bfloat16, jnp.float32
 
 
@@ -44,34 +44,141 @@
 OTHER_Y = pairs(lambda x, z, y, c, e: (x, z, y + 1, c, e))
 OTHER_CORE = pairs(lambda x, z, y, c, e: (x, z, y, c + 1, e))
 OTHER_EP = pairs(lambda x, z, y, c, e: (x, z, y, c, e + 1))
+OTHER_BOTH = pairs(lambda x, z, y, c, e: (x, z, y + 1, c, e + 1))
 
 
 def sent(value, to):
     return lax.ppermute(value, AXES, to)
 
 
-def ring(v, step):
-    half = v.shape[0] // 2
-    ahead, behind = sent(v, step(-1)), sent(v, step(1))
-    far_a = sent(ahead[:half], step(-1))
-    return ahead, behind, far_a, sent(behind[half:], step(1))
-
-
-def plus(a, *others):
-    total = a.astype(F32)
-    for b in others:
-        total = total + b.astype(F32)
-    return total.astype(BF16)
-
-
-def ring_back(own, ahead, behind, far, step):
-    half = own.shape[0] // 2
-    to_ahead = sent(far[:half], step(1))
-    to_behind = sent(far[half:], step(-1))
-    ahead = jnp.concatenate([plus(ahead[:half], to_ahead), ahead[half:]], axis=0)
-    behind = jnp.concatenate([behind[:half], plus(behind[half:], to_behind)], axis=0)
-    up = sent(ahead, step(1))
-    return plus(own, up, sent(behind, step(-1)))
+def joined_kernel(*refs):
+    out, at = refs[-1], 0
+    for r in refs[:-1]:
+        out[at : at + r.shape[0], :] = r[...]
+        at += r.shape[0]
+
+
+def packed_kernel(ep_ref, x_ref, y_ref, extra_ref, out_ref, done):
+    wide = x_ref.shape[1]
+    x_copy = pltpu.make_async_copy(x_ref, out_ref.at[:, :wide], done.at[0])
+    y_copy = pltpu.make_async_copy(y_ref, out_ref.at[:, wide : 2 * wide], done.at[1])
+    x_copy.start()
+    y_copy.start()
+    out_ref[:, 2 * wide :] = extra_ref[...]
+    x_copy.wait()
+    y_copy.wait()
+
+
+VM = pl.BlockSpec(memory_space=pltpu.VMEM)
+
+
+def joined(*arrays):
+    shape = (sum(a.shape[0] for a in arrays), arrays[0].shape[1])
+    return pl.pallas_call(
+        joined_kernel,
+        out_shape=jax.ShapeDtypeStruct(shape, BF16),
+        in_specs=[VM] * len(arrays),
+        out_specs=VM,
+        compiler_params=pltpu.CompilerParams(vmem_limit_bytes=8 * 1024 * 1024),
+        name="joined",
+    )(*arrays)
+
+
+def taken_kernel(start, v_ref, out_ref):
+    out_ref[...] = v_ref[start : start + out_ref.shape[0], :]
+
+
+def taken(v, start, rows):
+    return pl.pallas_call(
+        functools.partial(taken_kernel, start),
+        out_shape=jax.ShapeDtypeStruct((rows, v.shape[1]), BF16),
+        in_specs=[VM],
+        out_specs=VM,
+        compiler_params=pltpu.CompilerParams(vmem_limit_bytes=8 * 1024 * 1024),
+        name="taken",
+    )(v)
+
+
+def packed(ep, x, y, extra):
+    shape = (x.shape[0], x.shape[1] + y.shape[1] + extra.shape[1])
+    held = pl.BlockSpec(memory_space=pltpu.HBM)
+    return pl.pallas_call(
+        packed_kernel,
+        out_shape=jax.ShapeDtypeStruct(shape, BF16),
+        in_specs=[pl.BlockSpec(memory_space=pltpu.SMEM), held, held, VM],
+        out_specs=VM,
+        scratch_shapes=[pltpu.SemaphoreType.DMA((2,))],
+        compiler_params=pltpu.CompilerParams(vmem_limit_bytes=60 * 1024 * 1024),
+        name="packed",
+    )(ep, x, y, extra)
+
+
+def touched_kernel(*refs):
+    refs[-1][...] = jnp.zeros_like(refs[-1])
+
+
+def touched(*arrays):
+    return pl.pallas_call(
+        touched_kernel,
+        out_shape=jax.ShapeDtypeStruct((8, 128), F32),
+        in_specs=[VM] * len(arrays),
+        out_specs=VM,
+        compiler_params=pltpu.CompilerParams(
+            vmem_limit_bytes=1024 * 1024, has_side_effects=True
+        ),
+        name="touched",
+    )(*arrays)
+
+
+STEP = 16
+
+
+def sums_kernel(plan, count, *refs):
+    ins, outs = refs[:count], refs[count:]
+    for out, (rows, terms) in zip(outs, plan):
+        for r in range(0, rows, STEP):
+            total = None
+            for i, source, first_row, n in terms:
+                if first_row <= r < first_row + n:
+                    at = source + r - first_row
+                    part = ins[i][at : at + STEP, :].astype(F32)
+                    total = part if total is None else total + part
+            out[r : r + STEP, :] = total.astype(BF16)
+
+
+def sums(arrays, plan):
+    width = arrays[0].shape[1]
+    return pl.pallas_call(
+        functools.partial(sums_kernel, plan, len(arrays)),
+        out_shape=tuple(jax.ShapeDtypeStruct((rows, width), BF16) for rows, _ in plan),
+        in_specs=[VM] * len(arrays),
+        out_specs=(VM,) * len(plan),
+        compiler_params=pltpu.CompilerParams(vmem_limit_bytes=8 * 1024 * 1024),
+        name="sums",
+    )(*arrays)
+
+
+def last_kernel(own, same, other, other_pair, grad_ref, slot_ref):
+    total = (own[...].astype(F32) + same[...].astype(F32)) + (
+        other[...].astype(F32) + other_pair[...].astype(F32)
+    )
+    grad_ref[...] = total[:, :D].astype(BF16)
+    slot_ref[...] = total[:, D:]
+
+
+def last(*arrays):
+    rows = arrays[0].shape[0]
+    return pl.pallas_call(
+        last_kernel,
+        out_shape=(
+            jax.ShapeDtypeStruct((rows, D), BF16),
+            jax.ShapeDtypeStruct((rows, EXTRA), F32),
+        ),
+        in_specs=[VM] * 4,
+        out_specs=(VM, VM),
+        compiler_params=pltpu.CompilerParams(vmem_limit_bytes=4 * 1024 * 1024),
+        name="last",
+    )(*arrays)
 
 
 NT = (((1,), (1,)), ((), ()))
@@ -137,15 +244,14 @@
 def expert_group(ep, chunks, weights, held, at, total):
     tokens = sum(c.shape[0] for c in chunks)
     hidden2 = weights[0].shape[0]
-    vm = pl.BlockSpec(memory_space=pltpu.VMEM)
     part = jax.ShapeDtypeStruct((tokens // 2, D + EXTRA), BF16)
     whole = jax.ShapeDtypeStruct((total, D), BF16)
     before = 1 + len(chunks) + 3
     mine, theirs, *held = pl.pallas_call(
         functools.partial(expert_kernel, len(chunks), len(held), at),
         out_shape=(part, part, whole, whole, jax.ShapeDtypeStruct((3 * hidden2, total), BF16)),
-        in_specs=[pl.BlockSpec(memory_space=pltpu.SMEM)] + [vm] * (len(chunks) + 3 + len(held)),
-        out_specs=(vm,) * 5,
+        in_specs=[pl.BlockSpec(memory_space=pltpu.SMEM)] + [VM] * (len(chunks) + 3 + len(held)),
+        out_specs=(VM,) * 5,
         scratch_shapes=[pltpu.VMEM((tokens, hidden2), BF16), pltpu.VMEM((tokens, hidden2), BF16)],
         input_output_aliases={before + i: 2 + i for i in range(len(held))},
         cost_estimate=pl.CostEstimate(
@@ -169,12 +275,11 @@
 
 def weight_grad(which, side, coef):
     tokens, hidden2 = side.shape[0], coef.shape[0] // 3
-    vm = pl.BlockSpec(memory_space=pltpu.VMEM)
     return pl.pallas_call(
         functools.partial(weight_kernel, which),
         grid=(D // TILE,),
         out_shape=jax.ShapeDtypeStruct((hidden2, D), BF16),
-        in_specs=[vm, vm],
+        in_specs=[VM, VM],
         out_specs=pl.BlockSpec((hidden2, TILE), lambda j: (0, j)),
         cost_estimate=pl.CostEstimate(
             flops=2 * tokens * D * hidden2,
@@ -189,41 +294,86 @@
 def shards(hidden_in, out_grad, expert_ids, gate_values, w_gate, w_up, w_down):
     local, hidden = w_gate.shape[:2]
     wg, wu, wd = (w.reshape(local * hidden, D) for w in (w_gate, w_up, w_down))
+    touched(wg, wu, wd)
     ep = lax.axis_index("ep").astype(jnp.int32).reshape(1)
-    experts = lax.broadcasted_iota(jnp.int32, (1, EXTRA), 1)
-    weights = sum(
-        jnp.where(expert_ids[:, k : k + 1] == experts, gate_values[:, k : k + 1], 0)
-        for k in range(expert_ids.shape[1])
-    ).astype(BF16)
-    own = jnp.concatenate([hidden_in, out_grad, weights], axis=1)
-
-    two = jnp.concatenate([own, sent(own, OTHER_Y)], axis=0)
-    near = jnp.concatenate([two, *ring(two, first)], axis=0)
-    near_c = sent(near, OTHER_CORE)
-    ahead, behind, far_a, far_b = ring(near, second)
-    ahead_c, behind_c = sent(ahead, OTHER_CORE), sent(behind, OTHER_CORE)
-    far_ac, far_bc = sent(far_a, OTHER_CORE), sent(far_b, OTHER_CORE)
-
-    groups = ((near, near_c), (ahead, ahead_c), (behind, behind_c), (far_a, far_b, far_ac, far_bc))
-    sums, held, at = [], (), 0
-    tokens = hidden_in.shape[0] * X * Z * Y * CORE
-    for group in groups:
+    experts = lax.broadcasted_iota(jnp.int32, (1, 1, EXTRA), 2)
+    chosen = expert_ids[:, :, None] == experts
+    weights = jnp.sum(jnp.where(chosen, gate_values[:, :, None], jnp.zeros((), BF16)), axis=1)
+    own = packed(ep, hidden_in, out_grad, weights)
+    one = own.shape[0]
+    two = joined(own, sent(own, OTHER_Y))
+
+    n_a, n_b = sent(two, first(-1)), sent(two, first(1))
+    n_far = sent(two, first(2))
+    near = joined(n_a, n_b)
+    m_a, m_b = sent(near, second(-1)), sent(near, second(1))
+    rest = joined(two, n_far)
+    e_a, e_b = sent(rest, second(-1)), sent(rest, second(1))
+    h = two.shape[0]
+    fm_a = sent(taken(m_a, 0, h), second(-1))
+    fm_b = sent(taken(m_b, h, h), second(1))
+    fe_a = sent(taken(e_a, 0, h), second(-1))
+    fe_b = sent(taken(e_b, h, h), second(1))
+
+    groups = []
+    for group in ((near, rest), (m_a, m_b), (e_a, e_b), (fm_a, fm_b, fe_a, fe_b)):
+        both = [sent(c, OTHER_CORE) for c in group]
+        groups.append((*group, *both))
+
+    parts, held, at = {}, (), 0
+    tokens = one * X * Z * Y * CORE
+    for g in (0, 1, 3, 2):
+        group = groups[g]
         mine, theirs, held = expert_group(ep, group, (wg, wu, wd), held, at, tokens)
         at += sum(c.shape[0] for c in group)
-        sums.append(plus(mine, sent(theirs, OTHER_CORE)))
+        parts[g] = (mine, sent(theirs, OTHER_CORE))
     x_all, y_all, coef_all = held
 
-    total = ring_back(*sums, second)
-    q = total.shape[0] // 4
-    total = ring_back(*(total[i * q : (i + 1) * q] for i in range(4)), first)
-    q = total.shape[0] // 2
-    total = plus(total[:q], sent(total[q:], OTHER_Y))
-    other = sent(total, OTHER_EP)
-    total = total.astype(F32) + other.astype(F32)
-    input_grad = total[:, :D].astype(BF16)
-    slot = total[:, D : D + EXPERTS]
-    ids = lax.broadcasted_iota(jnp.int32, (1, 1, EXPERTS), 2)
-    gate_grad = jnp.sum(jnp.where(expert_ids[:, :, None] == ids, slot[:, None, :], 0.0), axis=2)
+    up, down = sums(
+        parts[3],
+        tuple(
+            (2 * h, tuple((i, s * h + k * 2 * h, k * h, h) for i in (0, 1) for k in (0, 1)))
+            for s in (0, 1)
+        ),
+    )
+    up, down = sent(up, second(1)), sent(down, second(-1))
+    n = 2 * h
+    g_a, t_a, g_b, t_b = sums(
+        (*parts[1], up, *parts[2], down),
+        (
+            (3 * h, ((0, 0, 0, n), (1, 0, 0, n), (2, 0, 0, h), (3, h, n, h), (4, h, n, h))),
+            (h, ((3, 0, 0, h), (4, 0, 0, h), (2, h, 0, h))),
+            (
+                3 * h,
+                ((0, n, 0, n), (1, n, 0, n), (5, 0, h, h))
+                + ((3, n + h, n, h), (4, n + h, n, h), (5, h, n, h)),
+            ),
+            (h, ((3, n, 0, h), (4, n, 0, h))),
+        ),
+    )
+    g_a, g_b = sent(g_a, second(1)), sent(g_b, second(-1))
+    t_a, t_b = sent(t_a, second(1)), sent(t_b, second(-1))
+    n_a, n_b, n_far = sums(
+        (*parts[0], g_a, g_b),
+        tuple(
+            (h, ((0, at, 0, h), (1, at, 0, h), (2, i * h, 0, h), (3, i * h, 0, h)))
+            for i, at in enumerate((0, h, 3 * h))
+        ),
+    )
+    n_a, n_b = sent(n_a, first(1)), sent(n_b, first(-1))
+    n_far = sent(n_far, first(2))
+    own, pair = sums(
+        (*parts[0], t_a, t_b, n_a, n_b, n_far),
+        tuple(
+            (one, tuple((i, a * one + (n if i < 2 else 0), 0, one) for i in range(7)))
+            for a in range(2)
+        ),
+    )
+    same = sent(pair, OTHER_Y)
+    other, other_pair = sent(own, OTHER_EP), sent(pair, OTHER_BOTH)
+    input_grad, slot = last(own, same, other, other_pair)
+    picked = expert_ids[:, :, None] == lax.broadcasted_iota(jnp.int32, (1, 1, EXPERTS), 2)
+    gate_grad = jnp.sum(jnp.where(picked, slot[:, None, :EXPERTS], 0.0), axis=2)
 
     grads = []
     for which, side in enumerate((x_all, x_all, y_all)):

time: 199 us -> 157 us (0.79)
  waiting for transfers between devices: 89.4 us -> 70.1 us
  local copies, waits for them, and re-layouts: 16.7 us -> 1.05 us
  Pallas kernels: 56.3 us -> 47.2 us
  starting transfers between devices: 30.1 us -> 36 us
  other arithmetic: 5.34 us -> 1.94 us
    ppermute x28 -> x38, waiting for transfers between devices: 89.4 us -> 70.1 us  [sent(): return lax.ppermute(value, AXES, to)]
    pallas_call x4, Pallas kernels: 37.3 us -> 25.3 us  [expert_group(): pl.pallas_call(functools.partial(expert_kernel, len(chunks), len(held), a...]
    unnamed x20 -> x10, local copies, waits for them, and re-layouts: 10.2 us -> 0.97 us
    ppermute x28 -> x38, starting transfers between devices: 30.1 us -> 36 us  [sent(): return lax.ppermute(value, AXES, to)]
    pallas_call x0 -> x14, Pallas kernels: none -> 5.6 us  [the longest x1 2.37 us: packed(): pl.pallas_call(packed_kernel, out_shape=jax.ShapeDtypeStruct(shape, BF16)...]
    slice x12 -> x1, local copies, waits for them, and re-layouts: 4.31 us -> 0.08 us  [shards(): gate_grad = jnp.sum(jnp.where(picked, slot[:, None, :EXPERTS], 0.0), axis=2)]
    concatenate x6 -> x0, other arithmetic: 2.9 us -> none  [the longest x1 1.71 us: shards(): own = jnp.concatenate([hidden_in, out_grad, weights], axis=1)]
    pallas_call x3, Pallas kernels: 19 us -> 16.3 us  [weight_grad(): pl.pallas_call(functools.partial(weight_kernel, which), grid=(D // TILE,)...]
  transfers between devices with their start and end apart: 28 -> 38, of which waited for: 16 -> 15; matrix products, arithmetic and copies ran while one was open for 4% -> 0% of each run, Pallas kernels for 24% -> 28%
where the time goes in v2:
time: 157 us
  waiting for transfers between devices  70.1 us (45%)
  Pallas kernels  47.2 us (30%)
  starting transfers between devices  36 us (23%)
  other arithmetic  1.94 us (1%)
    ppermute x38, waiting for transfers between devices, sent(): return lax.ppermute(value, AXES, to)  70.1 us
    ppermute x38, starting transfers between devices, sent(): return lax.ppermute(value, AXES, to)  36 us
    pallas_call x4, Pallas kernels, expert_group(): pl.pallas_call(functools.partial(expert_kernel, len(chunks), len(held), a...  25.3 us
    pallas_call x3, Pallas kernels, weight_grad(): pl.pallas_call(functools.partial(weight_kernel, which), grid=(D // TILE,)...  16.3 us
  transfers between devices with their start and end apart: 38, of which 15 were waited for; matrix products, arithmetic and copies ran while one was open for 0% of the time, Pallas kernels for 28%

profile of v2, /device:TPU:0, one launch (start us, length us, event | category | flops | bytes accessed | tf_op | source)
XLA Modules:
  0.0 157.1 jit_solution(6545264948742265374)
XLA Ops:
  0.6 1.4 fusion.1.extra_ref
  2.0 2.4 %packed.1.refs_0_ = bf16[16,8320]{1,0:T(8,128)(2,1)} custom-call(s32[1]{0:T(128)} %bitcast.3.ep_ref, bf16[16,4096]{1,0:T(8,128)(2,1)} %x_ref.1, bf16[16,4096]{1,0:T(8,128)(2,1)} %y_ref.1, bf16[16,128]{1,0:T(8,128)(2,1)} %fusion.1.extra_ref), custom_call_target="tpu_custom_call" | custom-call | tf_op jit(solution)/shard_map/packed/pallas_call | solution.py:105
  4.4 1.8 %collective-permute-start = (bf16[16,8320]{1,0:T(8,128)(2,1)}, bf16[16,8320]{1,0:T(8,128)(2,1)S(1)}, u32[]{:S(2)}, u32[]{:S(2)}) collective-permute-start(bf16[16,8320]{1,0:T(8,128)(2,1)} %packed.1.refs_0_), channel_id=1, source_target_pairs={{0,4},{1,5},{2,6},{3,7},{4,0},{5,1},{6,2},{7,3},{8,12},{9,13},{10,... | collective-permute-start | bytes 798728 | tf_op jit(solution)/shard_map/ppermute | solution.py:51
  6.1 6.6 %collective-permute-done.refs_1_ = bf16[16,8320]{1,0:T(8,128)(2,1)S(1)} collective-permute-done((bf16[16,8320]{1,0:T(8,128)(2,1)}, bf16[16,8320]{1,0:T(8,128)(2,1)S(1)}, u32[]{:S(2)}, u32[]{:S(2)}) %collective-permute-start) | collective-permute-done | bytes 266272 | tf_op jit(solution)/shard_map/ppermute | solution.py:51
  13.7 3.0 %collective-permute-start.1 = (bf16[32,8320]{1,0:T(8,128)(2,1)S(1)}, bf16[32,8320]{1,0:T(8,128)(2,1)S(1)}, u32[]{:S(2)}, u32[]{:S(2)}) collective-permute-start(bf16[32,8320]{1,0:T(8,128)(2,1)S(1)} %joined.3.refs_0_), channel_id=1, source_target_pairs={{0,96},{1,97},{2,26},{3,27},{4,100},{5,101},{6,30},{7,31},{8,104},... | collective-permute-start | bytes 1597448 | tf_op jit(solution)/shard_map/ppermute | solution.py:51
  16.7 6.8 %collective-permute-done.1.refs_0_ = bf16[32,8320]{1,0:T(8,128)(2,1)S(1)} collective-permute-done((bf16[32,8320]{1,0:T(8,128)(2,1)S(1)}, bf16[32,8320]{1,0:T(8,128)(2,1)S(1)}, u32[]{:S(2)}, u32[]{:S(2)}) %collective-permute-start.1) | collective-permute-done | bytes 532512 | tf_op jit(solution)/shard_map/ppermute | solution.py:51
  23.5 3.7 %collective-permute-done.2.refs_1_ = bf16[32,8320]{1,0:T(8,128)(2,1)S(1)} collective-permute-done((bf16[32,8320]{1,0:T(8,128)(2,1)S(1)}, bf16[32,8320]{1,0:T(8,128)(2,1)S(1)}, u32[]{:S(2)}, u32[]{:S(2)}) %collective-permute-start.2) | collective-permute-done | bytes 532512 | tf_op jit(solution)/shard_map/ppermute | solution.py:51
  27.3 4.1 %collective-permute-start.7 = (bf16[64,8320]{1,0:T(8,128)(2,1)S(1)}, bf16[64,8320]{1,0:T(8,128)(2,1)S(1)}, u32[]{:S(2)}, u32[]{:S(2)}) collective-permute-start(bf16[64,8320]{1,0:T(8,128)(2,1)S(1)} %joined.4.refs_0_), channel_id=1, source_target_pairs={{0,24},{1,25},{2,98},{3,99},{4,28},{5,29},{6,102},{7,103},{8,0},{9... | collective-permute-start | bytes 3194888 | tf_op jit(solution)/shard_map/ppermute | solution.py:51
  31.4 16.5 %collective-permute-done.3.refs_1_ = bf16[32,8320]{1,0:T(8,128)(2,1)S(1)} collective-permute-done((bf16[32,8320]{1,0:T(8,128)(2,1)S(1)}, bf16[32,8320]{1,0:T(8,128)(2,1)S(1)}, u32[]{:S(2)}, u32[]{:S(2)}) %collective-permute-start.3) | collective-permute-done | bytes 532512 | tf_op jit(solution)/shard_map/ppermute | solution.py:51
  48.4 1.6 %collective-permute-start.16 = (bf16[64,8320]{1,0:T(8,128)(2,1)S(1)}, bf16[64,8320]{1,0:T(8,128)(2,1)S(1)}, u32[]{:S(2)}, u32[]{:S(2)}) collective-permute-start(bf16[64,8320]{1,0:T(8,128)(2,1)S(1)} %joined.5.refs_1_), channel_id=1, source_target_pairs={{0,8},{1,9},{2,34},{3,35},{4,12},{5,13},{6,38},{7,39},{8,16},{9,17... | collective-permute-start | bytes 3194888 | tf_op jit(solution)/shard_map/ppermute | solution.py:51
  50.6 1.3 collective-permute-start.12
  52.0 11.0 %collective-permute-done.14.v_ref.refs_0_ = bf16[64,8320]{1,0:T(8,128)(2,1)S(1)} collective-permute-done((bf16[64,8320]{1,0:T(8,128)(2,1)S(1)}, bf16[64,8320]{1,0:T(8,128)(2,1)S(1)}, u32[]{:S(2)}, u32[]{:S(2)}) %collective-permute-start.14) | collective-permute-done | bytes 1064992 | tf_op jit(solution)/shard_map/ppermute | solution.py:51
  63.0 1.6 %collective-permute-done.16.v_ref.refs_1_ = bf16[64,8320]{1,0:T(8,128)(2,1)S(1)} collective-permute-done((bf16[64,8320]{1,0:T(8,128)(2,1)S(1)}, bf16[64,8320]{1,0:T(8,128)(2,1)S(1)}, u32[]{:S(2)}, u32[]{:S(2)}) %collective-permute-start.16) | collective-permute-done | bytes 1064992 | tf_op jit(solution)/shard_map/ppermute | solution.py:51
  65.1 2.9 %collective-permute-start.15 = (bf16[32,8320]{1,0:T(8,128)(2,1)S(1)}, bf16[32,8320]{1,0:T(8,128)(2,1)S(1)}, u32[]{:S(2)}, u32[]{:S(2)}) collective-permute-start(bf16[32,8320]{1,0:T(8,128)(2,1)S(1)} %taken.6), channel_id=1, source_target_pairs={{0,24},{1,25},{2,98},{3,99},{4,28},{5,29},{6,102},{7,103},{8,0},{9... | collective-permute-start | bytes 1597448 | tf_op jit(solution)/shard_map/ppermute | solution.py:51
  68.7 6.4 %collective-permute-done.13.refs_1_ = bf16[32,8320]{1,0:T(8,128)(2,1)S(1)} collective-permute-done((bf16[32,8320]{1,0:T(8,128)(2,1)S(1)}, bf16[32,8320]{1,0:T(8,128)(2,1)S(1)}, u32[]{:S(2)}, u32[]{:S(2)}) %collective-permute-start.13) | collective-permute-done | bytes 532512 | tf_op jit(solution)/shard_map/ppermute | solution.py:51
  75.6 5.2 %collective-permute-done.17.refs_3_ = bf16[32,8320]{1,0:T(8,128)(2,1)S(1)} collective-permute-done((bf16[32,8320]{1,0:T(8,128)(2,1)S(1)}, bf16[32,8320]{1,0:T(8,128)(2,1)S(1)}, u32[]{:S(2)}, u32[]{:S(2)}) %collective-permute-start.17) | collective-permute-done | bytes 532512 | tf_op jit(solution)/shard_map/ppermute | solution.py:51
  81.8 6.3 %experts.4 = (bf16[128,4224]{1,0:T(8,128)(2,1)S(1)}, bf16[128,4224]{1,0:T(8,128)(2,1)S(1)}, bf16[1024,4096]{1,0:T(8,128)(2,1)S(1)}, bf16[1024,4096]{1,0:T(8,128)(2,1)S(1)}, bf16[1344,1024]{1,0:T(8,128)(2,1)S(1)}) custom-call(s32[1]{0:T(128)} %bitcast.3.ep_ref, bf16[64,8320]{1,0:T(8,128)(2,1)S(1)} %joined.4.refs_0_, bf16[64,8320]{1,0:T(8,128)(2,1)S(1)} %joined.5.refs_1_, ...), custom_call_target="tpu_custom_call" | custom-call | flops 4697620480 | bytes 17301504 | tf_op jit(solution)/shard_map/experts/pallas_call | solution.py:250
  88.2 6.3 %experts.5 = (bf16[128,4224]{1,0:T(8,128)(2,1)S(1)}, bf16[128,4224]{1,0:T(8,128)(2,1)S(1)}, bf16[1024,4096]{1,0:T(8,128)(2,1)S(1)}, bf16[1024,4096]{1,0:T(8,128)(2,1)S(1)}, bf16[1344,1024]{1,0:T(8,128)(2,1)S(1)}) custom-call(s32[1]{0:T(128)} %bitcast.3.ep_ref, ...), custom_call_target="tpu_custom_call", output_to_operand_aliasing={{2}: (8, {}), {3}: (9, {}), {4}: (10, {})} | custom-call | flops 4697620480 | bytes 17301504 | tf_op jit(solution)/shard_map/experts/pallas_call | solution.py:250
  94.5 6.3 %experts.6 = (bf16[128,4224]{1,0:T(8,128)(2,1)S(1)}, bf16[128,4224]{1,0:T(8,128)(2,1)S(1)}, bf16[1024,4096]{1,0:T(8,128)(2,1)S(1)}, bf16[1024,4096]{1,0:T(8,128)(2,1)S(1)}, bf16[1344,1024]{1,0:T(8,128)(2,1)S(1)}) custom-call(s32[1]{0:T(128)} %bitcast.3.ep_ref, ...), custom_call_target="tpu_custom_call", output_to_operand_aliasing={{2}: (12, {}), {3}: (13, {}), {4}: (14, {})} | custom-call | flops 4697620480 | bytes 17301504 | tf_op jit(solution)/shard_map/experts/pallas_call | solution.py:250
  101.5 6.3 %experts.7 = (bf16[128,4224]{1,0:T(8,128)(2,1)S(1)}, bf16[128,4224]{1,0:T(8,128)(2,1)S(1)}, bf16[1024,4096]{1,0:T(8,128)(2,1)S(1)}, bf16[1024,4096]{1,0:T(8,128)(2,1)S(1)}, bf16[1344,1024]{1,0:T(8,128)(2,1)S(1)}) custom-call(s32[1]{0:T(128)} %bitcast.3.ep_ref, ...), custom_call_target="tpu_custom_call", output_to_operand_aliasing={{2}: (8, {}), {3}: (9, {}), {4}: (10, {})} | custom-call | flops 4697620480 | bytes 17301504 | tf_op jit(solution)/shard_map/experts/pallas_call | solution.py:250
  108.5 3.2 %collective-permute-start.27 = (bf16[64,4224]{1,0:T(8,128)(2,1)S(1)}, bf16[64,4224]{1,0:T(8,128)(2,1)S(1)}, u32[]{:S(2)}, u32[]{:S(2)}) collective-permute-start(bf16[64,4224]{1,0:T(8,128)(2,1)S(1)} %get-tuple-element.56), channel_id=1, source_target_pairs={{0,24},{1,25},{2,98},{3,99},{4,28},{5,29},{6,102},{7,103},{8,0},{9... | collective-permute-start | bytes 1622024 | tf_op jit(solution)/shard_map/ppermute | solution.py:51
  111.7 7.3 %collective-permute-done.23.refs_2_ = bf16[64,4224]{1,0:T(8,128)(2,1)S(1)} collective-permute-done((bf16[64,4224]{1,0:T(8,128)(2,1)S(1)}, bf16[64,4224]{1,0:T(8,128)(2,1)S(1)}, u32[]{:S(2)}, u32[]{:S(2)}) %collective-permute-start.23) | collective-permute-done | bytes 540704 | tf_op jit(solution)/shard_map/ppermute | solution.py:51
  119.8 3.3 %collective-permute-start.31 = (bf16[96,4224]{1,0:T(8,128)(2,1)S(1)}, bf16[96,4224]{1,0:T(8,128)(2,1)S(1)}, u32[]{:S(2)}, u32[]{:S(2)}) collective-permute-start(bf16[96,4224]{1,0:T(8,128)(2,1)S(1)} %get-tuple-element.60), channel_id=1, source_target_pairs={{0,24},{1,25},{2,98},{3,99},{4,28},{5,29},{6,102},{7,103},{8,0},{9... | collective-permute-start | bytes 2433032 | tf_op jit(solution)/shard_map/ppermute | solution.py:51
  123.7 5.4 %weights.3 = bf16[448,4096]{1,0:T(8,128)(2,1)} custom-call(bf16[1024,4096]{1,0:T(8,128)(2,1)S(1)} %get-tuple-element.68.side_ref, bf16[1344,1024]{1,0:T(8,128)(2,1)S(1)} %get-tuple-element.69.coef_ref), custom_call_target="tpu_custom_call" | custom-call | flops 3758096384 | bytes 12058624 | tf_op jit(solution)/shard_map/weights/pallas_call | solution.py:278
  129.2 3.2 %collective-permute-start.29 = (bf16[32,4224]{1,0:T(8,128)(2,1)S(1)}, bf16[32,4224]{1,0:T(8,128)(2,1)S(1)}, u32[]{:S(2)}, u32[]{:S(2)}) collective-permute-start(bf16[32,4224]{1,0:T(8,128)(2,1)S(1)} %get-tuple-element.58), channel_id=1, source_target_pairs={{0,24},{1,25},{2,98},{3,99},{4,28},{5,29},{6,102},{7,103},{8,0},{9... | collective-permute-start | bytes 811016 | tf_op jit(solution)/shard_map/ppermute | solution.py:51
  133.8 3.2 %collective-permute-start.33 = (bf16[32,4224]{1,0:T(8,128)(2,1)S(1)}, bf16[32,4224]{1,0:T(8,128)(2,1)S(1)}, u32[]{:S(2)}, u32[]{:S(2)}) collective-permute-start(bf16[32,4224]{1,0:T(8,128)(2,1)S(1)} %get-tuple-element.62), channel_id=1, source_target_pairs={{0,96},{1,97},{2,26},{3,27},{4,100},{5,101},{6,30},{7,31},{8,104},... | collective-permute-start | bytes 811016 | tf_op jit(solution)/shard_map/ppermute | solution.py:51
  137.0 5.4 %weights.4 = bf16[448,4096]{1,0:T(8,128)(2,1)} custom-call(bf16[1024,4096]{1,0:T(8,128)(2,1)S(1)} %get-tuple-element.68.side_ref, bf16[1344,1024]{1,0:T(8,128)(2,1)S(1)} %get-tuple-element.69.coef_ref), custom_call_target="tpu_custom_call" | custom-call | flops 3758096384 | bytes 12058624 | tf_op jit(solution)/shard_map/weights/pallas_call | solution.py:278
  142.5 1.4 collective-permute-done.33.refs_5_
  143.9 1.1 collective-permute-done.34.refs_6_
  145.2 1.7 %collective-permute-start.35 = (bf16[16,4224]{1,0:T(8,128)(2,1)S(1)}, bf16[16,4224]{1,0:T(8,128)(2,1)S(1)}, u32[]{:S(2)}, u32[]{:S(2)}) collective-permute-start(bf16[16,4224]{1,0:T(8,128)(2,1)S(1)} %get-tuple-element.65), channel_id=1, source_target_pairs={{0,4},{1,5},{2,6},{3,7},{4,0},{5,1},{6,2},{7,3},{8,12},{9,13},{10,... | collective-permute-start | bytes 405512 | tf_op jit(solution)/shard_map/ppermute | solution.py:51
  146.9 2.2 %collective-permute-start.37 = (bf16[16,4224]{1,0:T(8,128)(2,1)S(1)}, bf16[16,4224]{1,0:T(8,128)(2,1)S(1)}, u32[]{:S(2)}, u32[]{:S(2)}) collective-permute-start(bf16[16,4224]{1,0:T(8,128)(2,1)S(1)} %get-tuple-element.65), channel_id=1, source_target_pairs={{0,5},{1,4},{2,7},{3,6},{4,1},{5,0},{6,3},{7,2},{8,13},{9,12},{10,... | collective-permute-start | bytes 405512 | tf_op jit(solution)/shard_map/ppermute | solution.py:51
  149.8 5.4 %weights.5 = bf16[448,4096]{1,0:T(8,128)(2,1)} custom-call(bf16[1024,4096]{1,0:T(8,128)(2,1)S(1)} %get-tuple-element.70.side_ref, bf16[1344,1024]{1,0:T(8,128)(2,1)S(1)} %get-tuple-element.69.coef_ref), custom_call_target="tpu_custom_call" | custom-call | flops 3758096384 | bytes 12058624 | tf_op jit(solution)/shard_map/weights/pallas_call | solution.py:278
  (78 shorter events, 11.9 us)
Async XLA Ops:
  13.7 9.8 %collective-permute-start.1 = (bf16[32,8320]{1,0:T(8,128)(2,1)S(1)}, bf16[32,8320]{1,0:T(8,128)(2,1)S(1)}, u32[]{:S(2)}, u32[]{:S(2)}) collective-permute-start(bf16[32,8320]{1,0:T(8,128)(2,1)S(1)} %joined.3.refs_0_), channel_id=1, source_target_pairs={{0,96},{1,97},{2,26},{3,27},{4,100},{5,101},{6,30},{7,31},{8,104},... | collective-permute-start | bytes 1597448 | tf_op jit(solution)/shard_map/ppermute | solution.py:51
  16.7 10.5 %collective-permute-start.2 = (bf16[32,8320]{1,0:T(8,128)(2,1)S(1)}, bf16[32,8320]{1,0:T(8,128)(2,1)S(1)}, u32[]{:S(2)}, u32[]{:S(2)}) collective-permute-start(bf16[32,8320]{1,0:T(8,128)(2,1)S(1)} %joined.3.refs_0_), channel_id=1, source_target_pairs={{0,32},{1,33},{2,10},{3,11},{4,36},{5,37},{6,14},{7,15},{8,40},{9,... | collective-permute-start | bytes 1597448 | tf_op jit(solution)/shard_map/ppermute | solution.py:51
  27.3 22.8 %collective-permute-start.7 = (bf16[64,8320]{1,0:T(8,128)(2,1)S(1)}, bf16[64,8320]{1,0:T(8,128)(2,1)S(1)}, u32[]{:S(2)}, u32[]{:S(2)}) collective-permute-start(bf16[64,8320]{1,0:T(8,128)(2,1)S(1)} %joined.4.refs_0_), channel_id=1, source_target_pairs={{0,24},{1,25},{2,98},{3,99},{4,28},{5,29},{6,102},{7,103},{8,0},{9... | collective-permute-start | bytes 3194888 | tf_op jit(solution)/shard_map/ppermute | solution.py:51
  31.4 16.5 %collective-permute-start.3 = (bf16[32,8320]{1,0:T(8,128)(2,1)S(1)}, bf16[32,8320]{1,0:T(8,128)(2,1)S(1)}, u32[]{:S(2)}, u32[]{:S(2)}) collective-permute-start(bf16[32,8320]{1,0:T(8,128)(2,1)S(1)} %joined.3.refs_0_), channel_id=1, source_target_pairs={{0,64},{1,65},{2,18},{3,19},{4,68},{5,69},{6,22},{7,23},{8,72},{9,... | collective-permute-start | bytes 1597448 | tf_op jit(solution)/shard_map/ppermute | solution.py:51
  31.4 19.2 %collective-permute-start.8 = (bf16[64,8320]{1,0:T(8,128)(2,1)S(1)}, bf16[64,8320]{1,0:T(8,128)(2,1)S(1)}, u32[]{:S(2)}, u32[]{:S(2)}) collective-permute-start(bf16[64,8320]{1,0:T(8,128)(2,1)S(1)} %joined.4.refs_0_), channel_id=1, source_target_pairs={{0,8},{1,9},{2,34},{3,35},{4,12},{5,13},{6,38},{7,39},{8,16},{9,17... | collective-permute-start | bytes 3194888 | tf_op jit(solution)/shard_map/ppermute | solution.py:51
  31.4 20.5 %collective-permute-start.4 = (bf16[64,8320]{1,0:T(8,128)(2,1)S(1)}, bf16[64,8320]{1,0:T(8,128)(2,1)S(1)}, u32[]{:S(2)}, u32[]{:S(2)}) collective-permute-start(bf16[64,8320]{1,0:T(8,128)(2,1)S(1)} %joined.4.refs_0_), channel_id=1, source_target_pairs={{0,2},{1,3},{2,0},{3,1},{4,6},{5,7},{6,4},{7,5},{8,10},{9,11},{10,... | collective-permute-start | bytes 3194888 | tf_op jit(solution)/shard_map/ppermute | solution.py:51
  47.9 15.0 %collective-permute-start.14 = (bf16[64,8320]{1,0:T(8,128)(2,1)S(1)}, bf16[64,8320]{1,0:T(8,128)(2,1)S(1)}, u32[]{:S(2)}, u32[]{:S(2)}) collective-permute-start(bf16[64,8320]{1,0:T(8,128)(2,1)S(1)} %joined.5.refs_1_), channel_id=1, source_target_pairs={{0,24},{1,25},{2,98},{3,99},{4,28},{5,29},{6,102},{7,103},{8,0},{9... | collective-permute-start | bytes 3194888 | tf_op jit(solution)/shard_map/ppermute | solution.py:51
  48.4 16.2 %collective-permute-start.16 = (bf16[64,8320]{1,0:T(8,128)(2,1)S(1)}, bf16[64,8320]{1,0:T(8,128)(2,1)S(1)}, u32[]{:S(2)}, u32[]{:S(2)}) collective-permute-start(bf16[64,8320]{1,0:T(8,128)(2,1)S(1)} %joined.5.refs_1_), channel_id=1, source_target_pairs={{0,8},{1,9},{2,34},{3,35},{4,12},{5,13},{6,38},{7,39},{8,16},{9,17... | collective-permute-start | bytes 3194888 | tf_op jit(solution)/shard_map/ppermute | solution.py:51
  50.0 15.1 %collective-permute-start.5 = (bf16[64,8320]{1,0:T(8,128)(2,1)S(1)}, bf16[64,8320]{1,0:T(8,128)(2,1)S(1)}, u32[]{:S(2)}, u32[]{:S(2)}) collective-permute-start(bf16[64,8320]{1,0:T(8,128)(2,1)S(1)} %joined.5.refs_1_), channel_id=1, source_target_pairs={{0,2},{1,3},{2,0},{3,1},{4,6},{5,7},{6,4},{7,5},{8,10},{9,11},{10,... | collective-permute-start | bytes 3194888 | tf_op jit(solution)/shard_map/ppermute | solution.py:51
  50.6 18.1 %collective-permute-start.12 = (bf16[32,8320]{1,0:T(8,128)(2,1)S(1)}, bf16[32,8320]{1,0:T(8,128)(2,1)S(1)}, u32[]{:S(2)}, u32[]{:S(2)}) collective-permute-start(bf16[32,8320]{1,0:T(8,128)(2,1)S(1)} %taken.4), channel_id=1, source_target_pairs={{0,24},{1,25},{2,98},{3,99},{4,28},{5,29},{6,102},{7,103},{8,0},{9... | collective-permute-start | bytes 1597448 | tf_op jit(solution)/shard_map/ppermute | solution.py:51
  51.9 28.9 %collective-permute-start.9 = (bf16[64,8320]{1,0:T(8,128)(2,1)S(1)}, bf16[64,8320]{1,0:T(8,128)(2,1)S(1)}, u32[]{:S(2)}, u32[]{:S(2)}) collective-permute-start(bf16[64,8320]{1,0:T(8,128)(2,1)S(1)} %collective-permute-done.7.refs_0_.v_ref), channel_id=1, source_target_pairs={{0,2},{1,3},{2,0},{3,1},{4,6},{5,7},{6,4},{7,5},{8,10},{9,11},{10,... | collective-permute-start | bytes 3194888 | tf_op jit(solution)/shard_map/ppermute | solution.py:51
  63.0 18.3 %collective-permute-start.10 = (bf16[64,8320]{1,0:T(8,128)(2,1)S(1)}, bf16[64,8320]{1,0:T(8,128)(2,1)S(1)}, u32[]{:S(2)}, u32[]{:S(2)}) collective-permute-start(bf16[64,8320]{1,0:T(8,128)(2,1)S(1)} %collective-permute-done.8.refs_1_.v_ref), channel_id=1, source_target_pairs={{0,2},{1,3},{2,0},{3,1},{4,6},{5,7},{6,4},{7,5},{8,10},{9,11},{10,... | collective-permute-start | bytes 3194888 | tf_op jit(solution)/shard_map/ppermute | solution.py:51
  64.6 10.5 %collective-permute-start.13 = (bf16[32,8320]{1,0:T(8,128)(2,1)S(1)}, bf16[32,8320]{1,0:T(8,128)(2,1)S(1)}, u32[]{:S(2)}, u32[]{:S(2)}) collective-permute-start(bf16[32,8320]{1,0:T(8,128)(2,1)S(1)} %taken.5), channel_id=1, source_target_pairs={{0,8},{1,9},{2,34},{3,35},{4,12},{5,13},{6,38},{7,39},{8,16},{9,17... | collective-permute-start | bytes 1597448 | tf_op jit(solution)/shard_map/ppermute | solution.py:51
  65.1 10.0 %collective-permute-start.15 = (bf16[32,8320]{1,0:T(8,128)(2,1)S(1)}, bf16[32,8320]{1,0:T(8,128)(2,1)S(1)}, u32[]{:S(2)}, u32[]{:S(2)}) collective-permute-start(bf16[32,8320]{1,0:T(8,128)(2,1)S(1)} %taken.6), channel_id=1, source_target_pairs={{0,24},{1,25},{2,98},{3,99},{4,28},{5,29},{6,102},{7,103},{8,0},{9... | collective-permute-start | bytes 1597448 | tf_op jit(solution)/shard_map/ppermute | solution.py:51
  68.7 12.1 %collective-permute-start.17 = (bf16[32,8320]{1,0:T(8,128)(2,1)S(1)}, bf16[32,8320]{1,0:T(8,128)(2,1)S(1)}, u32[]{:S(2)}, u32[]{:S(2)}) collective-permute-start(bf16[32,8320]{1,0:T(8,128)(2,1)S(1)} %taken.7), channel_id=1, source_target_pairs={{0,8},{1,9},{2,34},{3,35},{4,12},{5,13},{6,38},{7,39},{8,16},{9,17... | collective-permute-start | bytes 1597448 | tf_op jit(solution)/shard_map/ppermute | solution.py:51
  75.1 26.4 %collective-permute-start.24 = (bf16[64,8320]{1,0:T(8,128)(2,1)S(1)}, bf16[64,8320]{1,0:T(8,128)(2,1)S(1)}, u32[]{:S(2)}, u32[]{:S(2)}) collective-permute-start(bf16[64,8320]{1,0:T(8,128)(2,1)S(1)} %collective-permute-done.14.v_ref.refs_0_), channel_id=1, source_target_pairs={{0,2},{1,3},{2,0},{3,1},{4,6},{5,7},{6,4},{7,5},{8,10},{9,11},{10,... | collective-permute-start | bytes 3194888 | tf_op jit(solution)/shard_map/ppermute | solution.py:51
  80.8 20.7 %collective-permute-start.25 = (bf16[64,8320]{1,0:T(8,128)(2,1)S(1)}, bf16[64,8320]{1,0:T(8,128)(2,1)S(1)}, u32[]{:S(2)}, u32[]{:S(2)}) collective-permute-start(bf16[64,8320]{1,0:T(8,128)(2,1)S(1)} %collective-permute-done.16.v_ref.refs_1_), channel_id=1, source_target_pairs={{0,2},{1,3},{2,0},{3,1},{4,6},{5,7},{6,4},{7,5},{8,10},{9,11},{10,... | collective-permute-start | bytes 3194888 | tf_op jit(solution)/shard_map/ppermute | solution.py:51
  80.8 13.7 %collective-permute-start.19 = (bf16[32,8320]{1,0:T(8,128)(2,1)S(1)}, bf16[32,8320]{1,0:T(8,128)(2,1)S(1)}, u32[]{:S(2)}, u32[]{:S(2)}) collective-permute-start(bf16[32,8320]{1,0:T(8,128)(2,1)S(1)} %collective-permute-done.13.refs_1_), channel_id=1, source_target_pairs={{0,2},{1,3},{2,0},{3,1},{4,6},{5,7},{6,4},{7,5},{8,10},{9,11},{10,... | collective-permute-start | bytes 1597448 | tf_op jit(solution)/shard_map/ppermute | solution.py:51
  81.3 13.2 %collective-permute-start.20 = (bf16[32,8320]{1,0:T(8,128)(2,1)S(1)}, bf16[32,8320]{1,0:T(8,128)(2,1)S(1)}, u32[]{:S(2)}, u32[]{:S(2)}) collective-permute-start(bf16[32,8320]{1,0:T(8,128)(2,1)S(1)} %collective-permute-done.15.refs_2_), channel_id=1, source_target_pairs={{0,2},{1,3},{2,0},{3,1},{4,6},{5,7},{6,4},{7,5},{8,10},{9,11},{10,... | collective-permute-start | bytes 1597448 | tf_op jit(solution)/shard_map/ppermute | solution.py:51
  81.4 13.1 %collective-permute-start.21 = (bf16[32,8320]{1,0:T(8,128)(2,1)S(1)}, bf16[32,8320]{1,0:T(8,128)(2,1)S(1)}, u32[]{:S(2)}, u32[]{:S(2)}) collective-permute-start(bf16[32,8320]{1,0:T(8,128)(2,1)S(1)} %collective-permute-done.17.refs_3_), channel_id=1, source_target_pairs={{0,2},{1,3},{2,0},{3,1},{4,6},{5,7},{6,4},{7,5},{8,10},{9,11},{10,... | collective-permute-start | bytes 1597448 | tf_op jit(solution)/shard_map/ppermute | solution.py:51
  101.2 10.5 %collective-permute-start.11 = (bf16[128,4224]{1,0:T(8,128)(2,1)S(1)}, bf16[128,4224]{1,0:T(8,128)(2,1)S(1)}, u32[]{:S(2)}, u32[]{:S(2)}) collective-permute-start(bf16[128,4224]{1,0:T(8,128)(2,1)S(1)} %get-tuple-element.44), channel_id=1, source_target_pairs={{0,2},{1,3},{2,0},{3,1},{4,6},{5,7},{6,4},{7,5},{8,10},{9,11},{10,... | collective-permute-start | bytes 3244040 | tf_op jit(solution)/shard_map/ppermute | solution.py:51
  108.4 10.6 %collective-permute-start.23 = (bf16[64,4224]{1,0:T(8,128)(2,1)S(1)}, bf16[64,4224]{1,0:T(8,128)(2,1)S(1)}, u32[]{:S(2)}, u32[]{:S(2)}) collective-permute-start(bf16[64,4224]{1,0:T(8,128)(2,1)S(1)} %get-tuple-element.50), channel_id=1, source_target_pairs={{0,8},{1,9},{2,34},{3,35},{4,12},{5,13},{6,38},{7,39},{8,16},{9,17... | collective-permute-start | bytes 1622024 | tf_op jit(solution)/shard_map/ppermute | solution.py:51
  108.5 10.6 %collective-permute-start.27 = (bf16[64,4224]{1,0:T(8,128)(2,1)S(1)}, bf16[64,4224]{1,0:T(8,128)(2,1)S(1)}, u32[]{:S(2)}, u32[]{:S(2)}) collective-permute-start(bf16[64,4224]{1,0:T(8,128)(2,1)S(1)} %get-tuple-element.56), channel_id=1, source_target_pairs={{0,24},{1,25},{2,98},{3,99},{4,28},{5,29},{6,102},{7,103},{8,0},{9... | collective-permute-start | bytes 1622024 | tf_op jit(solution)/shard_map/ppermute | solution.py:51
  111.7 20.7 %collective-permute-start.6 = (bf16[128,4224]{1,0:T(8,128)(2,1)S(1)}, bf16[128,4224]{1,0:T(8,128)(2,1)S(1)}, u32[]{:S(2)}, u32[]{:S(2)}) collective-permute-start(bf16[128,4224]{1,0:T(8,128)(2,1)S(1)} %get-tuple-element.39), channel_id=1, source_target_pairs={{0,2},{1,3},{2,0},{3,1},{4,6},{5,7},{6,4},{7,5},{8,10},{9,11},{10,... | collective-permute-start | bytes 3244040 | tf_op jit(solution)/shard_map/ppermute | solution.py:51
  119.7 13.5 %collective-permute-start.30 = (bf16[96,4224]{1,0:T(8,128)(2,1)S(1)}, bf16[96,4224]{1,0:T(8,128)(2,1)S(1)}, u32[]{:S(2)}, u32[]{:S(2)}) collective-permute-start(bf16[96,4224]{1,0:T(8,128)(2,1)S(1)} %get-tuple-element.59), channel_id=1, source_target_pairs={{0,8},{1,9},{2,34},{3,35},{4,12},{5,13},{6,38},{7,39},{8,16},{9,17... | collective-permute-start | bytes 2433032 | tf_op jit(solution)/shard_map/ppermute | solution.py:51
  119.8 13.5 %collective-permute-start.31 = (bf16[96,4224]{1,0:T(8,128)(2,1)S(1)}, bf16[96,4224]{1,0:T(8,128)(2,1)S(1)}, u32[]{:S(2)}, u32[]{:S(2)}) collective-permute-start(bf16[96,4224]{1,0:T(8,128)(2,1)S(1)} %get-tuple-element.60), channel_id=1, source_target_pairs={{0,24},{1,25},{2,98},{3,99},{4,28},{5,29},{6,102},{7,103},{8,0},{9... | collective-permute-start | bytes 2433032 | tf_op jit(solution)/shard_map/ppermute | solution.py:51
  129.2 13.3 %collective-permute-start.28 = (bf16[32,4224]{1,0:T(8,128)(2,1)S(1)}, bf16[32,4224]{1,0:T(8,128)(2,1)S(1)}, u32[]{:S(2)}, u32[]{:S(2)}) collective-permute-start(bf16[32,4224]{1,0:T(8,128)(2,1)S(1)} %get-tuple-element.57), channel_id=1, source_target_pairs={{0,8},{1,9},{2,34},{3,35},{4,12},{5,13},{6,38},{7,39},{8,16},{9,17... | collective-permute-start | bytes 811016 | tf_op jit(solution)/shard_map/ppermute | solution.py:51
  129.2 13.3 %collective-permute-start.29 = (bf16[32,4224]{1,0:T(8,128)(2,1)S(1)}, bf16[32,4224]{1,0:T(8,128)(2,1)S(1)}, u32[]{:S(2)}, u32[]{:S(2)}) collective-permute-start(bf16[32,4224]{1,0:T(8,128)(2,1)S(1)} %get-tuple-element.58), channel_id=1, source_target_pairs={{0,24},{1,25},{2,98},{3,99},{4,28},{5,29},{6,102},{7,103},{8,0},{9... | collective-permute-start | bytes 811016 | tf_op jit(solution)/shard_map/ppermute | solution.py:51
  133.7 8.8 %collective-permute-start.32 = (bf16[32,4224]{1,0:T(8,128)(2,1)S(1)}, bf16[32,4224]{1,0:T(8,128)(2,1)S(1)}, u32[]{:S(2)}, u32[]{:S(2)}) collective-permute-start(bf16[32,4224]{1,0:T(8,128)(2,1)S(1)} %get-tuple-element.61), channel_id=1, source_target_pairs={{0,32},{1,33},{2,10},{3,11},{4,36},{5,37},{6,14},{7,15},{8,40},{9,... | collective-permute-start | bytes 811016 | tf_op jit(solution)/shard_map/ppermute | solution.py:51
  133.8 10.1 %collective-permute-start.33 = (bf16[32,4224]{1,0:T(8,128)(2,1)S(1)}, bf16[32,4224]{1,0:T(8,128)(2,1)S(1)}, u32[]{:S(2)}, u32[]{:S(2)}) collective-permute-start(bf16[32,4224]{1,0:T(8,128)(2,1)S(1)} %get-tuple-element.62), channel_id=1, source_target_pairs={{0,96},{1,97},{2,26},{3,27},{4,100},{5,101},{6,30},{7,31},{8,104},... | collective-permute-start | bytes 811016 | tf_op jit(solution)/shard_map/ppermute | solution.py:51
  145.2 10.0 %collective-permute-start.35 = (bf16[16,4224]{1,0:T(8,128)(2,1)S(1)}, bf16[16,4224]{1,0:T(8,128)(2,1)S(1)}, u32[]{:S(2)}, u32[]{:S(2)}) collective-permute-start(bf16[16,4224]{1,0:T(8,128)(2,1)S(1)} %get-tuple-element.65), channel_id=1, source_target_pairs={{0,4},{1,5},{2,6},{3,7},{4,0},{5,1},{6,2},{7,3},{8,12},{9,13},{10,... | collective-permute-start | bytes 405512 | tf_op jit(solution)/shard_map/ppermute | solution.py:51
  146.9 8.8 %collective-permute-start.37 = (bf16[16,4224]{1,0:T(8,128)(2,1)S(1)}, bf16[16,4224]{1,0:T(8,128)(2,1)S(1)}, u32[]{:S(2)}, u32[]{:S(2)}) collective-permute-start(bf16[16,4224]{1,0:T(8,128)(2,1)S(1)} %get-tuple-element.65), channel_id=1, source_target_pairs={{0,5},{1,4},{2,7},{3,6},{4,1},{5,0},{6,3},{7,2},{8,13},{9,12},{10,... | collective-permute-start | bytes 405512 | tf_op jit(solution)/shard_map/ppermute | solution.py:51
  (11 other events, 180.2 us)

commit v3 on v2

--- a/solution.py
+++ b/solution.py
@@ -108,7 +108,7 @@
         in_specs=[pl.BlockSpec(memory_space=pltpu.SMEM), held, held, VM],
         out_specs=VM,
         scratch_shapes=[pltpu.SemaphoreType.DMA((2,))],
-        compiler_params=pltpu.CompilerParams(vmem_limit_bytes=60 * 1024 * 1024),
+        compiler_params=pltpu.CompilerParams(vmem_limit_bytes=8 * 1024 * 1024),
         name="packed",
     )(ep, x, y, extra)
 
@@ -303,20 +303,16 @@
     one = own.shape[0]
     two = joined(own, sent(own, OTHER_Y))
 
-    n_a, n_b = sent(two, first(-1)), sent(two, first(1))
-    n_far = sent(two, first(2))
-    near = joined(n_a, n_b)
+    n_a, n_b, n_far = sent(two, first(-1)), sent(two, first(1)), sent(two, first(2))
+    near = joined(n_a, n_b, two)
     m_a, m_b = sent(near, second(-1)), sent(near, second(1))
-    rest = joined(two, n_far)
-    e_a, e_b = sent(rest, second(-1)), sent(rest, second(1))
-    h = two.shape[0]
-    fm_a = sent(taken(m_a, 0, h), second(-1))
-    fm_b = sent(taken(m_b, h, h), second(1))
-    fe_a = sent(taken(e_a, 0, h), second(-1))
-    fe_b = sent(taken(e_b, h, h), second(1))
+    e_a, e_b = sent(n_far, second(-1)), sent(n_far, second(1))
+    k, j = near.shape[0] // 2, n_far.shape[0] // 2
+    fm_a, fm_b = sent(taken(m_a, 0, k), second(-1)), sent(taken(m_b, k, k), second(1))
+    fe_a, fe_b = sent(taken(e_a, 0, j), second(-1)), sent(taken(e_b, j, j), second(1))
 
     groups = []
-    for group in ((near, rest), (m_a, m_b), (e_a, e_b), (fm_a, fm_b, fe_a, fe_b)):
+    for group in ((near, n_far), (m_a, e_a), (m_b, e_b), (fm_a, fe_a, fm_b, fe_b)):
         both = [sent(c, OTHER_CORE) for c in group]
         groups.append((*group, *both))
 
@@ -329,26 +325,25 @@
         parts[g] = (mine, sent(theirs, OTHER_CORE))
     x_all, y_all, coef_all = held
 
+    h, r = two.shape[0], k + j
+    n = 2 * h
     up, down = sums(
-        parts[3],
-        tuple(
-            (2 * h, tuple((i, s * h + k * 2 * h, k * h, h) for i in (0, 1) for k in (0, 1)))
-            for s in (0, 1)
-        ),
+        parts[3], tuple((r, ((0, i * r, 0, r), (1, i * r, 0, r))) for i in (0, 1))
     )
     up, down = sent(up, second(1)), sent(down, second(-1))
-    n = 2 * h
-    g_a, t_a, g_b, t_b = sums(
-        (*parts[1], up, *parts[2], down),
+    line = ((0, 0, 0, n), (1, 0, 0, n), (0, n + h, n, h), (1, n + h, n, h))
+    g_a, t_a = sums(
+        (*parts[1], up),
         (
-            (3 * h, ((0, 0, 0, n), (1, 0, 0, n), (2, 0, 0, h), (3, h, n, h), (4, h, n, h))),
-            (h, ((3, 0, 0, h), (4, 0, 0, h), (2, h, 0, h))),
-            (
-                3 * h,
-                ((0, n, 0, n), (1, n, 0, n), (5, 0, h, h))
-                + ((3, n + h, n, h), (4, n + h, n, h), (5, h, n, h)),
-            ),
-            (h, ((3, n, 0, h), (4, n, 0, h))),
+            (n + h, (*line, (2, 0, 0, k), (2, k, n, j))),
+            (h, ((0, n, 0, h), (1, n, 0, h))),
+        ),
+    )
+    g_b, t_b = sums(
+        (*parts[2], down),
+        (
+            (n + h, (*line, (2, 0, k, n - k), (2, k, n + j, j))),
+            (h, ((0, n, 0, h), (1, n, 0, h), (2, n - k, 0, h))),
         ),
     )
     g_a, g_b = sent(g_a, second(1)), sent(g_b, second(-1))

time: 157 us -> 154 us (0.981)
  waiting for transfers between devices: 70.1 us -> 65 us
  starting transfers between devices: 36 us -> 39.7 us
  Pallas kernels: 47.2 us -> 45 us
    ppermute x38, waiting for transfers between devices: 70.1 us -> 65 us  [sent(): return lax.ppermute(value, AXES, to)]
    ppermute x38, starting transfers between devices: 36 us -> 39.7 us  [sent(): return lax.ppermute(value, AXES, to)]
    pallas_call x1, Pallas kernels: 2.37 us -> 0.17 us  [packed(): pl.pallas_call(packed_kernel, out_shape=jax.ShapeDtypeStruct(shape, BF16)...]
where the time goes in v3:
time: 154 us
  waiting for transfers between devices  65 us (42%)
  Pallas kernels  45 us (29%)
  starting transfers between devices  39.7 us (26%)
  local copies, waits for them, and re-layouts  1.91 us (1%)
    ppermute x38, waiting for transfers between devices, sent(): return lax.ppermute(value, AXES, to)  65 us
    ppermute x38, starting transfers between devices, sent(): return lax.ppermute(value, AXES, to)  39.7 us
    pallas_call x4, Pallas kernels, expert_group(): pl.pallas_call(functools.partial(expert_kernel, len(chunks), len(held), a...  25.3 us
    pallas_call x3, Pallas kernels, weight_grad(): pl.pallas_call(functools.partial(weight_kernel, which), grid=(D // TILE,)...  16.3 us
  transfers between devices with their start and end apart: 38, of which 15 were waited for; matrix products, arithmetic and copies ran while one was open for 0% of the time, Pallas kernels for 28%

profile of v3, /device:TPU:0, one launch (start us, length us, event | category | flops | bytes accessed | tf_op | source)
XLA Modules:
  0.0 153.8 jit_solution(16597191304577337808)
XLA Ops:
  3.4 1.8 %collective-permute-start = (bf16[16,8320]{1,0:T(8,128)(2,1)S(1)}, bf16[16,8320]{1,0:T(8,128)(2,1)S(1)}, u32[]{:S(2)}, u32[]{:S(2)}) collective-permute-start(bf16[16,8320]{1,0:T(8,128)(2,1)S(1)} %packed.1.refs_0_), channel_id=1, source_target_pairs={{0,4},{1,5},{2,6},{3,7},{4,0},{5,1},{6,2},{7,3},{8,12},{9,13},{10,... | collective-permute-start | bytes 798728 | tf_op jit(solution)/shard_map/ppermute | solution.py:51
  5.2 6.4 %collective-permute-done.refs_1_ = bf16[16,8320]{1,0:T(8,128)(2,1)S(1)} collective-permute-done((bf16[16,8320]{1,0:T(8,128)(2,1)S(1)}, bf16[16,8320]{1,0:T(8,128)(2,1)S(1)}, u32[]{:S(2)}, u32[]{:S(2)}) %collective-permute-start) | collective-permute-done | bytes 266272 | tf_op jit(solution)/shard_map/ppermute | solution.py:51
  11.6 3.0 %collective-permute-start.1 = (bf16[32,8320]{1,0:T(8,128)(2,1)S(1)}, bf16[32,8320]{1,0:T(8,128)(2,1)S(1)}, u32[]{:S(2)}, u32[]{:S(2)}) collective-permute-start(bf16[32,8320]{1,0:T(8,128)(2,1)S(1)} %joined.2.refs_2_), channel_id=1, source_target_pairs={{0,96},{1,97},{2,26},{3,27},{4,100},{5,101},{6,30},{7,31},{8,104},... | collective-permute-start | bytes 1597448 | tf_op jit(solution)/shard_map/ppermute | solution.py:51
  14.6 6.8 %collective-permute-done.1.refs_0_ = bf16[32,8320]{1,0:T(8,128)(2,1)S(1)} collective-permute-done((bf16[32,8320]{1,0:T(8,128)(2,1)S(1)}, bf16[32,8320]{1,0:T(8,128)(2,1)S(1)}, u32[]{:S(2)}, u32[]{:S(2)}) %collective-permute-start.1) | collective-permute-done | bytes 532512 | tf_op jit(solution)/shard_map/ppermute | solution.py:51
  21.4 3.7 %collective-permute-done.2.refs_1_ = bf16[32,8320]{1,0:T(8,128)(2,1)S(1)} collective-permute-done((bf16[32,8320]{1,0:T(8,128)(2,1)S(1)}, bf16[32,8320]{1,0:T(8,128)(2,1)S(1)}, u32[]{:S(2)}, u32[]{:S(2)}) %collective-permute-start.2) | collective-permute-done | bytes 532512 | tf_op jit(solution)/shard_map/ppermute | solution.py:51
  25.2 4.1 %collective-permute-start.7 = (bf16[96,8320]{1,0:T(8,128)(2,1)S(1)}, bf16[96,8320]{1,0:T(8,128)(2,1)S(1)}, u32[]{:S(2)}, u32[]{:S(2)}) collective-permute-start(bf16[96,8320]{1,0:T(8,128)(2,1)S(1)} %joined.3.refs_0_), channel_id=1, source_target_pairs={{0,24},{1,25},{2,98},{3,99},{4,28},{5,29},{6,102},{7,103},{8,0},{9... | collective-permute-start | bytes 4792328 | tf_op jit(solution)/shard_map/ppermute | solution.py:51
  29.3 16.5 %collective-permute-done.3.refs_1_ = bf16[32,8320]{1,0:T(8,128)(2,1)S(1)} collective-permute-done((bf16[32,8320]{1,0:T(8,128)(2,1)S(1)}, bf16[32,8320]{1,0:T(8,128)(2,1)S(1)}, u32[]{:S(2)}, u32[]{:S(2)}) %collective-permute-start.3) | collective-permute-done | bytes 532512 | tf_op jit(solution)/shard_map/ppermute | solution.py:51
  45.8 3.2 %collective-permute-start.8 = (bf16[32,8320]{1,0:T(8,128)(2,1)S(1)}, bf16[32,8320]{1,0:T(8,128)(2,1)S(1)}, u32[]{:S(2)}, u32[]{:S(2)}) collective-permute-start(bf16[32,8320]{1,0:T(8,128)(2,1)S(1)} %collective-permute-done.3.refs_1_), channel_id=1, source_target_pairs={{0,24},{1,25},{2,98},{3,99},{4,28},{5,29},{6,102},{7,103},{8,0},{9... | collective-permute-start | bytes 1597448 | tf_op jit(solution)/shard_map/ppermute | solution.py:51
  49.0 2.6 %collective-permute-done.7.refs_0_.v_ref = bf16[96,8320]{1,0:T(8,128)(2,1)S(1)} collective-permute-done((bf16[96,8320]{1,0:T(8,128)(2,1)S(1)}, bf16[96,8320]{1,0:T(8,128)(2,1)S(1)}, u32[]{:S(2)}, u32[]{:S(2)}) %collective-permute-start.7) | collective-permute-done | bytes 1597472 | tf_op jit(solution)/shard_map/ppermute | solution.py:51
  51.7 1.2 collective-permute-start.16
  52.9 1.3 collective-permute-done.14.v_ref.refs_0_
  54.3 1.3 collective-permute-start.12
  55.6 1.8 %collective-permute-done.8.refs_1_.v_ref = bf16[32,8320]{1,0:T(8,128)(2,1)S(1)} collective-permute-done((bf16[32,8320]{1,0:T(8,128)(2,1)S(1)}, bf16[32,8320]{1,0:T(8,128)(2,1)S(1)}, u32[]{:S(2)}, u32[]{:S(2)}) %collective-permute-start.8) | collective-permute-done | bytes 532512 | tf_op jit(solution)/shard_map/ppermute | solution.py:51
  57.4 1.2 collective-permute-start.15
  58.6 4.0 %collective-permute-done.16.v_ref.refs_1_ = bf16[32,8320]{1,0:T(8,128)(2,1)S(1)} collective-permute-done((bf16[32,8320]{1,0:T(8,128)(2,1)S(1)}, bf16[32,8320]{1,0:T(8,128)(2,1)S(1)}, u32[]{:S(2)}, u32[]{:S(2)}) %collective-permute-start.16) | collective-permute-done | bytes 532512 | tf_op jit(solution)/shard_map/ppermute | solution.py:51
  62.6 2.0 %collective-permute-start.13 = (bf16[16,8320]{1,0:T(8,128)(2,1)S(1)}, bf16[16,8320]{1,0:T(8,128)(2,1)S(1)}, u32[]{:S(2)}, u32[]{:S(2)}) collective-permute-start(bf16[16,8320]{1,0:T(8,128)(2,1)S(1)} %taken.5), channel_id=1, source_target_pairs={{0,24},{1,25},{2,98},{3,99},{4,28},{5,29},{6,102},{7,103},{8,0},{9... | collective-permute-start | bytes 798728 | tf_op jit(solution)/shard_map/ppermute | solution.py:51
  64.6 4.7 %collective-permute-done.13.refs_1_ = bf16[16,8320]{1,0:T(8,128)(2,1)S(1)} collective-permute-done((bf16[16,8320]{1,0:T(8,128)(2,1)S(1)}, bf16[16,8320]{1,0:T(8,128)(2,1)S(1)}, u32[]{:S(2)}, u32[]{:S(2)}) %collective-permute-start.13) | collective-permute-done | bytes 266272 | tf_op jit(solution)/shard_map/ppermute | solution.py:51
  70.0 7.0 %collective-permute-done.17.refs_3_ = bf16[16,8320]{1,0:T(8,128)(2,1)S(1)} collective-permute-done((bf16[16,8320]{1,0:T(8,128)(2,1)S(1)}, bf16[16,8320]{1,0:T(8,128)(2,1)S(1)}, u32[]{:S(2)}, u32[]{:S(2)}) %collective-permute-start.17) | collective-permute-done | bytes 266272 | tf_op jit(solution)/shard_map/ppermute | solution.py:51
  78.0 6.3 %experts.4 = (bf16[128,4224]{1,0:T(8,128)(2,1)S(1)}, bf16[128,4224]{1,0:T(8,128)(2,1)S(1)}, bf16[1024,4096]{1,0:T(8,128)(2,1)S(1)}, bf16[1024,4096]{1,0:T(8,128)(2,1)S(1)}, bf16[1344,1024]{1,0:T(8,128)(2,1)S(1)}) custom-call(s32[1]{0:T(128)} %bitcast.3.ep_ref, bf16[96,8320]{1,0:T(8,128)(2,1)S(1)} %joined.3.refs_0_, ...), custom_call_target="tpu_custom_call" | custom-call | flops 4697620480 | bytes 17301504 | tf_op jit(solution)/shard_map/experts/pallas_call | solution.py:250
  84.9 6.3 %experts.5 = (bf16[128,4224]{1,0:T(8,128)(2,1)S(1)}, bf16[128,4224]{1,0:T(8,128)(2,1)S(1)}, bf16[1024,4096]{1,0:T(8,128)(2,1)S(1)}, bf16[1024,4096]{1,0:T(8,128)(2,1)S(1)}, bf16[1344,1024]{1,0:T(8,128)(2,1)S(1)}) custom-call(s32[1]{0:T(128)} %bitcast.3.ep_ref, ...), custom_call_target="tpu_custom_call", output_to_operand_aliasing={{2}: (8, {}), {3}: (9, {}), {4}: (10, {})} | custom-call | flops 4697620480 | bytes 17301504 | tf_op jit(solution)/shard_map/experts/pallas_call | solution.py:250
  91.7 6.3 %experts.6 = (bf16[128,4224]{1,0:T(8,128)(2,1)S(1)}, bf16[128,4224]{1,0:T(8,128)(2,1)S(1)}, bf16[1024,4096]{1,0:T(8,128)(2,1)S(1)}, bf16[1024,4096]{1,0:T(8,128)(2,1)S(1)}, bf16[1344,1024]{1,0:T(8,128)(2,1)S(1)}) custom-call(s32[1]{0:T(128)} %bitcast.3.ep_ref, ...), custom_call_target="tpu_custom_call", output_to_operand_aliasing={{2}: (12, {}), {3}: (13, {}), {4}: (14, {})} | custom-call | flops 4697620480 | bytes 17301504 | tf_op jit(solution)/shard_map/experts/pallas_call | solution.py:250
  98.6 6.3 %experts.7 = (bf16[128,4224]{1,0:T(8,128)(2,1)S(1)}, bf16[128,4224]{1,0:T(8,128)(2,1)S(1)}, bf16[1024,4096]{1,0:T(8,128)(2,1)S(1)}, bf16[1024,4096]{1,0:T(8,128)(2,1)S(1)}, bf16[1344,1024]{1,0:T(8,128)(2,1)S(1)}) custom-call(s32[1]{0:T(128)} %bitcast.3.ep_ref, ...), custom_call_target="tpu_custom_call", output_to_operand_aliasing={{2}: (8, {}), {3}: (9, {}), {4}: (10, {})} | custom-call | flops 4697620480 | bytes 17301504 | tf_op jit(solution)/shard_map/experts/pallas_call | solution.py:250
  105.6 3.2 %collective-permute-start.28 = (bf16[64,4224]{1,0:T(8,128)(2,1)S(1)}, bf16[64,4224]{1,0:T(8,128)(2,1)S(1)}, u32[]{:S(2)}, u32[]{:S(2)}) collective-permute-start(bf16[64,4224]{1,0:T(8,128)(2,1)S(1)} %get-tuple-element.57), channel_id=1, source_target_pairs={{0,24},{1,25},{2,98},{3,99},{4,28},{5,29},{6,102},{7,103},{8,0},{9... | collective-permute-start | bytes 1622024 | tf_op jit(solution)/shard_map/ppermute | solution.py:51
  108.8 7.3 %collective-permute-done.23.refs_2_ = bf16[64,4224]{1,0:T(8,128)(2,1)S(1)} collective-permute-done((bf16[64,4224]{1,0:T(8,128)(2,1)S(1)}, bf16[64,4224]{1,0:T(8,128)(2,1)S(1)}, u32[]{:S(2)}, u32[]{:S(2)}) %collective-permute-start.23) | collective-permute-done | bytes 540704 | tf_op jit(solution)/shard_map/ppermute | solution.py:51
  116.9 3.3 %collective-permute-start.31 = (bf16[96,4224]{1,0:T(8,128)(2,1)S(1)}, bf16[96,4224]{1,0:T(8,128)(2,1)S(1)}, u32[]{:S(2)}, u32[]{:S(2)}) collective-permute-start(bf16[96,4224]{1,0:T(8,128)(2,1)S(1)} %get-tuple-element.60), channel_id=1, source_target_pairs={{0,24},{1,25},{2,98},{3,99},{4,28},{5,29},{6,102},{7,103},{8,0},{9... | collective-permute-start | bytes 2433032 | tf_op jit(solution)/shard_map/ppermute | solution.py:51
  120.8 5.4 %weights.3 = bf16[448,4096]{1,0:T(8,128)(2,1)} custom-call(bf16[1024,4096]{1,0:T(8,128)(2,1)S(1)} %get-tuple-element.68.side_ref, bf16[1344,1024]{1,0:T(8,128)(2,1)S(1)} %get-tuple-element.69.coef_ref), custom_call_target="tpu_custom_call" | custom-call | flops 3758096384 | bytes 12058624 | tf_op jit(solution)/shard_map/weights/pallas_call | solution.py:278
  126.2 3.2 %collective-permute-start.29 = (bf16[32,4224]{1,0:T(8,128)(2,1)S(1)}, bf16[32,4224]{1,0:T(8,128)(2,1)S(1)}, u32[]{:S(2)}, u32[]{:S(2)}) collective-permute-start(bf16[32,4224]{1,0:T(8,128)(2,1)S(1)} %get-tuple-element.58), channel_id=1, source_target_pairs={{0,24},{1,25},{2,98},{3,99},{4,28},{5,29},{6,102},{7,103},{8,0},{9... | collective-permute-start | bytes 811016 | tf_op jit(solution)/shard_map/ppermute | solution.py:51
  131.0 2.8 %collective-permute-start.33 = (bf16[32,4224]{1,0:T(8,128)(2,1)S(1)}, bf16[32,4224]{1,0:T(8,128)(2,1)S(1)}, u32[]{:S(2)}, u32[]{:S(2)}) collective-permute-start(bf16[32,4224]{1,0:T(8,128)(2,1)S(1)} %get-tuple-element.62), channel_id=1, source_target_pairs={{0,96},{1,97},{2,26},{3,27},{4,100},{5,101},{6,30},{7,31},{8,104},... | collective-permute-start | bytes 811016 | tf_op jit(solution)/shard_map/ppermute | solution.py:51
  134.5 5.4 %weights.4 = bf16[448,4096]{1,0:T(8,128)(2,1)} custom-call(bf16[1024,4096]{1,0:T(8,128)(2,1)S(1)} %get-tuple-element.68.side_ref, bf16[1344,1024]{1,0:T(8,128)(2,1)S(1)} %get-tuple-element.69.coef_ref), custom_call_target="tpu_custom_call" | custom-call | flops 3758096384 | bytes 12058624 | tf_op jit(solution)/shard_map/weights/pallas_call | solution.py:278
  142.1 1.7 %collective-permute-start.35 = (bf16[16,4224]{1,0:T(8,128)(2,1)S(1)}, bf16[16,4224]{1,0:T(8,128)(2,1)S(1)}, u32[]{:S(2)}, u32[]{:S(2)}) collective-permute-start(bf16[16,4224]{1,0:T(8,128)(2,1)S(1)} %get-tuple-element.65), channel_id=1, source_target_pairs={{0,4},{1,5},{2,6},{3,7},{4,0},{5,1},{6,2},{7,3},{8,12},{9,13},{10,... | collective-permute-start | bytes 405512 | tf_op jit(solution)/shard_map/ppermute | solution.py:51
  143.7 2.2 %collective-permute-start.37 = (bf16[16,4224]{1,0:T(8,128)(2,1)S(1)}, bf16[16,4224]{1,0:T(8,128)(2,1)S(1)}, u32[]{:S(2)}, u32[]{:S(2)}) collective-permute-start(bf16[16,4224]{1,0:T(8,128)(2,1)S(1)} %get-tuple-element.65), channel_id=1, source_target_pairs={{0,5},{1,4},{2,7},{3,6},{4,1},{5,0},{6,3},{7,2},{8,13},{9,12},{10,... | collective-permute-start | bytes 405512 | tf_op jit(solution)/shard_map/ppermute | solution.py:51
  146.6 5.4 %weights.5 = bf16[448,4096]{1,0:T(8,128)(2,1)} custom-call(bf16[1024,4096]{1,0:T(8,128)(2,1)S(1)} %get-tuple-element.70.side_ref, bf16[1344,1024]{1,0:T(8,128)(2,1)S(1)} %get-tuple-element.69.coef_ref), custom_call_target="tpu_custom_call" | custom-call | flops 3758096384 | bytes 12058624 | tf_op jit(solution)/shard_map/weights/pallas_call | solution.py:278
  (80 shorter events, 15.1 us)
Async XLA Ops:
  3.4 8.2 %collective-permute-start = (bf16[16,8320]{1,0:T(8,128)(2,1)S(1)}, bf16[16,8320]{1,0:T(8,128)(2,1)S(1)}, u32[]{:S(2)}, u32[]{:S(2)}) collective-permute-start(bf16[16,8320]{1,0:T(8,128)(2,1)S(1)} %packed.1.refs_0_), channel_id=1, source_target_pairs={{0,4},{1,5},{2,6},{3,7},{4,0},{5,1},{6,2},{7,3},{8,12},{9,13},{10,... | collective-permute-start | bytes 798728 | tf_op jit(solution)/shard_map/ppermute | solution.py:51
  11.6 9.8 %collective-permute-start.1 = (bf16[32,8320]{1,0:T(8,128)(2,1)S(1)}, bf16[32,8320]{1,0:T(8,128)(2,1)S(1)}, u32[]{:S(2)}, u32[]{:S(2)}) collective-permute-start(bf16[32,8320]{1,0:T(8,128)(2,1)S(1)} %joined.2.refs_2_), channel_id=1, source_target_pairs={{0,96},{1,97},{2,26},{3,27},{4,100},{5,101},{6,30},{7,31},{8,104},... | collective-permute-start | bytes 1597448 | tf_op jit(solution)/shard_map/ppermute | solution.py:51
  14.6 10.5 %collective-permute-start.2 = (bf16[32,8320]{1,0:T(8,128)(2,1)S(1)}, bf16[32,8320]{1,0:T(8,128)(2,1)S(1)}, u32[]{:S(2)}, u32[]{:S(2)}) collective-permute-start(bf16[32,8320]{1,0:T(8,128)(2,1)S(1)} %joined.2.refs_2_), channel_id=1, source_target_pairs={{0,32},{1,33},{2,10},{3,11},{4,36},{5,37},{6,14},{7,15},{8,40},{9,... | collective-permute-start | bytes 1597448 | tf_op jit(solution)/shard_map/ppermute | solution.py:51
  25.2 26.5 %collective-permute-start.7 = (bf16[96,8320]{1,0:T(8,128)(2,1)S(1)}, bf16[96,8320]{1,0:T(8,128)(2,1)S(1)}, u32[]{:S(2)}, u32[]{:S(2)}) collective-permute-start(bf16[96,8320]{1,0:T(8,128)(2,1)S(1)} %joined.3.refs_0_), channel_id=1, source_target_pairs={{0,24},{1,25},{2,98},{3,99},{4,28},{5,29},{6,102},{7,103},{8,0},{9... | collective-permute-start | bytes 4792328 | tf_op jit(solution)/shard_map/ppermute | solution.py:51
  29.3 24.9 %collective-permute-start.14 = (bf16[96,8320]{1,0:T(8,128)(2,1)S(1)}, bf16[96,8320]{1,0:T(8,128)(2,1)S(1)}, u32[]{:S(2)}, u32[]{:S(2)}) collective-permute-start(bf16[96,8320]{1,0:T(8,128)(2,1)S(1)} %joined.3.refs_0_), channel_id=1, source_target_pairs={{0,8},{1,9},{2,34},{3,35},{4,12},{5,13},{6,38},{7,39},{8,16},{9,17... | collective-permute-start | bytes 4792328 | tf_op jit(solution)/shard_map/ppermute | solution.py:51
  29.3 16.5 %collective-permute-start.3 = (bf16[32,8320]{1,0:T(8,128)(2,1)S(1)}, bf16[32,8320]{1,0:T(8,128)(2,1)S(1)}, u32[]{:S(2)}, u32[]{:S(2)}) collective-permute-start(bf16[32,8320]{1,0:T(8,128)(2,1)S(1)} %joined.2.refs_2_), channel_id=1, source_target_pairs={{0,64},{1,65},{2,18},{3,19},{4,68},{5,69},{6,22},{7,23},{8,72},{9,... | collective-permute-start | bytes 1597448 | tf_op jit(solution)/shard_map/ppermute | solution.py:51
  29.3 47.7 %collective-permute-start.4 = (bf16[96,8320]{1,0:T(8,128)(2,1)S(1)}, bf16[96,8320]{1,0:T(8,128)(2,1)S(1)}, u32[]{:S(2)}, u32[]{:S(2)}) collective-permute-start(bf16[96,8320]{1,0:T(8,128)(2,1)S(1)} %joined.3.refs_0_), channel_id=1, source_target_pairs={{0,2},{1,3},{2,0},{3,1},{4,6},{5,7},{6,4},{7,5},{8,10},{9,11},{10,... | collective-permute-start | bytes 4792328 | tf_op jit(solution)/shard_map/ppermute | solution.py:51
  45.8 8.5 %collective-permute-start.5 = (bf16[32,8320]{1,0:T(8,128)(2,1)S(1)}, bf16[32,8320]{1,0:T(8,128)(2,1)S(1)}, u32[]{:S(2)}, u32[]{:S(2)}) collective-permute-start(bf16[32,8320]{1,0:T(8,128)(2,1)S(1)} %collective-permute-done.3.refs_1_), channel_id=1, source_target_pairs={{0,2},{1,3},{2,0},{3,1},{4,6},{5,7},{6,4},{7,5},{8,10},{9,11},{10,... | collective-permute-start | bytes 1597448 | tf_op jit(solution)/shard_map/ppermute | solution.py:51
  45.8 11.6 %collective-permute-start.8 = (bf16[32,8320]{1,0:T(8,128)(2,1)S(1)}, bf16[32,8320]{1,0:T(8,128)(2,1)S(1)}, u32[]{:S(2)}, u32[]{:S(2)}) collective-permute-start(bf16[32,8320]{1,0:T(8,128)(2,1)S(1)} %collective-permute-done.3.refs_1_), channel_id=1, source_target_pairs={{0,24},{1,25},{2,98},{3,99},{4,28},{5,29},{6,102},{7,103},{8,0},{9... | collective-permute-start | bytes 1597448 | tf_op jit(solution)/shard_map/ppermute | solution.py:51
  51.7 10.9 %collective-permute-start.16 = (bf16[32,8320]{1,0:T(8,128)(2,1)S(1)}, bf16[32,8320]{1,0:T(8,128)(2,1)S(1)}, u32[]{:S(2)}, u32[]{:S(2)}) collective-permute-start(bf16[32,8320]{1,0:T(8,128)(2,1)S(1)} %collective-permute-done.3.refs_1_), channel_id=1, source_target_pairs={{0,8},{1,9},{2,34},{3,35},{4,12},{5,13},{6,38},{7,39},{8,16},{9,17... | collective-permute-start | bytes 1597448 | tf_op jit(solution)/shard_map/ppermute | solution.py:51
  54.2 30.4 %collective-permute-start.9 = (bf16[96,8320]{1,0:T(8,128)(2,1)S(1)}, bf16[96,8320]{1,0:T(8,128)(2,1)S(1)}, u32[]{:S(2)}, u32[]{:S(2)}) collective-permute-start(bf16[96,8320]{1,0:T(8,128)(2,1)S(1)} %collective-permute-done.7.refs_0_.v_ref), channel_id=1, source_target_pairs={{0,2},{1,3},{2,0},{3,1},{4,6},{5,7},{6,4},{7,5},{8,10},{9,11},{10,... | collective-permute-start | bytes 4792328 | tf_op jit(solution)/shard_map/ppermute | solution.py:51
  54.3 23.2 %collective-permute-start.12 = (bf16[48,8320]{1,0:T(8,128)(2,1)S(1)}, bf16[48,8320]{1,0:T(8,128)(2,1)S(1)}, u32[]{:S(2)}, u32[]{:S(2)}) collective-permute-start(bf16[48,8320]{1,0:T(8,128)(2,1)S(1)} %taken.4), channel_id=1, source_target_pairs={{0,24},{1,25},{2,98},{3,99},{4,28},{5,29},{6,102},{7,103},{8,0},{9... | collective-permute-start | bytes 2396168 | tf_op jit(solution)/shard_map/ppermute | solution.py:51
  57.4 20.2 %collective-permute-start.15 = (bf16[48,8320]{1,0:T(8,128)(2,1)S(1)}, bf16[48,8320]{1,0:T(8,128)(2,1)S(1)}, u32[]{:S(2)}, u32[]{:S(2)}) collective-permute-start(bf16[48,8320]{1,0:T(8,128)(2,1)S(1)} %taken.6), channel_id=1, source_target_pairs={{0,8},{1,9},{2,34},{3,35},{4,12},{5,13},{6,38},{7,39},{8,16},{9,17... | collective-permute-start | bytes 2396168 | tf_op jit(solution)/shard_map/ppermute | solution.py:51
  69.3 7.6 %collective-permute-start.17 = (bf16[16,8320]{1,0:T(8,128)(2,1)S(1)}, bf16[16,8320]{1,0:T(8,128)(2,1)S(1)}, u32[]{:S(2)}, u32[]{:S(2)}) collective-permute-start(bf16[16,8320]{1,0:T(8,128)(2,1)S(1)} %taken.7), channel_id=1, source_target_pairs={{0,8},{1,9},{2,34},{3,35},{4,12},{5,13},{6,38},{7,39},{8,16},{9,17... | collective-permute-start | bytes 798728 | tf_op jit(solution)/shard_map/ppermute | solution.py:51
  77.0 21.6 %collective-permute-start.25 = (bf16[96,8320]{1,0:T(8,128)(2,1)S(1)}, bf16[96,8320]{1,0:T(8,128)(2,1)S(1)}, u32[]{:S(2)}, u32[]{:S(2)}) collective-permute-start(bf16[96,8320]{1,0:T(8,128)(2,1)S(1)} %collective-permute-done.14.v_ref.refs_0_), channel_id=1, source_target_pairs={{0,2},{1,3},{2,0},{3,1},{4,6},{5,7},{6,4},{7,5},{8,10},{9,11},{10,... | collective-permute-start | bytes 4792328 | tf_op jit(solution)/shard_map/ppermute | solution.py:51
  77.0 7.4 %collective-permute-start.10 = (bf16[32,8320]{1,0:T(8,128)(2,1)S(1)}, bf16[32,8320]{1,0:T(8,128)(2,1)S(1)}, u32[]{:S(2)}, u32[]{:S(2)}) collective-permute-start(bf16[32,8320]{1,0:T(8,128)(2,1)S(1)} %collective-permute-done.8.refs_1_.v_ref), channel_id=1, source_target_pairs={{0,2},{1,3},{2,0},{3,1},{4,6},{5,7},{6,4},{7,5},{8,10},{9,11},{10,... | collective-permute-start | bytes 1597448 | tf_op jit(solution)/shard_map/ppermute | solution.py:51
  77.5 14.2 %collective-permute-start.18 = (bf16[48,8320]{1,0:T(8,128)(2,1)S(1)}, bf16[48,8320]{1,0:T(8,128)(2,1)S(1)}, u32[]{:S(2)}, u32[]{:S(2)}) collective-permute-start(bf16[48,8320]{1,0:T(8,128)(2,1)S(1)} %collective-permute-done.12.refs_0_), channel_id=1, source_target_pairs={{0,2},{1,3},{2,0},{3,1},{4,6},{5,7},{6,4},{7,5},{8,10},{9,11},{10,... | collective-permute-start | bytes 2396168 | tf_op jit(solution)/shard_map/ppermute | solution.py:51
  77.6 14.1 %collective-permute-start.20 = (bf16[48,8320]{1,0:T(8,128)(2,1)S(1)}, bf16[48,8320]{1,0:T(8,128)(2,1)S(1)}, u32[]{:S(2)}, u32[]{:S(2)}) collective-permute-start(bf16[48,8320]{1,0:T(8,128)(2,1)S(1)} %collective-permute-done.15.refs_2_), channel_id=1, source_target_pairs={{0,2},{1,3},{2,0},{3,1},{4,6},{5,7},{6,4},{7,5},{8,10},{9,11},{10,... | collective-permute-start | bytes 2396168 | tf_op jit(solution)/shard_map/ppermute | solution.py:51
  98.3 10.5 %collective-permute-start.11 = (bf16[128,4224]{1,0:T(8,128)(2,1)S(1)}, bf16[128,4224]{1,0:T(8,128)(2,1)S(1)}, u32[]{:S(2)}, u32[]{:S(2)}) collective-permute-start(bf16[128,4224]{1,0:T(8,128)(2,1)S(1)} %get-tuple-element.44), channel_id=1, source_target_pairs={{0,2},{1,3},{2,0},{3,1},{4,6},{5,7},{6,4},{7,5},{8,10},{9,11},{10,... | collective-permute-start | bytes 3244040 | tf_op jit(solution)/shard_map/ppermute | solution.py:51
  105.0 11.6 %collective-permute-start.27 = (bf16[128,4224]{1,0:T(8,128)(2,1)S(1)}, bf16[128,4224]{1,0:T(8,128)(2,1)S(1)}, u32[]{:S(2)}, u32[]{:S(2)}) collective-permute-start(bf16[128,4224]{1,0:T(8,128)(2,1)S(1)} %get-tuple-element.56), channel_id=1, source_target_pairs={{0,2},{1,3},{2,0},{3,1},{4,6},{5,7},{6,4},{7,5},{8,10},{9,11},{10,... | collective-permute-start | bytes 3244040 | tf_op jit(solution)/shard_map/ppermute | solution.py:51
  105.5 10.6 %collective-permute-start.23 = (bf16[64,4224]{1,0:T(8,128)(2,1)S(1)}, bf16[64,4224]{1,0:T(8,128)(2,1)S(1)}, u32[]{:S(2)}, u32[]{:S(2)}) collective-permute-start(bf16[64,4224]{1,0:T(8,128)(2,1)S(1)} %get-tuple-element.50), channel_id=1, source_target_pairs={{0,8},{1,9},{2,34},{3,35},{4,12},{5,13},{6,38},{7,39},{8,16},{9,17... | collective-permute-start | bytes 1622024 | tf_op jit(solution)/shard_map/ppermute | solution.py:51
  105.6 11.0 %collective-permute-start.28 = (bf16[64,4224]{1,0:T(8,128)(2,1)S(1)}, bf16[64,4224]{1,0:T(8,128)(2,1)S(1)}, u32[]{:S(2)}, u32[]{:S(2)}) collective-permute-start(bf16[64,4224]{1,0:T(8,128)(2,1)S(1)} %get-tuple-element.57), channel_id=1, source_target_pairs={{0,24},{1,25},{2,98},{3,99},{4,28},{5,29},{6,102},{7,103},{8,0},{9... | collective-permute-start | bytes 1622024 | tf_op jit(solution)/shard_map/ppermute | solution.py:51
  108.8 20.6 %collective-permute-start.6 = (bf16[128,4224]{1,0:T(8,128)(2,1)S(1)}, bf16[128,4224]{1,0:T(8,128)(2,1)S(1)}, u32[]{:S(2)}, u32[]{:S(2)}) collective-permute-start(bf16[128,4224]{1,0:T(8,128)(2,1)S(1)} %get-tuple-element.39), channel_id=1, source_target_pairs={{0,2},{1,3},{2,0},{3,1},{4,6},{5,7},{6,4},{7,5},{8,10},{9,11},{10,... | collective-permute-start | bytes 3244040 | tf_op jit(solution)/shard_map/ppermute | solution.py:51
  116.5 13.5 %collective-permute-start.30 = (bf16[96,4224]{1,0:T(8,128)(2,1)S(1)}, bf16[96,4224]{1,0:T(8,128)(2,1)S(1)}, u32[]{:S(2)}, u32[]{:S(2)}) collective-permute-start(bf16[96,4224]{1,0:T(8,128)(2,1)S(1)} %get-tuple-element.59), channel_id=1, source_target_pairs={{0,8},{1,9},{2,34},{3,35},{4,12},{5,13},{6,38},{7,39},{8,16},{9,17... | collective-permute-start | bytes 2433032 | tf_op jit(solution)/shard_map/ppermute | solution.py:51
  116.9 13.1 %collective-permute-start.31 = (bf16[96,4224]{1,0:T(8,128)(2,1)S(1)}, bf16[96,4224]{1,0:T(8,128)(2,1)S(1)}, u32[]{:S(2)}, u32[]{:S(2)}) collective-permute-start(bf16[96,4224]{1,0:T(8,128)(2,1)S(1)} %get-tuple-element.60), channel_id=1, source_target_pairs={{0,24},{1,25},{2,98},{3,99},{4,28},{5,29},{6,102},{7,103},{8,0},{9... | collective-permute-start | bytes 2433032 | tf_op jit(solution)/shard_map/ppermute | solution.py:51
  126.2 13.7 %collective-permute-start.24 = (bf16[32,4224]{1,0:T(8,128)(2,1)S(1)}, bf16[32,4224]{1,0:T(8,128)(2,1)S(1)}, u32[]{:S(2)}, u32[]{:S(2)}) collective-permute-start(bf16[32,4224]{1,0:T(8,128)(2,1)S(1)} %get-tuple-element.51), channel_id=1, source_target_pairs={{0,8},{1,9},{2,34},{3,35},{4,12},{5,13},{6,38},{7,39},{8,16},{9,17... | collective-permute-start | bytes 811016 | tf_op jit(solution)/shard_map/ppermute | solution.py:51
  126.2 13.7 %collective-permute-start.29 = (bf16[32,4224]{1,0:T(8,128)(2,1)S(1)}, bf16[32,4224]{1,0:T(8,128)(2,1)S(1)}, u32[]{:S(2)}, u32[]{:S(2)}) collective-permute-start(bf16[32,4224]{1,0:T(8,128)(2,1)S(1)} %get-tuple-element.58), channel_id=1, source_target_pairs={{0,24},{1,25},{2,98},{3,99},{4,28},{5,29},{6,102},{7,103},{8,0},{9... | collective-permute-start | bytes 811016 | tf_op jit(solution)/shard_map/ppermute | solution.py:51
  130.4 9.5 %collective-permute-start.32 = (bf16[32,4224]{1,0:T(8,128)(2,1)S(1)}, bf16[32,4224]{1,0:T(8,128)(2,1)S(1)}, u32[]{:S(2)}, u32[]{:S(2)}) collective-permute-start(bf16[32,4224]{1,0:T(8,128)(2,1)S(1)} %get-tuple-element.61), channel_id=1, source_target_pairs={{0,32},{1,33},{2,10},{3,11},{4,36},{5,37},{6,14},{7,15},{8,40},{9,... | collective-permute-start | bytes 811016 | tf_op jit(solution)/shard_map/ppermute | solution.py:51
  131.0 9.7 %collective-permute-start.33 = (bf16[32,4224]{1,0:T(8,128)(2,1)S(1)}, bf16[32,4224]{1,0:T(8,128)(2,1)S(1)}, u32[]{:S(2)}, u32[]{:S(2)}) collective-permute-start(bf16[32,4224]{1,0:T(8,128)(2,1)S(1)} %get-tuple-element.62), channel_id=1, source_target_pairs={{0,96},{1,97},{2,26},{3,27},{4,100},{5,101},{6,30},{7,31},{8,104},... | collective-permute-start | bytes 811016 | tf_op jit(solution)/shard_map/ppermute | solution.py:51
  133.7 8.1 %collective-permute-start.34 = (bf16[32,4224]{1,0:T(8,128)(2,1)S(1)}, bf16[32,4224]{1,0:T(8,128)(2,1)S(1)}, u32[]{:S(2)}, u32[]{:S(2)}) collective-permute-start(bf16[32,4224]{1,0:T(8,128)(2,1)S(1)} %get-tuple-element.63), channel_id=1, source_target_pairs={{0,64},{1,65},{2,18},{3,19},{4,68},{5,69},{6,22},{7,23},{8,72},{9,... | collective-permute-start | bytes 811016 | tf_op jit(solution)/shard_map/ppermute | solution.py:51
  142.1 10.0 %collective-permute-start.35 = (bf16[16,4224]{1,0:T(8,128)(2,1)S(1)}, bf16[16,4224]{1,0:T(8,128)(2,1)S(1)}, u32[]{:S(2)}, u32[]{:S(2)}) collective-permute-start(bf16[16,4224]{1,0:T(8,128)(2,1)S(1)} %get-tuple-element.65), channel_id=1, source_target_pairs={{0,4},{1,5},{2,6},{3,7},{4,0},{5,1},{6,2},{7,3},{8,12},{9,13},{10,... | collective-permute-start | bytes 405512 | tf_op jit(solution)/shard_map/ppermute | solution.py:51
  143.7 8.7 %collective-permute-start.37 = (bf16[16,4224]{1,0:T(8,128)(2,1)S(1)}, bf16[16,4224]{1,0:T(8,128)(2,1)S(1)}, u32[]{:S(2)}, u32[]{:S(2)}) collective-permute-start(bf16[16,4224]{1,0:T(8,128)(2,1)S(1)} %get-tuple-element.65), channel_id=1, source_target_pairs={{0,5},{1,4},{2,7},{3,6},{4,1},{5,0},{6,3},{7,2},{8,13},{9,12},{10,... | collective-permute-start | bytes 405512 | tf_op jit(solution)/shard_map/ppermute | solution.py:51
  (12 other events, 230.9 us)

commit v4 on v3

--- a/solution.py
+++ b/solution.py
@@ -158,23 +158,26 @@
     )(*arrays)
 
 
-def last_kernel(own, same, other, other_pair, grad_ref, slot_ref):
+def last_kernel(own, same, other, other_pair, ids_ref, grad_ref, gate_ref):
     total = (own[...].astype(F32) + same[...].astype(F32)) + (
         other[...].astype(F32) + other_pair[...].astype(F32)
     )
     grad_ref[...] = total[:, :D].astype(BF16)
-    slot_ref[...] = total[:, D:]
+    slot = total[:, D:].T
+    gate_ref[...] = sum(
+        jnp.where(ids_ref[...] == e, slot[e : e + 1, :], 0.0) for e in range(EXPERTS)
+    )
 
 
 def last(*arrays):
-    rows = arrays[0].shape[0]
+    rows, ids = arrays[0].shape[0], arrays[-1]
     return pl.pallas_call(
         last_kernel,
         out_shape=(
             jax.ShapeDtypeStruct((rows, D), BF16),
-            jax.ShapeDtypeStruct((rows, EXTRA), F32),
-        ),
-        in_specs=[VM] * 4,
+            jax.ShapeDtypeStruct(ids.shape, F32),
+        ),
+        in_specs=[VM] * 5,
         out_specs=(VM, VM),
         compiler_params=pltpu.CompilerParams(vmem_limit_bytes=4 * 1024 * 1024),
         name="last",
@@ -366,9 +369,8 @@
     )
     same = sent(pair, OTHER_Y)
     other, other_pair = sent(own, OTHER_EP), sent(pair, OTHER_BOTH)
-    input_grad, slot = last(own, same, other, other_pair)
-    picked = expert_ids[:, :, None] == lax.broadcasted_iota(jnp.int32, (1, 1, EXPERTS), 2)
-    gate_grad = jnp.sum(jnp.where(picked, slot[:, None, :EXPERTS], 0.0), axis=2)
+    input_grad, gate_grad = last(own, same, other, other_pair, expert_ids.T)
+    gate_grad = gate_grad.T
 
     grads = []
     for which, side in enumerate((x_all, x_all, y_all)):

time: 154 us -> 153 us (level)
  transfers between devices with their start and end apart: 38 -> 38, of which waited for: 15 -> 15; matrix products, arithmetic and copies ran while one was open for 0% -> 0% of each run, Pallas kernels for 28% -> 29%
where the time goes in v4:
time: 153 us
  waiting for transfers between devices  65 us (42%)
  Pallas kernels  45 us (29%)
  starting transfers between devices  39.7 us (26%)
  local copies, waits for them, and re-layouts  1.83 us (1%)
    ppermute x38, waiting for transfers between devices, sent(): return lax.ppermute(value, AXES, to)  65 us
    ppermute x38, starting transfers between devices, sent(): return lax.ppermute(value, AXES, to)  39.7 us
    pallas_call x4, Pallas kernels, expert_group(): pl.pallas_call(functools.partial(expert_kernel, len(chunks), len(held), a...  25.3 us
    pallas_call x3, Pallas kernels, weight_grad(): pl.pallas_call(functools.partial(weight_kernel, which), grid=(D // TILE,)...  16.3 us
  transfers between devices with their start and end apart: 38, of which 15 were waited for; matrix products, arithmetic and copies ran while one was open for 0% of the time, Pallas kernels for 29%

profile of v4, /device:TPU:0, one launch (start us, length us, event | category | flops | bytes accessed | tf_op | source)
XLA Modules:
  0.0 153.2 jit_solution(2137252087534903046)
XLA Ops:
  3.4 1.8 %collective-permute-start = (bf16[16,8320]{1,0:T(8,128)(2,1)S(1)}, bf16[16,8320]{1,0:T(8,128)(2,1)S(1)}, u32[]{:S(2)}, u32[]{:S(2)}) collective-permute-start(bf16[16,8320]{1,0:T(8,128)(2,1)S(1)} %packed.1.refs_0_), channel_id=1, source_target_pairs={{0,4},{1,5},{2,6},{3,7},{4,0},{5,1},{6,2},{7,3},{8,12},{9,13},{10,... | collective-permute-start | bytes 798728 | tf_op jit(solution)/shard_map/ppermute | solution.py:51
  5.2 6.4 %collective-permute-done.refs_1_ = bf16[16,8320]{1,0:T(8,128)(2,1)S(1)} collective-permute-done((bf16[16,8320]{1,0:T(8,128)(2,1)S(1)}, bf16[16,8320]{1,0:T(8,128)(2,1)S(1)}, u32[]{:S(2)}, u32[]{:S(2)}) %collective-permute-start) | collective-permute-done | bytes 266272 | tf_op jit(solution)/shard_map/ppermute | solution.py:51
  11.6 3.0 %collective-permute-start.1 = (bf16[32,8320]{1,0:T(8,128)(2,1)S(1)}, bf16[32,8320]{1,0:T(8,128)(2,1)S(1)}, u32[]{:S(2)}, u32[]{:S(2)}) collective-permute-start(bf16[32,8320]{1,0:T(8,128)(2,1)S(1)} %joined.2.refs_2_), channel_id=1, source_target_pairs={{0,96},{1,97},{2,26},{3,27},{4,100},{5,101},{6,30},{7,31},{8,104},... | collective-permute-start | bytes 1597448 | tf_op jit(solution)/shard_map/ppermute | solution.py:51
  14.6 6.8 %collective-permute-done.1.refs_0_ = bf16[32,8320]{1,0:T(8,128)(2,1)S(1)} collective-permute-done((bf16[32,8320]{1,0:T(8,128)(2,1)S(1)}, bf16[32,8320]{1,0:T(8,128)(2,1)S(1)}, u32[]{:S(2)}, u32[]{:S(2)}) %collective-permute-start.1) | collective-permute-done | bytes 532512 | tf_op jit(solution)/shard_map/ppermute | solution.py:51
  21.4 3.7 %collective-permute-done.2.refs_1_ = bf16[32,8320]{1,0:T(8,128)(2,1)S(1)} collective-permute-done((bf16[32,8320]{1,0:T(8,128)(2,1)S(1)}, bf16[32,8320]{1,0:T(8,128)(2,1)S(1)}, u32[]{:S(2)}, u32[]{:S(2)}) %collective-permute-start.2) | collective-permute-done | bytes 532512 | tf_op jit(solution)/shard_map/ppermute | solution.py:51
  25.2 4.1 %collective-permute-start.7 = (bf16[96,8320]{1,0:T(8,128)(2,1)S(1)}, bf16[96,8320]{1,0:T(8,128)(2,1)S(1)}, u32[]{:S(2)}, u32[]{:S(2)}) collective-permute-start(bf16[96,8320]{1,0:T(8,128)(2,1)S(1)} %joined.3.refs_0_), channel_id=1, source_target_pairs={{0,24},{1,25},{2,98},{3,99},{4,28},{5,29},{6,102},{7,103},{8,0},{9... | collective-permute-start | bytes 4792328 | tf_op jit(solution)/shard_map/ppermute | solution.py:51
  29.3 16.5 %collective-permute-done.3.refs_1_ = bf16[32,8320]{1,0:T(8,128)(2,1)S(1)} collective-permute-done((bf16[32,8320]{1,0:T(8,128)(2,1)S(1)}, bf16[32,8320]{1,0:T(8,128)(2,1)S(1)}, u32[]{:S(2)}, u32[]{:S(2)}) %collective-permute-start.3) | collective-permute-done | bytes 532512 | tf_op jit(solution)/shard_map/ppermute | solution.py:51
  45.8 3.2 %collective-permute-start.8 = (bf16[32,8320]{1,0:T(8,128)(2,1)S(1)}, bf16[32,8320]{1,0:T(8,128)(2,1)S(1)}, u32[]{:S(2)}, u32[]{:S(2)}) collective-permute-start(bf16[32,8320]{1,0:T(8,128)(2,1)S(1)} %collective-permute-done.3.refs_1_), channel_id=1, source_target_pairs={{0,24},{1,25},{2,98},{3,99},{4,28},{5,29},{6,102},{7,103},{8,0},{9... | collective-permute-start | bytes 1597448 | tf_op jit(solution)/shard_map/ppermute | solution.py:51
  49.0 2.6 %collective-permute-done.7.refs_0_.v_ref = bf16[96,8320]{1,0:T(8,128)(2,1)S(1)} collective-permute-done((bf16[96,8320]{1,0:T(8,128)(2,1)S(1)}, bf16[96,8320]{1,0:T(8,128)(2,1)S(1)}, u32[]{:S(2)}, u32[]{:S(2)}) %collective-permute-start.7) | collective-permute-done | bytes 1597472 | tf_op jit(solution)/shard_map/ppermute | solution.py:51
  51.7 1.2 collective-permute-start.16
  52.9 1.3 collective-permute-done.14.v_ref.refs_0_
  54.3 1.3 collective-permute-start.12
  55.6 1.8 %collective-permute-done.8.refs_1_.v_ref = bf16[32,8320]{1,0:T(8,128)(2,1)S(1)} collective-permute-done((bf16[32,8320]{1,0:T(8,128)(2,1)S(1)}, bf16[32,8320]{1,0:T(8,128)(2,1)S(1)}, u32[]{:S(2)}, u32[]{:S(2)}) %collective-permute-start.8) | collective-permute-done | bytes 532512 | tf_op jit(solution)/shard_map/ppermute | solution.py:51
  57.4 1.2 collective-permute-start.15
  58.6 4.0 %collective-permute-done.16.v_ref.refs_1_ = bf16[32,8320]{1,0:T(8,128)(2,1)S(1)} collective-permute-done((bf16[32,8320]{1,0:T(8,128)(2,1)S(1)}, bf16[32,8320]{1,0:T(8,128)(2,1)S(1)}, u32[]{:S(2)}, u32[]{:S(2)}) %collective-permute-start.16) | collective-permute-done | bytes 532512 | tf_op jit(solution)/shard_map/ppermute | solution.py:51
  62.6 2.0 %collective-permute-start.13 = (bf16[16,8320]{1,0:T(8,128)(2,1)S(1)}, bf16[16,8320]{1,0:T(8,128)(2,1)S(1)}, u32[]{:S(2)}, u32[]{:S(2)}) collective-permute-start(bf16[16,8320]{1,0:T(8,128)(2,1)S(1)} %taken.5), channel_id=1, source_target_pairs={{0,24},{1,25},{2,98},{3,99},{4,28},{5,29},{6,102},{7,103},{8,0},{9... | collective-permute-start | bytes 798728 | tf_op jit(solution)/shard_map/ppermute | solution.py:51
  64.6 4.7 %collective-permute-done.13.refs_1_ = bf16[16,8320]{1,0:T(8,128)(2,1)S(1)} collective-permute-done((bf16[16,8320]{1,0:T(8,128)(2,1)S(1)}, bf16[16,8320]{1,0:T(8,128)(2,1)S(1)}, u32[]{:S(2)}, u32[]{:S(2)}) %collective-permute-start.13) | collective-permute-done | bytes 266272 | tf_op jit(solution)/shard_map/ppermute | solution.py:51
  70.0 7.0 %collective-permute-done.17.refs_3_ = bf16[16,8320]{1,0:T(8,128)(2,1)S(1)} collective-permute-done((bf16[16,8320]{1,0:T(8,128)(2,1)S(1)}, bf16[16,8320]{1,0:T(8,128)(2,1)S(1)}, u32[]{:S(2)}, u32[]{:S(2)}) %collective-permute-start.17) | collective-permute-done | bytes 266272 | tf_op jit(solution)/shard_map/ppermute | solution.py:51
  78.0 6.3 %experts.4 = (bf16[128,4224]{1,0:T(8,128)(2,1)S(1)}, bf16[128,4224]{1,0:T(8,128)(2,1)S(1)}, bf16[1024,4096]{1,0:T(8,128)(2,1)S(1)}, bf16[1024,4096]{1,0:T(8,128)(2,1)S(1)}, bf16[1344,1024]{1,0:T(8,128)(2,1)S(1)}) custom-call(s32[1]{0:T(128)} %bitcast.3.ep_ref, bf16[96,8320]{1,0:T(8,128)(2,1)S(1)} %joined.3.refs_0_, ...), custom_call_target="tpu_custom_call" | custom-call | flops 4697620480 | bytes 17301504 | tf_op jit(solution)/shard_map/experts/pallas_call | solution.py:253
  84.9 6.3 %experts.5 = (bf16[128,4224]{1,0:T(8,128)(2,1)S(1)}, bf16[128,4224]{1,0:T(8,128)(2,1)S(1)}, bf16[1024,4096]{1,0:T(8,128)(2,1)S(1)}, bf16[1024,4096]{1,0:T(8,128)(2,1)S(1)}, bf16[1344,1024]{1,0:T(8,128)(2,1)S(1)}) custom-call(s32[1]{0:T(128)} %bitcast.3.ep_ref, ...), custom_call_target="tpu_custom_call", output_to_operand_aliasing={{2}: (8, {}), {3}: (9, {}), {4}: (10, {})} | custom-call | flops 4697620480 | bytes 17301504 | tf_op jit(solution)/shard_map/experts/pallas_call | solution.py:253
  91.7 6.3 %experts.6 = (bf16[128,4224]{1,0:T(8,128)(2,1)S(1)}, bf16[128,4224]{1,0:T(8,128)(2,1)S(1)}, bf16[1024,4096]{1,0:T(8,128)(2,1)S(1)}, bf16[1024,4096]{1,0:T(8,128)(2,1)S(1)}, bf16[1344,1024]{1,0:T(8,128)(2,1)S(1)}) custom-call(s32[1]{0:T(128)} %bitcast.3.ep_ref, ...), custom_call_target="tpu_custom_call", output_to_operand_aliasing={{2}: (12, {}), {3}: (13, {}), {4}: (14, {})} | custom-call | flops 4697620480 | bytes 17301504 | tf_op jit(solution)/shard_map/experts/pallas_call | solution.py:253
  98.6 6.3 %experts.7 = (bf16[128,4224]{1,0:T(8,128)(2,1)S(1)}, bf16[128,4224]{1,0:T(8,128)(2,1)S(1)}, bf16[1024,4096]{1,0:T(8,128)(2,1)S(1)}, bf16[1024,4096]{1,0:T(8,128)(2,1)S(1)}, bf16[1344,1024]{1,0:T(8,128)(2,1)S(1)}) custom-call(s32[1]{0:T(128)} %bitcast.3.ep_ref, ...), custom_call_target="tpu_custom_call", output_to_operand_aliasing={{2}: (8, {}), {3}: (9, {}), {4}: (10, {})} | custom-call | flops 4697620480 | bytes 17301504 | tf_op jit(solution)/shard_map/experts/pallas_call | solution.py:253
  105.6 3.2 %collective-permute-start.28 = (bf16[64,4224]{1,0:T(8,128)(2,1)S(1)}, bf16[64,4224]{1,0:T(8,128)(2,1)S(1)}, u32[]{:S(2)}, u32[]{:S(2)}) collective-permute-start(bf16[64,4224]{1,0:T(8,128)(2,1)S(1)} %get-tuple-element.57), channel_id=1, source_target_pairs={{0,24},{1,25},{2,98},{3,99},{4,28},{5,29},{6,102},{7,103},{8,0},{9... | collective-permute-start | bytes 1622024 | tf_op jit(solution)/shard_map/ppermute | solution.py:51
  108.8 7.3 %collective-permute-done.23.refs_2_ = bf16[64,4224]{1,0:T(8,128)(2,1)S(1)} collective-permute-done((bf16[64,4224]{1,0:T(8,128)(2,1)S(1)}, bf16[64,4224]{1,0:T(8,128)(2,1)S(1)}, u32[]{:S(2)}, u32[]{:S(2)}) %collective-permute-start.23) | collective-permute-done | bytes 540704 | tf_op jit(solution)/shard_map/ppermute | solution.py:51
  116.9 3.3 %collective-permute-start.31 = (bf16[96,4224]{1,0:T(8,128)(2,1)S(1)}, bf16[96,4224]{1,0:T(8,128)(2,1)S(1)}, u32[]{:S(2)}, u32[]{:S(2)}) collective-permute-start(bf16[96,4224]{1,0:T(8,128)(2,1)S(1)} %get-tuple-element.60), channel_id=1, source_target_pairs={{0,24},{1,25},{2,98},{3,99},{4,28},{5,29},{6,102},{7,103},{8,0},{9... | collective-permute-start | bytes 2433032 | tf_op jit(solution)/shard_map/ppermute | solution.py:51
  120.8 5.4 %weights.3 = bf16[448,4096]{1,0:T(8,128)(2,1)} custom-call(bf16[1024,4096]{1,0:T(8,128)(2,1)S(1)} %get-tuple-element.68.side_ref, bf16[1344,1024]{1,0:T(8,128)(2,1)S(1)} %get-tuple-element.69.coef_ref), custom_call_target="tpu_custom_call" | custom-call | flops 3758096384 | bytes 12058624 | tf_op jit(solution)/shard_map/weights/pallas_call | solution.py:281
  126.2 3.2 %collective-permute-start.29 = (bf16[32,4224]{1,0:T(8,128)(2,1)S(1)}, bf16[32,4224]{1,0:T(8,128)(2,1)S(1)}, u32[]{:S(2)}, u32[]{:S(2)}) collective-permute-start(bf16[32,4224]{1,0:T(8,128)(2,1)S(1)} %get-tuple-element.58), channel_id=1, source_target_pairs={{0,24},{1,25},{2,98},{3,99},{4,28},{5,29},{6,102},{7,103},{8,0},{9... | collective-permute-start | bytes 811016 | tf_op jit(solution)/shard_map/ppermute | solution.py:51
  131.0 2.8 %collective-permute-start.33 = (bf16[32,4224]{1,0:T(8,128)(2,1)S(1)}, bf16[32,4224]{1,0:T(8,128)(2,1)S(1)}, u32[]{:S(2)}, u32[]{:S(2)}) collective-permute-start(bf16[32,4224]{1,0:T(8,128)(2,1)S(1)} %get-tuple-element.62), channel_id=1, source_target_pairs={{0,96},{1,97},{2,26},{3,27},{4,100},{5,101},{6,30},{7,31},{8,104},... | collective-permute-start | bytes 811016 | tf_op jit(solution)/shard_map/ppermute | solution.py:51
  134.5 5.4 %weights.4 = bf16[448,4096]{1,0:T(8,128)(2,1)} custom-call(bf16[1024,4096]{1,0:T(8,128)(2,1)S(1)} %get-tuple-element.68.side_ref, bf16[1344,1024]{1,0:T(8,128)(2,1)S(1)} %get-tuple-element.69.coef_ref), custom_call_target="tpu_custom_call" | custom-call | flops 3758096384 | bytes 12058624 | tf_op jit(solution)/shard_map/weights/pallas_call | solution.py:281
  142.1 1.7 %collective-permute-start.35 = (bf16[16,4224]{1,0:T(8,128)(2,1)S(1)}, bf16[16,4224]{1,0:T(8,128)(2,1)S(1)}, u32[]{:S(2)}, u32[]{:S(2)}) collective-permute-start(bf16[16,4224]{1,0:T(8,128)(2,1)S(1)} %get-tuple-element.65), channel_id=1, source_target_pairs={{0,4},{1,5},{2,6},{3,7},{4,0},{5,1},{6,2},{7,3},{8,12},{9,13},{10,... | collective-permute-start | bytes 405512 | tf_op jit(solution)/shard_map/ppermute | solution.py:51
  143.7 2.2 %collective-permute-start.37 = (bf16[16,4224]{1,0:T(8,128)(2,1)S(1)}, bf16[16,4224]{1,0:T(8,128)(2,1)S(1)}, u32[]{:S(2)}, u32[]{:S(2)}) collective-permute-start(bf16[16,4224]{1,0:T(8,128)(2,1)S(1)} %get-tuple-element.65), channel_id=1, source_target_pairs={{0,5},{1,4},{2,7},{3,6},{4,1},{5,0},{6,3},{7,2},{8,13},{9,12},{10,... | collective-permute-start | bytes 405512 | tf_op jit(solution)/shard_map/ppermute | solution.py:51
  146.6 5.4 %weights.5 = bf16[448,4096]{1,0:T(8,128)(2,1)} custom-call(bf16[1024,4096]{1,0:T(8,128)(2,1)S(1)} %get-tuple-element.70.side_ref, bf16[1344,1024]{1,0:T(8,128)(2,1)S(1)} %get-tuple-element.69.coef_ref), custom_call_target="tpu_custom_call" | custom-call | flops 3758096384 | bytes 12058624 | tf_op jit(solution)/shard_map/weights/pallas_call | solution.py:281
  (78 shorter events, 14.5 us)
Async XLA Ops:
  3.4 8.2 %collective-permute-start = (bf16[16,8320]{1,0:T(8,128)(2,1)S(1)}, bf16[16,8320]{1,0:T(8,128)(2,1)S(1)}, u32[]{:S(2)}, u32[]{:S(2)}) collective-permute-start(bf16[16,8320]{1,0:T(8,128)(2,1)S(1)} %packed.1.refs_0_), channel_id=1, source_target_pairs={{0,4},{1,5},{2,6},{3,7},{4,0},{5,1},{6,2},{7,3},{8,12},{9,13},{10,... | collective-permute-start | bytes 798728 | tf_op jit(solution)/shard_map/ppermute | solution.py:51
  11.6 9.8 %collective-permute-start.1 = (bf16[32,8320]{1,0:T(8,128)(2,1)S(1)}, bf16[32,8320]{1,0:T(8,128)(2,1)S(1)}, u32[]{:S(2)}, u32[]{:S(2)}) collective-permute-start(bf16[32,8320]{1,0:T(8,128)(2,1)S(1)} %joined.2.refs_2_), channel_id=1, source_target_pairs={{0,96},{1,97},{2,26},{3,27},{4,100},{5,101},{6,30},{7,31},{8,104},... | collective-permute-start | bytes 1597448 | tf_op jit(solution)/shard_map/ppermute | solution.py:51
  14.6 10.5 %collective-permute-start.2 = (bf16[32,8320]{1,0:T(8,128)(2,1)S(1)}, bf16[32,8320]{1,0:T(8,128)(2,1)S(1)}, u32[]{:S(2)}, u32[]{:S(2)}) collective-permute-start(bf16[32,8320]{1,0:T(8,128)(2,1)S(1)} %joined.2.refs_2_), channel_id=1, source_target_pairs={{0,32},{1,33},{2,10},{3,11},{4,36},{5,37},{6,14},{7,15},{8,40},{9,... | collective-permute-start | bytes 1597448 | tf_op jit(solution)/shard_map/ppermute | solution.py:51
  25.2 26.5 %collective-permute-start.7 = (bf16[96,8320]{1,0:T(8,128)(2,1)S(1)}, bf16[96,8320]{1,0:T(8,128)(2,1)S(1)}, u32[]{:S(2)}, u32[]{:S(2)}) collective-permute-start(bf16[96,8320]{1,0:T(8,128)(2,1)S(1)} %joined.3.refs_0_), channel_id=1, source_target_pairs={{0,24},{1,25},{2,98},{3,99},{4,28},{5,29},{6,102},{7,103},{8,0},{9... | collective-permute-start | bytes 4792328 | tf_op jit(solution)/shard_map/ppermute | solution.py:51
  29.3 24.9 %collective-permute-start.14 = (bf16[96,8320]{1,0:T(8,128)(2,1)S(1)}, bf16[96,8320]{1,0:T(8,128)(2,1)S(1)}, u32[]{:S(2)}, u32[]{:S(2)}) collective-permute-start(bf16[96,8320]{1,0:T(8,128)(2,1)S(1)} %joined.3.refs_0_), channel_id=1, source_target_pairs={{0,8},{1,9},{2,34},{3,35},{4,12},{5,13},{6,38},{7,39},{8,16},{9,17... | collective-permute-start | bytes 4792328 | tf_op jit(solution)/shard_map/ppermute | solution.py:51
  29.3 16.5 %collective-permute-start.3 = (bf16[32,8320]{1,0:T(8,128)(2,1)S(1)}, bf16[32,8320]{1,0:T(8,128)(2,1)S(1)}, u32[]{:S(2)}, u32[]{:S(2)}) collective-permute-start(bf16[32,8320]{1,0:T(8,128)(2,1)S(1)} %joined.2.refs_2_), channel_id=1, source_target_pairs={{0,64},{1,65},{2,18},{3,19},{4,68},{5,69},{6,22},{7,23},{8,72},{9,... | collective-permute-start | bytes 1597448 | tf_op jit(solution)/shard_map/ppermute | solution.py:51
  29.3 47.7 %collective-permute-start.4 = (bf16[96,8320]{1,0:T(8,128)(2,1)S(1)}, bf16[96,8320]{1,0:T(8,128)(2,1)S(1)}, u32[]{:S(2)}, u32[]{:S(2)}) collective-permute-start(bf16[96,8320]{1,0:T(8,128)(2,1)S(1)} %joined.3.refs_0_), channel_id=1, source_target_pairs={{0,2},{1,3},{2,0},{3,1},{4,6},{5,7},{6,4},{7,5},{8,10},{9,11},{10,... | collective-permute-start | bytes 4792328 | tf_op jit(solution)/shard_map/ppermute | solution.py:51
  45.8 8.5 %collective-permute-start.5 = (bf16[32,8320]{1,0:T(8,128)(2,1)S(1)}, bf16[32,8320]{1,0:T(8,128)(2,1)S(1)}, u32[]{:S(2)}, u32[]{:S(2)}) collective-permute-start(bf16[32,8320]{1,0:T(8,128)(2,1)S(1)} %collective-permute-done.3.refs_1_), channel_id=1, source_target_pairs={{0,2},{1,3},{2,0},{3,1},{4,6},{5,7},{6,4},{7,5},{8,10},{9,11},{10,... | collective-permute-start | bytes 1597448 | tf_op jit(solution)/shard_map/ppermute | solution.py:51
  45.8 11.6 %collective-permute-start.8 = (bf16[32,8320]{1,0:T(8,128)(2,1)S(1)}, bf16[32,8320]{1,0:T(8,128)(2,1)S(1)}, u32[]{:S(2)}, u32[]{:S(2)}) collective-permute-start(bf16[32,8320]{1,0:T(8,128)(2,1)S(1)} %collective-permute-done.3.refs_1_), channel_id=1, source_target_pairs={{0,24},{1,25},{2,98},{3,99},{4,28},{5,29},{6,102},{7,103},{8,0},{9... | collective-permute-start | bytes 1597448 | tf_op jit(solution)/shard_map/ppermute | solution.py:51
  51.7 10.9 %collective-permute-start.16 = (bf16[32,8320]{1,0:T(8,128)(2,1)S(1)}, bf16[32,8320]{1,0:T(8,128)(2,1)S(1)}, u32[]{:S(2)}, u32[]{:S(2)}) collective-permute-start(bf16[32,8320]{1,0:T(8,128)(2,1)S(1)} %collective-permute-done.3.refs_1_), channel_id=1, source_target_pairs={{0,8},{1,9},{2,34},{3,35},{4,12},{5,13},{6,38},{7,39},{8,16},{9,17... | collective-permute-start | bytes 1597448 | tf_op jit(solution)/shard_map/ppermute | solution.py:51
  54.2 30.4 %collective-permute-start.9 = (bf16[96,8320]{1,0:T(8,128)(2,1)S(1)}, bf16[96,8320]{1,0:T(8,128)(2,1)S(1)}, u32[]{:S(2)}, u32[]{:S(2)}) collective-permute-start(bf16[96,8320]{1,0:T(8,128)(2,1)S(1)} %collective-permute-done.7.refs_0_.v_ref), channel_id=1, source_target_pairs={{0,2},{1,3},{2,0},{3,1},{4,6},{5,7},{6,4},{7,5},{8,10},{9,11},{10,... | collective-permute-start | bytes 4792328 | tf_op jit(solution)/shard_map/ppermute | solution.py:51
  54.3 23.2 %collective-permute-start.12 = (bf16[48,8320]{1,0:T(8,128)(2,1)S(1)}, bf16[48,8320]{1,0:T(8,128)(2,1)S(1)}, u32[]{:S(2)}, u32[]{:S(2)}) collective-permute-start(bf16[48,8320]{1,0:T(8,128)(2,1)S(1)} %taken.4), channel_id=1, source_target_pairs={{0,24},{1,25},{2,98},{3,99},{4,28},{5,29},{6,102},{7,103},{8,0},{9... | collective-permute-start | bytes 2396168 | tf_op jit(solution)/shard_map/ppermute | solution.py:51
  57.4 20.2 %collective-permute-start.15 = (bf16[48,8320]{1,0:T(8,128)(2,1)S(1)}, bf16[48,8320]{1,0:T(8,128)(2,1)S(1)}, u32[]{:S(2)}, u32[]{:S(2)}) collective-permute-start(bf16[48,8320]{1,0:T(8,128)(2,1)S(1)} %taken.6), channel_id=1, source_target_pairs={{0,8},{1,9},{2,34},{3,35},{4,12},{5,13},{6,38},{7,39},{8,16},{9,17... | collective-permute-start | bytes 2396168 | tf_op jit(solution)/shard_map/ppermute | solution.py:51
  69.3 7.6 %collective-permute-start.17 = (bf16[16,8320]{1,0:T(8,128)(2,1)S(1)}, bf16[16,8320]{1,0:T(8,128)(2,1)S(1)}, u32[]{:S(2)}, u32[]{:S(2)}) collective-permute-start(bf16[16,8320]{1,0:T(8,128)(2,1)S(1)} %taken.7), channel_id=1, source_target_pairs={{0,8},{1,9},{2,34},{3,35},{4,12},{5,13},{6,38},{7,39},{8,16},{9,17... | collective-permute-start | bytes 798728 | tf_op jit(solution)/shard_map/ppermute | solution.py:51
  77.0 21.6 %collective-permute-start.25 = (bf16[96,8320]{1,0:T(8,128)(2,1)S(1)}, bf16[96,8320]{1,0:T(8,128)(2,1)S(1)}, u32[]{:S(2)}, u32[]{:S(2)}) collective-permute-start(bf16[96,8320]{1,0:T(8,128)(2,1)S(1)} %collective-permute-done.14.v_ref.refs_0_), channel_id=1, source_target_pairs={{0,2},{1,3},{2,0},{3,1},{4,6},{5,7},{6,4},{7,5},{8,10},{9,11},{10,... | collective-permute-start | bytes 4792328 | tf_op jit(solution)/shard_map/ppermute | solution.py:51
  77.0 7.4 %collective-permute-start.10 = (bf16[32,8320]{1,0:T(8,128)(2,1)S(1)}, bf16[32,8320]{1,0:T(8,128)(2,1)S(1)}, u32[]{:S(2)}, u32[]{:S(2)}) collective-permute-start(bf16[32,8320]{1,0:T(8,128)(2,1)S(1)} %collective-permute-done.8.refs_1_.v_ref), channel_id=1, source_target_pairs={{0,2},{1,3},{2,0},{3,1},{4,6},{5,7},{6,4},{7,5},{8,10},{9,11},{10,... | collective-permute-start | bytes 1597448 | tf_op jit(solution)/shard_map/ppermute | solution.py:51
  77.5 14.2 %collective-permute-start.18 = (bf16[48,8320]{1,0:T(8,128)(2,1)S(1)}, bf16[48,8320]{1,0:T(8,128)(2,1)S(1)}, u32[]{:S(2)}, u32[]{:S(2)}) collective-permute-start(bf16[48,8320]{1,0:T(8,128)(2,1)S(1)} %collective-permute-done.12.refs_0_), channel_id=1, source_target_pairs={{0,2},{1,3},{2,0},{3,1},{4,6},{5,7},{6,4},{7,5},{8,10},{9,11},{10,... | collective-permute-start | bytes 2396168 | tf_op jit(solution)/shard_map/ppermute | solution.py:51
  77.6 14.1 %collective-permute-start.20 = (bf16[48,8320]{1,0:T(8,128)(2,1)S(1)}, bf16[48,8320]{1,0:T(8,128)(2,1)S(1)}, u32[]{:S(2)}, u32[]{:S(2)}) collective-permute-start(bf16[48,8320]{1,0:T(8,128)(2,1)S(1)} %collective-permute-done.15.refs_2_), channel_id=1, source_target_pairs={{0,2},{1,3},{2,0},{3,1},{4,6},{5,7},{6,4},{7,5},{8,10},{9,11},{10,... | collective-permute-start | bytes 2396168 | tf_op jit(solution)/shard_map/ppermute | solution.py:51
  98.3 10.5 %collective-permute-start.11 = (bf16[128,4224]{1,0:T(8,128)(2,1)S(1)}, bf16[128,4224]{1,0:T(8,128)(2,1)S(1)}, u32[]{:S(2)}, u32[]{:S(2)}) collective-permute-start(bf16[128,4224]{1,0:T(8,128)(2,1)S(1)} %get-tuple-element.44), channel_id=1, source_target_pairs={{0,2},{1,3},{2,0},{3,1},{4,6},{5,7},{6,4},{7,5},{8,10},{9,11},{10,... | collective-permute-start | bytes 3244040 | tf_op jit(solution)/shard_map/ppermute | solution.py:51
  105.0 11.6 %collective-permute-start.27 = (bf16[128,4224]{1,0:T(8,128)(2,1)S(1)}, bf16[128,4224]{1,0:T(8,128)(2,1)S(1)}, u32[]{:S(2)}, u32[]{:S(2)}) collective-permute-start(bf16[128,4224]{1,0:T(8,128)(2,1)S(1)} %get-tuple-element.56), channel_id=1, source_target_pairs={{0,2},{1,3},{2,0},{3,1},{4,6},{5,7},{6,4},{7,5},{8,10},{9,11},{10,... | collective-permute-start | bytes 3244040 | tf_op jit(solution)/shard_map/ppermute | solution.py:51
  105.5 10.6 %collective-permute-start.23 = (bf16[64,4224]{1,0:T(8,128)(2,1)S(1)}, bf16[64,4224]{1,0:T(8,128)(2,1)S(1)}, u32[]{:S(2)}, u32[]{:S(2)}) collective-permute-start(bf16[64,4224]{1,0:T(8,128)(2,1)S(1)} %get-tuple-element.50), channel_id=1, source_target_pairs={{0,8},{1,9},{2,34},{3,35},{4,12},{5,13},{6,38},{7,39},{8,16},{9,17... | collective-permute-start | bytes 1622024 | tf_op jit(solution)/shard_map/ppermute | solution.py:51
  105.6 11.0 %collective-permute-start.28 = (bf16[64,4224]{1,0:T(8,128)(2,1)S(1)}, bf16[64,4224]{1,0:T(8,128)(2,1)S(1)}, u32[]{:S(2)}, u32[]{:S(2)}) collective-permute-start(bf16[64,4224]{1,0:T(8,128)(2,1)S(1)} %get-tuple-element.57), channel_id=1, source_target_pairs={{0,24},{1,25},{2,98},{3,99},{4,28},{5,29},{6,102},{7,103},{8,0},{9... | collective-permute-start | bytes 1622024 | tf_op jit(solution)/shard_map/ppermute | solution.py:51
  108.8 20.6 %collective-permute-start.6 = (bf16[128,4224]{1,0:T(8,128)(2,1)S(1)}, bf16[128,4224]{1,0:T(8,128)(2,1)S(1)}, u32[]{:S(2)}, u32[]{:S(2)}) collective-permute-start(bf16[128,4224]{1,0:T(8,128)(2,1)S(1)} %get-tuple-element.39), channel_id=1, source_target_pairs={{0,2},{1,3},{2,0},{3,1},{4,6},{5,7},{6,4},{7,5},{8,10},{9,11},{10,... | collective-permute-start | bytes 3244040 | tf_op jit(solution)/shard_map/ppermute | solution.py:51
  116.5 13.5 %collective-permute-start.30 = (bf16[96,4224]{1,0:T(8,128)(2,1)S(1)}, bf16[96,4224]{1,0:T(8,128)(2,1)S(1)}, u32[]{:S(2)}, u32[]{:S(2)}) collective-permute-start(bf16[96,4224]{1,0:T(8,128)(2,1)S(1)} %get-tuple-element.59), channel_id=1, source_target_pairs={{0,8},{1,9},{2,34},{3,35},{4,12},{5,13},{6,38},{7,39},{8,16},{9,17... | collective-permute-start | bytes 2433032 | tf_op jit(solution)/shard_map/ppermute | solution.py:51
  116.9 13.1 %collective-permute-start.31 = (bf16[96,4224]{1,0:T(8,128)(2,1)S(1)}, bf16[96,4224]{1,0:T(8,128)(2,1)S(1)}, u32[]{:S(2)}, u32[]{:S(2)}) collective-permute-start(bf16[96,4224]{1,0:T(8,128)(2,1)S(1)} %get-tuple-element.60), channel_id=1, source_target_pairs={{0,24},{1,25},{2,98},{3,99},{4,28},{5,29},{6,102},{7,103},{8,0},{9... | collective-permute-start | bytes 2433032 | tf_op jit(solution)/shard_map/ppermute | solution.py:51
  126.2 13.7 %collective-permute-start.24 = (bf16[32,4224]{1,0:T(8,128)(2,1)S(1)}, bf16[32,4224]{1,0:T(8,128)(2,1)S(1)}, u32[]{:S(2)}, u32[]{:S(2)}) collective-permute-start(bf16[32,4224]{1,0:T(8,128)(2,1)S(1)} %get-tuple-element.51), channel_id=1, source_target_pairs={{0,8},{1,9},{2,34},{3,35},{4,12},{5,13},{6,38},{7,39},{8,16},{9,17... | collective-permute-start | bytes 811016 | tf_op jit(solution)/shard_map/ppermute | solution.py:51
  126.2 13.7 %collective-permute-start.29 = (bf16[32,4224]{1,0:T(8,128)(2,1)S(1)}, bf16[32,4224]{1,0:T(8,128)(2,1)S(1)}, u32[]{:S(2)}, u32[]{:S(2)}) collective-permute-start(bf16[32,4224]{1,0:T(8,128)(2,1)S(1)} %get-tuple-element.58), channel_id=1, source_target_pairs={{0,24},{1,25},{2,98},{3,99},{4,28},{5,29},{6,102},{7,103},{8,0},{9... | collective-permute-start | bytes 811016 | tf_op jit(solution)/shard_map/ppermute | solution.py:51
  130.4 9.5 %collective-permute-start.32 = (bf16[32,4224]{1,0:T(8,128)(2,1)S(1)}, bf16[32,4224]{1,0:T(8,128)(2,1)S(1)}, u32[]{:S(2)}, u32[]{:S(2)}) collective-permute-start(bf16[32,4224]{1,0:T(8,128)(2,1)S(1)} %get-tuple-element.61), channel_id=1, source_target_pairs={{0,32},{1,33},{2,10},{3,11},{4,36},{5,37},{6,14},{7,15},{8,40},{9,... | collective-permute-start | bytes 811016 | tf_op jit(solution)/shard_map/ppermute | solution.py:51
  131.0 9.7 %collective-permute-start.33 = (bf16[32,4224]{1,0:T(8,128)(2,1)S(1)}, bf16[32,4224]{1,0:T(8,128)(2,1)S(1)}, u32[]{:S(2)}, u32[]{:S(2)}) collective-permute-start(bf16[32,4224]{1,0:T(8,128)(2,1)S(1)} %get-tuple-element.62), channel_id=1, source_target_pairs={{0,96},{1,97},{2,26},{3,27},{4,100},{5,101},{6,30},{7,31},{8,104},... | collective-permute-start | bytes 811016 | tf_op jit(solution)/shard_map/ppermute | solution.py:51
  133.7 8.1 %collective-permute-start.34 = (bf16[32,4224]{1,0:T(8,128)(2,1)S(1)}, bf16[32,4224]{1,0:T(8,128)(2,1)S(1)}, u32[]{:S(2)}, u32[]{:S(2)}) collective-permute-start(bf16[32,4224]{1,0:T(8,128)(2,1)S(1)} %get-tuple-element.63), channel_id=1, source_target_pairs={{0,64},{1,65},{2,18},{3,19},{4,68},{5,69},{6,22},{7,23},{8,72},{9,... | collective-permute-start | bytes 811016 | tf_op jit(solution)/shard_map/ppermute | solution.py:51
  142.1 10.0 %collective-permute-start.35 = (bf16[16,4224]{1,0:T(8,128)(2,1)S(1)}, bf16[16,4224]{1,0:T(8,128)(2,1)S(1)}, u32[]{:S(2)}, u32[]{:S(2)}) collective-permute-start(bf16[16,4224]{1,0:T(8,128)(2,1)S(1)} %get-tuple-element.65), channel_id=1, source_target_pairs={{0,4},{1,5},{2,6},{3,7},{4,0},{5,1},{6,2},{7,3},{8,12},{9,13},{10,... | collective-permute-start | bytes 405512 | tf_op jit(solution)/shard_map/ppermute | solution.py:51
  143.7 8.7 %collective-permute-start.37 = (bf16[16,4224]{1,0:T(8,128)(2,1)S(1)}, bf16[16,4224]{1,0:T(8,128)(2,1)S(1)}, u32[]{:S(2)}, u32[]{:S(2)}) collective-permute-start(bf16[16,4224]{1,0:T(8,128)(2,1)S(1)} %get-tuple-element.65), channel_id=1, source_target_pairs={{0,5},{1,4},{2,7},{3,6},{4,1},{5,0},{6,3},{7,2},{8,13},{9,12},{10,... | collective-permute-start | bytes 405512 | tf_op jit(solution)/shard_map/ppermute | solution.py:51
  (12 other events, 230.1 us)
